TPU v7x, 8 devices: a whole 2x2x1 slice. The times are simulated.
8 devices in a mesh: vp: 8 (over z, y, x, core).
Axes of the slice: x: 2, y: 2, z: 1, core: 2. Of those that a mesh axis runs over, the one named last changes fastest.
Arguments:
- table_in: float32 [50304, 768], P('vp')
- table_out: float32 [50304, 768], P('vp')
- center_ids: int32 [65536], P('vp')
- context_ids: int32 [65536], P('vp')
- negative_ids: int32 [32768], P('vp')
Outputs:
- output 1: float32 [50304, 768], P('vp')
- output 2: float32 [50304, 768], P('vp')
All inputs are finite; a program needn't handle non-finite values.
Results may differ from a plain program's by a relative error of at most 0.001.
Values sent between devices are 32-bit elements.
A program may use at most 1 GiB of HBM per device.

v0:
```python
import jax
import jax.numpy as jnp
from jax import lax
from jax.sharding import PartitionSpec as P

LEARN_RATE = 1.0
NEG_WEIGHT = 5.0
AXIS_NAME = 'vp'


def list_capacity(num_ids, shards):
    common_slots = 3 * num_ids // shards
    return common_slots + (num_ids - common_slots + shards - 1) // shards


def send_layout(id_list, shard_rows, shards, capacity):
    num_ids = id_list.shape[0]
    owner_idx = id_list // shard_rows
    sort_order = jnp.argsort(owner_idx, stable=True).astype(jnp.int32)
    owner_sorted = owner_idx[sort_order]
    per_owner = jax.ops.segment_sum(jnp.ones_like(owner_idx), owner_idx, num_segments=shards)
    owner_start = jnp.cumsum(per_owner) - per_owner
    cell_sorted = owner_sorted * capacity + jnp.arange(num_ids, dtype=jnp.int32) - owner_start[owner_sorted]
    cell_of_id = jnp.zeros_like(id_list).at[sort_order].set(cell_sorted)
    slot_of_cell = jnp.full((shards * capacity,), num_ids, jnp.int32).at[cell_sorted].set(sort_order)
    filler = (jnp.arange(shards * capacity, dtype=jnp.int32) // capacity) * shard_rows
    id_of_cell = jnp.take(id_list, slot_of_cell, axis=0, mode='fill', fill_value=-1)
    id_of_cell = jnp.where(slot_of_cell < num_ids, id_of_cell, filler)
    return cell_of_id, slot_of_cell, id_of_cell


def fetch_rows(table_shard, id_of_cell, shards, capacity):
    ids_asked = lax.all_to_all(id_of_cell.reshape(shards, capacity), AXIS_NAME, 0, 0)
    local_rows = ids_asked - lax.axis_index(AXIS_NAME) * table_shard.shape[0]
    rows_found = jnp.take(table_shard, local_rows, axis=0)
    returned = lax.all_to_all(rows_found, AXIS_NAME, 0, 0)
    return local_rows.reshape(-1), returned.reshape(shards * capacity, table_shard.shape[1])


def send_grads(grad_cells, local_rows, shards, capacity, shard_rows):
    arrived = lax.all_to_all(grad_cells.reshape(shards, capacity, -1), AXIS_NAME, 0, 0)
    return jax.ops.segment_sum(arrived.reshape(shards * capacity, -1), local_rows, num_segments=shard_rows)


def pair_grads(center_vec, context_vec, negative_vec):
    neg_scale = NEG_WEIGHT / negative_vec.shape[0]
    pos_score = jnp.sum(center_vec * context_vec, axis=1)
    center_half = center_vec.astype(jnp.bfloat16)
    negative_half = negative_vec.astype(jnp.bfloat16)
    neg_score = lax.dot_general(center_half, negative_half, (((1,), (1,)), ((), ())), preferred_element_type=jnp.float32)
    pos_grad = (jax.nn.sigmoid(pos_score) - 1.0)[:, None]
    neg_grad = (neg_scale * jax.nn.sigmoid(neg_score)).astype(jnp.bfloat16)
    d_center = pos_grad * context_vec + jnp.dot(neg_grad, negative_half, preferred_element_type=jnp.float32)
    d_context = pos_grad * center_vec
    d_negative = lax.dot_general(neg_grad, center_half, (((0,), (0,)), ((), ())), preferred_element_type=jnp.float32)
    return d_center, d_context, d_negative


def solution(mesh):
    shards = mesh.shape[AXIS_NAME]

    def device_step(in_shard, out_shard, center_ids, context_ids, negative_ids):
        shard_rows = in_shard.shape[0]
        pairs_dev = center_ids.shape[0]
        cap_pairs = list_capacity(pairs_dev, shards)
        cap_out = cap_pairs + list_capacity(negative_ids.shape[0], shards)
        out_ids = jnp.concatenate([context_ids, negative_ids])
        in_cell, in_slot, in_asks = send_layout(center_ids, shard_rows, shards, cap_pairs)
        out_cell, out_slot, out_asks = send_layout(out_ids, shard_rows, shards, cap_out)
        in_local, in_rows = fetch_rows(in_shard, in_asks, shards, cap_pairs)
        out_local, out_rows = fetch_rows(out_shard, out_asks, shards, cap_out)
        center_vec = jnp.take(in_rows, in_cell, axis=0)
        looked_up = jnp.take(out_rows, out_cell, axis=0)
        d_center, d_context, d_negative = pair_grads(center_vec, looked_up[:pairs_dev], looked_up[pairs_dev:])
        in_cells = jnp.take(d_center, in_slot, axis=0, mode='fill', fill_value=0.0)
        out_cells = jnp.take(jnp.concatenate([d_context, d_negative]), out_slot, axis=0, mode='fill', fill_value=0.0)
        in_sum = send_grads(in_cells, in_local, shards, cap_pairs, shard_rows)
        out_sum = send_grads(out_cells, out_local, shards, cap_out, shard_rows)
        return in_shard - LEARN_RATE * in_sum, out_shard - LEARN_RATE * out_sum

    return jax.shard_map(device_step, mesh=mesh, in_specs=(P(AXIS_NAME, None), P(AXIS_NAME, None), P(AXIS_NAME), P(AXIS_NAME), P(AXIS_NAME)), out_specs=(P(AXIS_NAME, None), P(AXIS_NAME, None)), check_vma=False)
```

profile of v0, /device:TPU:0, one launch (start us, length us, event | category | flops | bytes accessed | tf_op | source)
XLA Modules:
  0.0 6846.1 jit_solution(11240422952318956036)
XLA Ops:
  8.9 45.5 gather_fusion
  54.6 57.0 scatter_custom_fusion
  118.3 30.5 scatter_custom_fusion.1
  148.9 163.7 %gather_fusion.1 = s32[29696]{0:T(1024)S(1)} fusion(s32[8192]{0:T(1024)S(1)} %copy-done, s32[29696]{0:T(1024)S(1)} %fusion.15), kind=kCustom, calls=%fused_computation.1 | custom fusion | bytes 356352 | tf_op jit(solution)/shard_map/jit(_take)/gather | solution.py:27
  326.8 68.0 gather_fusion.4
  395.3 85.2 %scatter_custom_fusion.3 = s32[8]{0:T(128)S(1)} fusion(s32[12288]{0:T(1024)S(1)} %bitcast.74, s32[12288]{0:T(1024)S(1)} %ne.88, s32[]{:T(128)} %constant.117.clone.1), kind=kCustom, calls=%fused_computation.124 | custom fusion | flops 12288 | bytes 36 | tf_op jit(solution)/shard_map/scatter-add | solution.py:21
  487.2 45.4 scatter_custom_fusion.5
  532.7 228.1 %gather_fusion.5 = s32[44544]{0:T(1024)S(1)} fusion(s32[12288]{0:T(1024)S(1)} %constant_dynamic-update-slice_fusion, s32[45056]{0:T(1024)S(1)} %pad_clamp_fusion.1), kind=kCustom, calls=%fused_computation.5 | custom fusion | bytes 534528 | tf_op jit(solution)/shard_map/jit(_take)/gather | solution.py:27
  766.3 146.5 %gather_fusion.2 = f32[29696,768]{1,0:T(8,128)} fusion(f32[6288,768]{1,0:T(8,128)} %param.5, s32[29696]{0:T(1024)S(1)} %broadcast_clamp_fusion), kind=kCustom, calls=%fused_computation.2 | custom fusion | bytes 182571008 | tf_op jit(solution)/shard_map/jit(_take)/gather | solution.py:35
  912.7 59.0 broadcast_select_fusion.3
  985.7 163.7 %gather_fusion.6 = f32[44544,768]{1,0:T(8,128)} fusion(f32[6288,768]{1,0:T(8,128)} %param.6, s32[45056]{0:T(1024)S(1)} %pad_clamp_fusion), kind=kCustom, calls=%fused_computation.6 | custom fusion | bytes 273856512 | tf_op jit(solution)/shard_map/jit(_take)/gather | solution.py:35
  1149.5 87.7 %broadcast_select_fusion.1 = f32[8,5568,768]{2,1,0:T(8,128)} fusion(f32[8,5568,768]{2,1,0:T(8,128)} %bitcast.38, pred[8,5568]{1,0:T(8,128)(4,1)S(1)} %compare_and_fusion), kind=kLoop, calls=%fused_computation.20 | loop fusion | flops 34209792 | bytes 273722880 | tf_op jit(solution)/shard_map/jit(_take)/select_n | solution.py:35
  1237.2 727.4 %all-to-all-done.1 = f32[8,3712,768]{2,1,0:T(8,128)} async-done(((f32[8,3712,768]{2,1,0:T(8,128)}), f32[8,3712,768]{2,1,0:T(8,128)}, u32[]{:S(2)}, u32[]{:S(2)}) %all-to-all-start.1) | async-done | bytes 91226144 | tf_op jit(solution)/shard_map/all_to_all | solution.py:36
  1977.5 45.5 scatter_custom_fusion.4
  2023.0 31.1 scatter_custom_fusion.2
  2055.3 143.5 %gather_fusion.3 = f32[8192,768]{1,0:T(8,128)} fusion(f32[29696,768]{1,0:T(8,128)} %bitcast.19, s32[8192]{0:T(1024)S(1)} %fusion.23), kind=kCustom, calls=%fused_computation.3 | custom fusion | bytes 50364416 | tf_op jit(solution)/shard_map/jit(_take)/gather | solution.py:72
  2198.9 1249.5 %all-to-all-done.3 = f32[8,5568,768]{2,1,0:T(8,128)} async-done(((f32[8,5568,768]{2,1,0:T(8,128)}), f32[8,5568,768]{2,1,0:T(8,128)}, u32[]{:S(2)}, u32[]{:S(2)}) %all-to-all-start.3) | async-done | bytes 136839200 | tf_op jit(solution)/shard_map/all_to_all | solution.py:36
  3448.4 215.3 %gather_fusion.7 = f32[12288,768]{1,0:T(8,128)} fusion(f32[44544,768]{1,0:T(8,128)} %bitcast.39, s32[12288]{0:T(1024)S(1)} %fusion.21), kind=kCustom, calls=%fused_computation.7 | custom fusion | bytes 75546624 | tf_op jit(solution)/shard_map/jit(_take)/gather | solution.py:73
  3663.6 28.4 broadcast_select_fusion.4
  3692.1 76.4 %multiply_convert_fusion = bf16[8192,4096]{1,0:T(8,128)(2,1)} fusion(f32[12288,768]{1,0:T(8,128)} %broadcast_select_fusion.4, f32[8192,768]{1,0:T(8,128)} %gather_fusion.3, pred[8192]{0:T(1024)(128)(4,1)S(1)} %copy-done.19), kind=kOutput, calls=%fused_computation.18 | convolution fusion | flops 51713671168 | bytes 98574336 | tf_op jit(solution)/shard_map/dot_general | solution.py:50
  3785.4 63.0 multiply_add_fusion
  3848.4 148.2 %gather_fusion.8 = f32[29696,768]{1,0:T(8,128)} fusion(f32[8192,768]{1,0:T(8,128)} %multiply_add_fusion, s32[29696]{0:T(1024)S(1)} %copy-done.10), kind=kCustom, calls=%fused_computation.8 | custom fusion | bytes 182571008 | tf_op jit(solution)/shard_map/jit(_take)/gather | solution.py:75
  3996.5 59.0 broadcast_select_fusion.2
  4085.3 65.4 fusion.32
  4150.7 25.5 pad_maximum_fusion
  4176.2 169.0 %gather_fusion.9 = f32[44544,768]{1,0:T(8,128)} fusion(f32[12288,768]{1,0:T(8,128)} %pad_maximum_fusion, s32[45056]{0:T(1024)S(1)} %copy-done.6), kind=kCustom, calls=%fused_computation.9 | custom fusion | bytes 273856512 | tf_op jit(solution)/shard_map/jit(_take)/gather | solution.py:76
  4345.1 88.8 %broadcast_select_fusion = f32[8,5568,768]{2,1,0:T(8,128)} fusion(f32[8,5568,768]{2,1,0:T(8,128)} %bitcast.42, pred[8,5568]{1,0:T(8,128)(4,1)S(1)} %copy-done.13), kind=kLoop, calls=%fused_computation.19 | loop fusion | flops 34209792 | bytes 273722880 | tf_op jit(solution)/shard_map/jit(_take)/select_n | solution.py:76
  4433.9 614.6 %all-to-all-done.4 = f32[8,3712,768]{2,1,0:T(8,128)} async-done(((f32[8,3712,768]{2,1,0:T(8,128)}), f32[8,3712,768]{2,1,0:T(8,128)}, u32[]{:S(2)}, u32[]{:S(2)}) %all-to-all-start.4) | async-done | bytes 91226144 | tf_op jit(solution)/shard_map/all_to_all | solution.py:41
  5061.0 198.7 %scatter_custom_fusion.6 = f32[6288,768]{1,0:T(8,128)} fusion(s32[29696]{0:T(1024)} %bitcast.66, f32[29696,768]{1,0:T(8,128)} %bitcast.41, f32[]{:T(128)} %constant.107.clone.1), kind=kCustom, calls=%fused_computation.32 | custom fusion | flops 22806528 | bytes 19317248 | tf_op jit(solution)/shard_map/scatter-add | solution.py:42
  5259.7 20.0 sub.148
  5279.6 1252.9 %all-to-all-done.5 = f32[8,5568,768]{2,1,0:T(8,128)} async-done(((f32[8,5568,768]{2,1,0:T(8,128)}), f32[8,5568,768]{2,1,0:T(8,128)}, u32[]{:S(2)}, u32[]{:S(2)}) %all-to-all-start.5) | async-done | bytes 136839200 | tf_op jit(solution)/shard_map/all_to_all | solution.py:41
  6532.5 293.2 %scatter_custom_fusion.7 = f32[6288,768]{1,0:T(8,128)} fusion(s32[44544]{0:T(1024)S(1)} %reshape.557, f32[44544,768]{1,0:T(8,128)} %bitcast.43, f32[]{:T(128)} %constant.107.clone.1), kind=kCustom, calls=%fused_computation.30 | custom fusion | flops 34209792 | bytes 19317248 | tf_op jit(solution)/shard_map/scatter-add | solution.py:42
  (108 shorter events, 149.0 us)
Async XLA Ops:
  0.6 148.2 %copy-start = (s32[8192]{0:T(1024)S(1)}, s32[8192]{0:T(1024)}, u32[]{:S(2)}) copy-start(s32[8192]{0:T(1024)} %param.7) | copy-start | bytes 98308
  148.8 163.8 %copy-start.3 = (s32[29696]{0:T(1024)}, s32[29696]{0:T(1024)S(1)}, u32[]{:S(2)}) copy-start(s32[29696]{0:T(1024)S(1)} %scatter_custom_fusion.1) | copy-start | bytes 356356
  148.9 163.7 %copy-start.9 = (s32[29696]{0:T(1024)}, s32[29696]{0:T(1024)S(1)}, u32[]{:S(2)}) copy-start(s32[29696]{0:T(1024)S(1)} %fusion.15) | copy-start | bytes 356356
  148.9 169.0 %copy-start.16 = (s32[8192]{0:T(1024)S(1)}, s32[8192]{0:T(1024)}, u32[]{:S(2)}) copy-start(s32[8192]{0:T(1024)} %param.8) | copy-start | bytes 98308
  148.9 169.0 %copy-start.21 = (s32[4096]{0:T(1024)S(1)}, s32[4096]{0:T(1024)}, u32[]{:S(2)}) copy-start(s32[4096]{0:T(1024)} %param.9) | copy-start | bytes 49156
  313.3 448.6 %all-to-all-start = ((s32[8,1,3712]{2,1,0:T(1,128)}), s32[8,1,3712]{2,1,0:T(1,128)S(1)}, u32[]{:S(2)}, u32[]{:S(2)}) async-start(s32[8,1,3712]{2,1,0:T(1,128)} %bitcast.14), calls=%async_computation | async-start | bytes 237568 | tf_op jit(solution)/shard_map/all_to_all | solution.py:33
  532.7 228.2 %copy-start.1 = (s32[44544]{0:T(1024)}, s32[44544]{0:T(1024)S(1)}, u32[]{:S(2)}) copy-start(s32[44544]{0:T(1024)S(1)} %scatter_custom_fusion.5) | copy-start | bytes 534532
  532.7 228.1 %copy-start.5 = (s32[45056]{0:T(1024)}, s32[45056]{0:T(1024)S(1)}, u32[]{:S(2)}) copy-start(s32[45056]{0:T(1024)S(1)} %pad_clamp_fusion.1) | copy-start | bytes 540676
  761.9 209.8 %all-to-all-start.2 = ((s32[8,1,5568]{2,1,0:T(1,128)}), s32[8,1,5568]{2,1,0:T(1,128)}, u32[]{:S(2)}, u32[]{:S(2)}) async-start(s32[8,1,5568]{2,1,0:T(1,128)} %all_to_all.27), calls=%async_computation.2 | async-start | bytes 360448 | tf_op jit(solution)/shard_map/all_to_all | solution.py:33
  765.0 0.6 copy-start.12
  766.2 146.5 %copy-start.17 = (pred[8,3712]{1,0:T(8,128)(4,1)S(1)}, pred[8,3712]{1,0:T(8,128)(4,1)}, u32[]{:S(2)}) copy-start(pred[8,3712]{1,0:T(8,128)(4,1)} %compare_and_fusion.2) | copy-start | bytes 89092
  971.7 992.9 %all-to-all-start.1 = ((f32[8,3712,768]{2,1,0:T(8,128)}), f32[8,3712,768]{2,1,0:T(8,128)}, u32[]{:S(2)}, u32[]{:S(2)}) async-start(f32[8,3712,768]{2,1,0:T(8,128)} %broadcast_select_fusion.3), calls=%async_computation.1 | async-start | bytes 182452224 | tf_op jit(solution)/shard_map/all_to_all | solution.py:36
  984.3 0.7 copy-start.7
  985.7 163.8 %copy-start.8 = (s32[8,1,5568]{2,1,0:T(1,128)S(1)}, s32[8,1,5568]{2,1,0:T(1,128)}, u32[]{:S(2)}) copy-start(s32[8,1,5568]{2,1,0:T(1,128)} %copy-done.7) | copy-start | bytes 534532
  1237.2 739.5 %copy-start.4 = (s32[29696]{0:T(1024)S(1)}, s32[29696]{0:T(1024)}, u32[]{:S(2)}) copy-start(s32[29696]{0:T(1024)} %copy-done.3) | copy-start | bytes 356356
  1964.6 1483.7 %all-to-all-start.3 = ((f32[8,5568,768]{2,1,0:T(8,128)}), f32[8,5568,768]{2,1,0:T(8,128)}, u32[]{:S(2)}, u32[]{:S(2)}) async-start(f32[8,5568,768]{2,1,0:T(8,128)} %broadcast_select_fusion.1), calls=%async_computation.3 | async-start | bytes 273678336 | tf_op jit(solution)/shard_map/all_to_all | solution.py:36
  3448.4 215.3 %copy-start.22 = (pred[12288]{0:T(1024)(128)(4,1)S(1)}, pred[12288]{0:T(1024)(128)(4,1)}, u32[]{:S(2)}) copy-start(pred[12288]{0:T(1024)(128)(4,1)} %compare_and_fusion.4) | copy-start | bytes 36868
  3663.6 28.4 copy-start.19
  3784.8 0.6 copy-start.14
  3785.4 63.0 copy-start.10
  3848.4 148.2 %copy-start.18 = (pred[8,3712]{1,0:T(8,128)(4,1)S(1)}, pred[8,3712]{1,0:T(8,128)(4,1)}, u32[]{:S(2)}) copy-start(pred[8,3712]{1,0:T(8,128)(4,1)} %broadcast_in_dim.107) | copy-start | bytes 89092
  4055.5 10.6 copy-start.2
  4055.5 11.4 copy-start.15
  4055.5 11.4 copy-start.20
  4055.5 993.1 %all-to-all-start.4 = ((f32[8,3712,768]{2,1,0:T(8,128)}), f32[8,3712,768]{2,1,0:T(8,128)}, u32[]{:S(2)}, u32[]{:S(2)}) async-start(f32[8,3712,768]{2,1,0:T(8,128)} %broadcast_select_fusion.2), calls=%async_computation.4 | async-start | bytes 182452224 | tf_op jit(solution)/shard_map/all_to_all | solution.py:41
  4150.7 25.5 copy-start.6
  4176.2 169.0 %copy-start.13 = (pred[8,5568]{1,0:T(8,128)(4,1)S(1)}, pred[8,5568]{1,0:T(8,128)(4,1)}, u32[]{:S(2)}) copy-start(pred[8,5568]{1,0:T(8,128)(4,1)} %broadcast_in_dim.123) | copy-start | bytes 133636
  4433.9 626.9 %copy-start.11 = (s32[8,5568]{1,0:T(8,128)S(1)}, s32[8,5568]{1,0:T(8,128)}, u32[]{:S(2)}) copy-start(s32[8,5568]{1,0:T(8,128)} %get-tuple-element.6) | copy-start | bytes 534532
  5048.6 1484.0 %all-to-all-start.5 = ((f32[8,5568,768]{2,1,0:T(8,128)}), f32[8,5568,768]{2,1,0:T(8,128)}, u32[]{:S(2)}, u32[]{:S(2)}) async-start(f32[8,5568,768]{2,1,0:T(8,128)} %broadcast_select_fusion), calls=%async_computation.5 | async-start | bytes 273678336 | tf_op jit(solution)/shard_map/all_to_all | solution.py:41
where the time goes:
time: 6870 us; the launch traced here: 6850 us
  waiting for transfers between devices  3840 us (56%)
  local copies, waits for them, and re-layouts  1650 us (24%)
  other arithmetic  1090 us (16%)
  matrix products  205 us (3%)
    all_to_all x2, waiting for transfers between devices, fetch_rows(): returned = lax.all_to_all(rows_found, AXIS_NAME, 0, 0)  1980 us
    all_to_all x2, waiting for transfers between devices, send_grads(): lax.all_to_all(grad_cells.reshape(shards, capacity, -1), AXIS_NAME, 0, 0)  1870 us
    scatter-add x2, other arithmetic, send_grads(): jax.ops.segment_sum(arrived.reshape(shards * capacity, -1), local_rows, n...  492 us
    gather x2, local copies, waits for them, and re-layouts, send_layout(): jnp.take(id_list, slot_of_cell, axis=0, mode='fill', fill_value=-1)  392 us
    gather x2, local copies, waits for them, and re-layouts, fetch_rows(): rows_found = jnp.take(table_shard, local_rows, axis=0)  310 us
    gather x1, local copies, waits for them, and re-layouts, device_step(): looked_up = jnp.take(out_rows, out_cell, axis=0)  215 us
    gather x1, local copies, waits for them, and re-layouts, device_step(): jnp.take(jnp.concatenate([d_context, d_negative]), out_slot, axis=0, mode...  169 us
    gather x1, local copies, waits for them, and re-layouts, device_step(): in_cells = jnp.take(d_center, in_slot, axis=0, mode='fill', fill_value=0.0)  148 us
  transfers between devices with their start and end apart: 6, of which 4 were waited for; matrix products, arithmetic and copies ran while one was open for 25% of the time, Pallas kernels for 0%

commit v1 on v0

v1 whole, which is shorter than its diff:
```python
import functools

import jax
import jax.numpy as jnp
from jax import lax
from jax.experimental import pallas as pl
from jax.sharding import PartitionSpec as P

LEARN_RATE = 1.0
NEG_WEIGHT = 5.0
AXIS_NAME = 'vp'
HOT_ROWS = 768


def unique_capacity(num_ids, shards):
    common_slots = 3 * num_ids // shards
    return common_slots // 4 + (num_ids - common_slots + shards - 1) // shards


def tight_capacity(num_ids, shards):
    return (num_ids - 3 * num_ids // shards + shards - 1) // shards


def running_count(flags):
    lanes = 128
    rows = flags.shape[0] // lanes
    grid = flags.reshape(rows, lanes).astype(jnp.bfloat16)
    upper = (jnp.arange(lanes)[:, None] <= jnp.arange(lanes)[None, :]).astype(jnp.bfloat16)
    inner = jnp.dot(grid, upper, preferred_element_type=jnp.float32)
    lower = (jnp.arange(rows)[:, None] > jnp.arange(rows)[None, :]).astype(jnp.bfloat16)
    outer = jnp.dot(lower, inner[:, -1:].astype(jnp.bfloat16), preferred_element_type=jnp.float32)
    return (inner + outer).astype(jnp.int32).reshape(-1)


def plan_unique(sorted_ids, shard_rows, shards, hot, capacity):
    num_ids = sorted_ids.shape[0]
    previous = jnp.concatenate([jnp.full((1,), -1, jnp.int32), sorted_ids[:-1]])
    first = (sorted_ids != previous) & (sorted_ids >= hot)
    owner = sorted_ids // shard_rows
    rank = running_count(first) - 1
    owners = jnp.arange(shards, dtype=jnp.int32)
    counts = jnp.sum((first[None, :] & (owner[None, :] == owners[:, None])).astype(jnp.int32), axis=1)
    starts = jnp.sum(jnp.where(owners[None, :] < owners[:, None], counts[None, :], 0), axis=1)
    start_of = jnp.sum(jnp.where(owner[:, None] == owners[None, :], starts[None, :], 0), axis=1)
    packed = lax.sort(jnp.where(first, sorted_ids, jnp.int32(2**30)))
    packed = jnp.concatenate([packed, jnp.full((capacity,), 2**30, jnp.int32)])
    asked = jnp.stack([lax.dynamic_slice(packed, (starts[s],), (capacity,)) for s in range(shards)])
    return owner, rank - start_of, asked, jnp.max(counts)


def cell_of(sorted_ids, owner, rank, shards, hot, capacity):
    return jnp.where(sorted_ids < hot, shards * capacity + sorted_ids, owner * capacity + rank)


def round_rows(rows, block=512):
    def body(x_ref, y_ref):
        y_ref[...] = x_ref[...].astype(jnp.bfloat16)

    spec = pl.BlockSpec((block, rows.shape[1]), lambda i: (i, 0))
    return pl.pallas_call(body, grid=(rows.shape[0] // block,), in_specs=[spec], out_specs=spec, out_shape=jax.ShapeDtypeStruct(rows.shape, jnp.bfloat16))(rows)


def exchange(rows, shards):
    return lax.all_to_all(rows.reshape(shards, -1, rows.shape[-1]), AXIS_NAME, 0, 0).reshape(rows.shape)


def solution(mesh):
    shards = mesh.shape[AXIS_NAME]

    def device_step(in_shard, out_shard, center_ids, context_ids, negative_ids):
        shard_rows = in_shard.shape[0]
        num_pairs = center_ids.shape[0]
        num_negs = negative_ids.shape[0]
        hot = HOT_ROWS
        me = lax.axis_index(AXIS_NAME)
        full_pairs, full_negs = unique_capacity(num_pairs, shards), unique_capacity(num_negs, shards)
        tight_pairs, tight_negs = tight_capacity(num_pairs, shards), tight_capacity(num_negs, shards)

        hot_both = jnp.concatenate([in_shard[:hot], out_shard[:hot]])
        hot_both = lax.psum(jnp.where(me == 0, hot_both, 0.0), AXIS_NAME)
        hot_in, hot_out = hot_both[:hot], hot_both[hot:]

        neg_sorted = lax.sort(negative_ids)
        cen_sorted, con_moved = lax.sort((center_ids, context_ids), num_keys=1)
        con_sorted, con_pos = lax.sort((con_moved, jnp.arange(num_pairs, dtype=jnp.int32)), num_keys=1)
        neg_owner, neg_rank, neg_asked, neg_max = plan_unique(neg_sorted, shard_rows, shards, hot, full_negs)
        cen_owner, cen_rank, cen_asked, cen_max = plan_unique(cen_sorted, shard_rows, shards, hot, full_pairs)
        con_owner, con_rank, con_asked, con_max = plan_unique(con_sorted, shard_rows, shards, hot, full_pairs)
        fits = (neg_max <= tight_negs) & (cen_max <= tight_pairs) & (con_max <= tight_pairs)
        spill = jnp.broadcast_to(1 - fits.astype(jnp.int32), (shards, 1))
        asked = lax.all_to_all(jnp.concatenate([neg_asked, cen_asked, con_asked, spill], axis=1), AXIS_NAME, 0, 0)
        all_fit = jnp.sum(asked[:, -1]) == 0
        local = jnp.clip(asked[:, :-1] - me * shard_rows, 0, shard_rows - 1)
        neg_local = local[:, :full_negs]
        cen_local = local[:, full_negs:full_negs + full_pairs]
        con_local = local[:, full_negs + full_pairs:]

        def run(cap_pairs, cap_negs, in_shard, out_shard, hot_in, hot_out, neg_local, cen_local, con_local):
            neg_rows = neg_local[:, :cap_negs].reshape(-1)
            cen_rows = cen_local[:, :cap_pairs].reshape(-1)
            con_rows = con_local[:, :cap_pairs].reshape(-1)
            neg_cell = cell_of(neg_sorted, neg_owner, neg_rank, shards, hot, cap_negs)
            cen_cell = cell_of(cen_sorted, cen_owner, cen_rank, shards, hot, cap_pairs)
            con_cell = cell_of(con_sorted, con_owner, con_rank, shards, hot, cap_pairs)
            con_cell = lax.sort((con_pos, con_cell), num_keys=1)[1]

            take = functools.partial(jnp.take, axis=0, mode='clip')
            neg_got = exchange(take(out_shard, neg_rows), shards)
            cen_send = take(in_shard, cen_rows)
            cen_send, neg_got = lax.optimization_barrier((cen_send, neg_got))
            cen_got = exchange(cen_send, shards)
            con_send = take(out_shard, con_rows)
            con_send, cen_got = lax.optimization_barrier((con_send, cen_got))
            con_got = exchange(con_send, shards)

            negative_half = round_rows(take(jnp.concatenate([neg_got, hot_out]), neg_cell))
            center_vec = take(jnp.concatenate([cen_got, hot_in]), cen_cell)
            center_half = center_vec.astype(jnp.bfloat16)
            neg_scale = NEG_WEIGHT / num_negs
            neg_score = lax.dot_general(center_half, negative_half, (((1,), (1,)), ((), ())), preferred_element_type=jnp.float32)
            neg_grad = (neg_scale * jax.nn.sigmoid(neg_score)).astype(jnp.bfloat16)
            d_negative = lax.dot_general(neg_grad, center_half, (((0,), (0,)), ((), ())), preferred_element_type=jnp.float32)
            neg_sum = jax.ops.segment_sum(d_negative, neg_cell, num_segments=shards * cap_negs + hot, indices_are_sorted=False)
            d_center = jnp.dot(neg_grad, negative_half, preferred_element_type=jnp.float32)

            context_vec = take(jnp.concatenate([con_got, hot_out]), con_cell)
            pos_score = jnp.sum(center_vec * context_vec, axis=1)
            pos_grad = (jax.nn.sigmoid(pos_score) - 1.0)[:, None]
            d_context = pos_grad * center_vec
            con_sum = jax.ops.segment_sum(d_context, con_cell, num_segments=shards * cap_pairs + hot)
            d_center = d_center + pos_grad * context_vec
            cen_sum = jax.ops.segment_sum(d_center, cen_cell, num_segments=shards * cap_pairs + hot)

            neg_back = exchange(neg_sum[:shards * cap_negs], shards)
            con_part = con_sum[:shards * cap_pairs]
            con_part, neg_back = lax.optimization_barrier((con_part, neg_back))
            con_back = exchange(con_part, shards)
            cen_part = cen_sum[:shards * cap_pairs]
            cen_part, con_back = lax.optimization_barrier((cen_part, con_back))
            cen_back = exchange(cen_part, shards)
            out_hot = con_sum[shards * cap_pairs:] + neg_sum[shards * cap_negs:]
            hot_sum = lax.psum(jnp.concatenate([cen_sum[shards * cap_pairs:], out_hot]), AXIS_NAME)
            hot_sum = jnp.where(me == 0, hot_sum, 0.0)

            new_out = out_shard.at[neg_rows].add(-neg_back).at[con_rows].add(-con_back).at[:hot].add(-hot_sum[hot:])
            new_in = in_shard.at[cen_rows].add(-cen_back).at[:hot].add(-hot_sum[:hot])
            return new_in, new_out

        return lax.cond(all_fit, functools.partial(run, tight_pairs, tight_negs), functools.partial(run, full_pairs, full_negs), in_shard, out_shard, hot_in, hot_out, neg_local, cen_local, con_local)

    return jax.shard_map(device_step, mesh=mesh, in_specs=(P(AXIS_NAME, None), P(AXIS_NAME, None), P(AXIS_NAME), P(AXIS_NAME), P(AXIS_NAME)), out_specs=(P(AXIS_NAME, None), P(AXIS_NAME, None)), check_vma=False)
```

time: 6870 us -> 1440 us (0.21)
  waiting for transfers between devices: 3840 us -> 432 us
  local copies, waits for them, and re-layouts: 1650 us -> 266 us
  other arithmetic: 1090 us -> 426 us
    all_to_all x6 -> x7, waiting for transfers between devices: 3840 us -> 183 us  [the longest x6 183 us: exchange(): lax.all_to_all(rows.reshape(shards, -1, rows.shape[-1]), AXIS_NAME, 0, 0)]
    gather x12 -> x6, local copies, waits for them, and re-layouts: 1490 us -> 195 us  [the longest x1 45.6 us: run(): center_vec = take(jnp.concatenate([cen_got, hot_in]), cen_cell)]
    scatter-add x4 -> x7, other arithmetic: 634 us -> 298 us  [the longest x3 86.8 us: run(): out_shard.at[neg_rows].add(-neg_back).at[con_rows].add(-con_back).at[:hot]]
    select_n x17 -> x7, other arithmetic: 327 us -> 7.49 us  [the longest x1 4.8 us: run(): hot_sum = jnp.where(me == 0, hot_sum, 0.0)]
    psum x0 -> x2, waiting for transfers between devices: none -> 249 us  [the longest x1 176 us: run(): lax.psum(jnp.concatenate([cen_sum[shards * cap_pairs:], out_hot]), AXIS_N...]
    scatter x4 -> x0, local copies, waits for them, and re-layouts: 153 us -> none  [the longest x2 76.6 us: send_layout(): cell_of_id = jnp.zeros_like(id_list).at[sort_order].set(cell_sorted)]
    dot_general x3 -> x9, matrix products: 205 us -> 197 us  [the longest x1 71.3 us: run(): lax.dot_general(center_half, negative_half, (((1,), (1,)), ((), ())), pre...]
  transfers between devices with their start and end apart: 6 -> 9, of which waited for: 4 -> 5; matrix products, arithmetic and copies ran while one was open for 25% -> 51% of each run, Pallas kernels for 0% -> 1%
where the time goes in v1:
time: 1440 us; the launch traced here: 1430 us
  waiting for transfers between devices  432 us (30%)
  other arithmetic  426 us (30%)
  local copies, waits for them, and re-layouts  266 us (18%)
  matrix products  197 us (14%)
  between operations  62 us (4%)
  starting transfers between devices  29.7 us (2%)
    all_to_all x6, waiting for transfers between devices, exchange(): lax.all_to_all(rows.reshape(shards, -1, rows.shape[-1]), AXIS_NAME, 0, 0)  183 us
    psum x1, waiting for transfers between devices, run(): lax.psum(jnp.concatenate([cen_sum[shards * cap_pairs:], out_hot]), AXIS_N...  176 us
    scatter-add x3, other arithmetic, run(): out_shard.at[neg_rows].add(-neg_back).at[con_rows].add(-con_back).at[:hot]  86.8 us
    psum x1, waiting for transfers between devices, device_step(): hot_both = lax.psum(jnp.where(me == 0, hot_both, 0.0), AXIS_NAME)  73.7 us
    dot_general x1, matrix products, run(): lax.dot_general(center_half, negative_half, (((1,), (1,)), ((), ())), pre...  71.3 us
    scatter-add x1, other arithmetic, run(): jax.ops.segment_sum(d_center, cen_cell, num_segments=shards * cap_pairs +...  66.2 us
    scatter-add x1, other arithmetic, run(): jax.ops.segment_sum(d_context, con_cell, num_segments=shards * cap_pairs...  65.4 us
    dot_general x1, matrix products, run(): lax.dot_general(neg_grad, center_half, (((0,), (0,)), ((), ())), preferre...  64.6 us
  transfers between devices with their start and end apart: 9, of which 5 were waited for; matrix products, arithmetic and copies ran while one was open for 51% of the time, Pallas kernels for 1%

profile of v1, /device:TPU:0, one launch (start us, length us, event | category | flops | bytes accessed | tf_op | source)
XLA Modules:
  0.0 1427.4 jit_solution(12546774032459475252)
XLA Ops:
  7.2 15.1 %copy.37 = f32[6288,768]{1,0:T(8,128)} copy(f32[6288,768]{1,0:T(8,128)} %param.15) | data formatting | bytes 38633472
  26.2 7.3 copy.38
  101.7 7.0 sort.145
  138.6 73.7 %all-reduce.11.cloned.1.call-done = f32[1536,768]{1,0:T(8,128)} async-done(((f32[1536,768]{1,0:T(8,128)}), f32[1536,768]{1,0:T(8,128)}) %all-reduce.11.cloned.1.call-update) | async-done | bytes 4718608 | tf_op jit(solution)/shard_map/psum | solution.py:80
  212.4 1207.7 %conditional.1 = (f32[6288,768]{1,0:T(8,128)}, f32[6288,768]{1,0:T(8,128)}) conditional(s32[]{:T(128)} %convert_element_type.52, (s32[8,3520]{1,0:T(8,128)S(1)}, s32[8192]{0:T(1024)}, s32[8192]{0:T(1024)}, s32[64,128]{1,0:T(8,128)S(1)}, s32[8,3520]{1,0:T(8,128)S(1)}, /*index=5*/f32[6288,768]{1,0:T(8,128)}, f32[6288,768]{1,0:T(8,128)}, ...), branch_computations={%region_20.30_spmd, %region_30.40_spmd} | conditional | flops 154920370176 | bytes 2078214528 | solution.py:149
  216.7 16.9 %gather_fusion.8 = f32[2560,768]{1,0:T(8,128)} fusion(f32[6288,768]{1,0:T(8,128)} %get-tuple-element.162, s32[3072]{0:T(1024)S(1)} %pad_clamp_fusion.1), kind=kCustom, calls=%fused_computation.8 | custom fusion | bytes 15738880 | tf_op jit(solution)/shard_map/cond/branch_1_fun/jit(_take)/gather | solution.py:108
  237.9 31.6 %gather_fusion.7 = f32[5120,768]{1,0:T(8,128)} fusion(f32[6288,768]{1,0:T(8,128)} %get-tuple-element.157, s32[5120]{0:T(1024)S(1)} %broadcast_clamp_fusion.7), kind=kCustom, calls=%fused_computation.7 | custom fusion | bytes 31477760 | tf_op jit(solution)/shard_map/cond/branch_1_fun/jit(_take)/gather | solution.py:109
  269.5 56.1 %all-to-all-done = f32[8,320,768]{2,1,0:T(8,128)} async-done(((f32[8,320,768]{2,1,0:T(8,128)}), f32[8,320,768]{2,1,0:T(8,128)}, u32[]{:S(2)}, u32[]{:S(2)}) %all-to-all-start) | async-done | bytes 7864352 | tf_op jit(solution)/shard_map/cond/branch_1_fun/all_to_all | solution.py:64
  336.0 31.5 %gather_fusion.6 = f32[5120,768]{1,0:T(8,128)} fusion(f32[6288,768]{1,0:T(8,128)} %get-tuple-element.162, s32[5120]{0:T(1024)S(1)} %broadcast_clamp_fusion.8), kind=kCustom, calls=%fused_computation.6 | custom fusion | bytes 31477760 | tf_op jit(solution)/shard_map/cond/branch_1_fun/jit(_take)/gather | solution.py:112
  369.2 7.8 pad_maximum_fusion.6
  377.0 24.2 %gather_fusion.10 = f32[4096,768]{1,0:T(8,128)} fusion(f32[3328,768]{1,0:T(8,128)} %pad_maximum_fusion.6, s32[4096]{0:T(1024)S(1)} %get-tuple-element.312), kind=kCustom, calls=%fused_computation.10 | custom fusion | bytes 25182208 | tf_op jit(solution)/shard_map/cond/branch_1_fun/jit(_take)/gather | solution.py:116
  401.1 9.3 branch_1_fun.1
  410.4 92.2 %all-to-all-done.1 = f32[8,640,768]{2,1,0:T(8,128)} async-done(((f32[8,640,768]{2,1,0:T(8,128)}), f32[8,640,768]{2,1,0:T(8,128)}, u32[]{:S(2)}, u32[]{:S(2)}) %all-to-all-start.1) | async-done | bytes 15728672 | tf_op jit(solution)/shard_map/cond/branch_1_fun/all_to_all | solution.py:64
  507.3 13.9 pad_maximum_fusion.4
  521.2 45.6 %gather_fusion.9 = f32[8192,768]{1,0:T(8,128)} fusion(f32[5888,768]{1,0:T(8,128)} %pad_maximum_fusion.4, s32[8192]{0:T(1024)S(1)} %get-tuple-element.310), kind=kCustom, calls=%fused_computation.9 | custom fusion | bytes 50364416 | tf_op jit(solution)/shard_map/cond/branch_1_fun/jit(_take)/gather | solution.py:117
  566.7 71.3 %multiply_convert_fusion.1 = bf16[8192,4096]{1,0:T(8,128)(2,1)} fusion(bf16[4096,768]{1,0:T(8,128)(2,1)} %branch_1_fun.1, f32[8192,768]{1,0:T(8,128)} %gather_fusion.9), kind=kOutput, calls=%fused_computation.81 | convolution fusion | flops 51713671168 | bytes 98566144 | tf_op jit(solution)/shard_map/cond/branch_1_fun/dot_general | solution.py:120
  638.1 64.6 %fusion.42 = f32[4096,768]{1,0:T(8,128)} fusion(bf16[8192,4096]{1,0:T(8,128)(2,1)} %multiply_convert_fusion.1, f32[8192,768]{1,0:T(8,128)} %gather_fusion.9), kind=kOutput, calls=%fused_computation.99 | convolution fusion | flops 51545899008 | bytes 104857600 | tf_op jit(solution)/shard_map/cond/branch_1_fun/dot_general | solution.py:122
  702.6 32.0 %scatter_custom_fusion.8 = f32[3328,768]{1,0:T(8,128)} fusion(s32[4096]{0:T(1024)} %get-tuple-element.313, f32[4096,768]{1,0:T(8,128)} %fusion.42, f32[]{:T(128)} %constant.181.clone), kind=kCustom, calls=%fused_computation.102 | custom fusion | flops 3145728 | bytes 10224128 | tf_op jit(solution)/shard_map/cond/branch_1_fun/scatter-add | solution.py:123
  752.2 13.8 pad_maximum_fusion.5
  766.1 45.5 %gather_fusion.11 = f32[8192,768]{1,0:T(8,128)} fusion(f32[5888,768]{1,0:T(8,128)} %pad_maximum_fusion.5, s32[8192]{0:T(1024)S(1)} %broadcast_clamp_fusion.5), kind=kCustom, calls=%fused_computation.11 | custom fusion | bytes 50364416 | tf_op jit(solution)/shard_map/cond/branch_1_fun/jit(_take)/gather | solution.py:126
  811.6 16.4 %multiply_reduce_fusion.1 = f32[8192]{0:T(1024)S(1)} fusion(f32[8192,768]{1,0:T(8,128)} %gather_fusion.9, f32[8192,768]{1,0:T(8,128)} %gather_fusion.11), kind=kLoop, calls=%fused_computation.87 | loop fusion | flops 12574720 | bytes 50364416 | tf_op jit(solution)/shard_map/cond/branch_1_fun/reduce_sum | solution.py:127
  828.1 65.4 %scatter_custom_fusion.7 = f32[5888,768]{1,0:T(8,128)} fusion(s32[8192]{0:T(1024)S(1)} %get-tuple-element.178, f32[8192,768]{1,0:T(8,128)} %gather_fusion.9, f32[8192]{0:T(1024)S(1)} %divide_add_fusion.1, f32[]{:T(128)} %constant.181.clone), kind=kCustom, calls=%fused_computation.82 | custom fusion | flops 12582912 | bytes 43286532 | tf_op jit(solution)/shard_map/cond/branch_1_fun/scatter-add | solution.py:130
  893.5 12.0 slice.340
  909.8 60.0 %fusion.95 = f32[8192,768]{1,0:T(8,128)} fusion(bf16[8192,4096]{1,0:T(8,128)(2,1)} %multiply_convert_fusion.1, bf16[4096,768]{1,0:T(8,128)(2,1)} %branch_1_fun.1), kind=kOutput, calls=%fused_computation.233 | convolution fusion | flops 51539607552 | bytes 98566144 | tf_op jit(solution)/shard_map/cond/branch_1_fun/dot_general | solution.py:124
  969.8 66.2 %scatter_custom_fusion.6 = f32[5888,768]{1,0:T(8,128)} fusion(s32[8192]{0:T(1024)} %get-tuple-element.311, f32[8192,768]{1,0:T(8,128)} %fusion.95, f32[8192,768]{1,0:T(8,128)} %gather_fusion.11, f32[8192]{0:T(1024)S(1)} %divide_add_fusion.1, f32[]{:T(128)} %constant.181.clone), kind=kCustom, calls=%fused_computation.84 | custom fusion | flops 18874368 | bytes 68452864 | tf_op jit(solution)/shard_map/cond/branch_1_fun/scatter-add | solution.py:132
  1036.0 11.9 slice.339
  1048.0 34.6 %all-to-all-done.4 = f32[8,640,768]{2,1,0:T(8,128)} async-done(((f32[8,640,768]{2,1,0:T(8,128)}), f32[8,640,768]{2,1,0:T(8,128)}, u32[]{:S(2)}, u32[]{:S(2)}) %all-to-all-start.4) | async-done | bytes 15728672 | tf_op jit(solution)/shard_map/cond/branch_1_fun/all_to_all | solution.py:64
  1092.6 31.8 %scatter_custom_fusion.10 = f32[6288,768]{1,0:T(8,128)} fusion(f32[6288,768]{1,0:T(8,128)} %get-tuple-element.162, s32[2560]{0:T(1024)S(1)} %fusion.57, f32[2560,768]{1,0:T(8,128)} %bitcast.28), kind=kCustom, calls=%fused_computation.97 | custom fusion | flops 3932160 | bytes 27181056 | tf_op jit(solution)/shard_map/cond/branch_1_fun/scatter-add | solution.py:145
  1124.4 175.6 %all-reduce.9.cloned.1.call-done = f32[1536,768]{1,0:T(8,128)} async-done(((f32[1536,768]{1,0:T(8,128)}), f32[1536,768]{1,0:T(8,128)}) %all-reduce.9.cloned.1.call-update) | async-done | bytes 4718608 | tf_op jit(solution)/shard_map/cond/branch_1_fun/psum | solution.py:142
  1304.7 48.5 %scatter_custom_fusion.11 = f32[6288,768]{1,0:T(8,128)} fusion(f32[6288,768]{1,0:T(8,128)} %scatter_custom_fusion.10, s32[5120]{0:T(1024)S(1)} %bitcast.178, f32[5120,768]{1,0:T(8,128)} %bitcast.30), kind=kCustom, calls=%fused_computation.90 | custom fusion | flops 7864320 | bytes 35045376 | tf_op jit(solution)/shard_map/cond/branch_1_fun/scatter-add | solution.py:145
  1353.2 12.6 neg.50
  1365.8 47.5 %scatter_fusion.1 = f32[6288,768]{1,0:T(8,128)} fusion(f32[6288,768]{1,0:T(8,128)} %get-tuple-element.157, s32[5120]{0:T(1024)S(1)} %bitcast.174, f32[5120,768]{1,0:T(8,128)} %bitcast.161), kind=kCustom, calls=%fused_computation.21 | custom fusion | flops 3932160 | bytes 47206400 | tf_op jit(solution)/shard_map/cond/branch_1_fun/scatter-add | solution.py:146
  (189 shorter events, 118.9 us)
Async XLA Ops:
  26.2 25.2 %copy-start.62 = (s32[8192]{0:T(1024)S(1)}, s32[8192]{0:T(1024)}, u32[]{:S(2)}) copy-start(s32[8192]{0:T(1024)} %param.17) | copy-start | bytes 98308
  26.2 25.2 %copy-start.63 = (s32[8192]{0:T(1024)S(1)}, s32[8192]{0:T(1024)}, u32[]{:S(2)}) copy-start(s32[8192]{0:T(1024)} %param.18) | copy-start | bytes 98308
  26.2 106.9 %slice-start = ((f32[6288,768]{1,0:T(8,128)}), f32[768,768]{1,0:T(8,128)S(1)}, s32[]{:S(2)}) async-start(f32[6288,768]{1,0:T(8,128)} %copy.37), calls=%async_computation.16 | async-start | bytes 4718592 | tf_op jit(solution)/shard_map/slice | solution.py:79
  39.2 25.8 %copy-start.35 = (s32[4096]{0:T(1024)}, s32[4096]{0:T(1024)S(1)}, u32[]{:S(2)}) copy-start(s32[4096]{0:T(1024)S(1)} %get-tuple-element.194) | copy-start | bytes 49156
  40.1 172.3 %copy-start.20 = (s32[4096]{0:T(1024)S(1)}, s32[4096]{0:T(1024)}, u32[]{:S(2)}) copy-start(s32[4096]{0:T(1024)} %copy-done.19) | copy-start | bytes 49156
  40.2 24.9 %copy-start.53 = (s32[8]{0:T(128)}, s32[8]{0:T(128)S(1)}, u32[]{:S(2)}) copy-start(s32[8]{0:T(128)S(1)} %select_reduce_fusion.8) | copy-start | bytes 100
  58.3 153.9 %copy-start.23 = (s32[8192]{0:T(1024)}, s32[8192]{0:T(1024)S(1)}, u32[]{:S(2)}) copy-start(s32[8192]{0:T(1024)S(1)} %get-tuple-element.196) | copy-start | bytes 98308
  65.1 147.2 %copy-start.26 = (s32[8192]{0:T(1024)}, s32[8192]{0:T(1024)S(1)}, u32[]{:S(2)}) copy-start(s32[8192]{0:T(1024)S(1)} %get-tuple-element.199) | copy-start | bytes 98308
  65.1 147.3 %copy-start.36 = (s32[4096]{0:T(1024)S(1)}, s32[4096]{0:T(1024)}, u32[]{:S(2)}) copy-start(s32[4096]{0:T(1024)} %copy-done.35) | copy-start | bytes 49156
  65.2 147.0 %copy-start.14 = (s32[8192]{0:T(1024)}, s32[8192]{0:T(1024)S(1)}, u32[]{:S(2)}) copy-start(s32[8192]{0:T(1024)S(1)} %get-tuple-element.389) | copy-start | bytes 98308
  66.0 146.4 %copy-start.11 = (s32[8192]{0:T(1024)S(1)}, s32[8192]{0:T(1024)}, u32[]{:S(2)}) copy-start(s32[8192]{0:T(1024)} %copy-done.10) | copy-start | bytes 98308
  66.8 21.6 %copy-start.56 = (s32[8]{0:T(128)}, s32[8]{0:T(128)S(1)}, u32[]{:S(2)}) copy-start(s32[8]{0:T(128)S(1)} %select_reduce_fusion.6) | copy-start | bytes 100
  126.9 10.3 all-to-all-start.12
  131.2 81.0 %all-reduce.11.cloned.1.call-start = ((), (), s32[]{:S(2)}) async-start(), calls=%async_computation.15 | async-start | bytes 9437184 | tf_op jit(solution)/shard_map/psum | solution.py:80
  233.5 92.0 %all-to-all-start = ((f32[8,320,768]{2,1,0:T(8,128)}), f32[8,320,768]{2,1,0:T(8,128)}, u32[]{:S(2)}, u32[]{:S(2)}) async-start(f32[8,320,768]{2,1,0:T(8,128)} %bitcast.165), calls=%async_computation | async-start | bytes 15728640 | tf_op jit(solution)/shard_map/cond/branch_1_fun/all_to_all | solution.py:64
  325.6 177.1 %all-to-all-start.1 = ((f32[8,640,768]{2,1,0:T(8,128)}), f32[8,640,768]{2,1,0:T(8,128)}, u32[]{:S(2)}, u32[]{:S(2)}) async-start(f32[8,640,768]{2,1,0:T(8,128)} %bitcast.163), calls=%async_computation.1 | async-start | bytes 31457280 | tf_op jit(solution)/shard_map/cond/branch_1_fun/all_to_all | solution.py:64
  331.8 37.4 %copy-start = (f32[768,768]{1,0:T(8,128)}, f32[768,768]{1,0:T(8,128)S(1)}, u32[]{:S(2)}) copy-start(f32[768,768]{1,0:T(8,128)S(1)} %slice.301) | copy-start | bytes 7077892 | tf_op jit(solution)/shard_map/cond
  335.9 31.6 %copy-start.55 = (s32[8]{0:T(128)S(1)}, s32[8]{0:T(128)}, u32[]{:S(2)}) copy-start(s32[8]{0:T(128)} %get-tuple-element.287) | copy-start | bytes 100 | tf_op jit(solution)/shard_map/cond
  335.9 31.7 %copy-start.16 = (s32[8192]{0:T(1024)S(1)}, s32[8192]{0:T(1024)}, u32[]{:S(2)}) copy-start(s32[8192]{0:T(1024)} %get-tuple-element.297) | copy-start | bytes 98308 | tf_op jit(solution)/shard_map/cond
  335.9 31.7 %copy-start.58 = (s32[8]{0:T(128)S(1)}, s32[8]{0:T(128)}, u32[]{:S(2)}) copy-start(s32[8]{0:T(128)} %get-tuple-element.295) | copy-start | bytes 100 | tf_op jit(solution)/shard_map/cond
  335.9 31.7 %copy-start.61 = (s32[8]{0:T(128)S(1)}, s32[8]{0:T(128)}, u32[]{:S(2)}) copy-start(s32[8]{0:T(128)} %get-tuple-element.279) | copy-start | bytes 100 | tf_op jit(solution)/shard_map/cond
  335.9 32.6 %copy-start.25 = (s32[8192]{0:T(1024)S(1)}, s32[8192]{0:T(1024)}, u32[]{:S(2)}) copy-start(s32[8192]{0:T(1024)} %get-tuple-element.159) | copy-start | bytes 98308 | tf_op jit(solution)/shard_map/cond
  336.0 32.6 %copy-start.28 = (s32[8192]{0:T(1024)S(1)}, s32[8192]{0:T(1024)}, u32[]{:S(2)}) copy-start(s32[8192]{0:T(1024)} %get-tuple-element.175) | copy-start | bytes 98308 | tf_op jit(solution)/shard_map/cond
  410.4 96.8 %copy-start.5 = (f32[768,768]{1,0:T(8,128)S(1)}, f32[768,768]{1,0:T(8,128)}, u32[]{:S(2)}) copy-start(f32[768,768]{1,0:T(8,128)} %slice.299) | copy-start | bytes 7077892 | tf_op jit(solution)/shard_map/cond
  502.7 238.8 %all-to-all-start.2 = ((f32[8,640,768]{2,1,0:T(8,128)}), f32[8,640,768]{2,1,0:T(8,128)}, u32[]{:S(2)}, u32[]{:S(2)}) async-start(f32[8,640,768]{2,1,0:T(8,128)} %bitcast.162), calls=%async_computation.2 | async-start | bytes 31457280 | tf_op jit(solution)/shard_map/cond/branch_1_fun/all_to_all | solution.py:64
  702.6 42.7 %copy-start.46 = (s32[8192]{0:T(1024)S(1)}, s32[8192]{0:T(1024)}, u32[]{:S(2)}) copy-start(s32[8192]{0:T(1024)} %get-tuple-element.174) | copy-start | bytes 98308 | tf_op jit(solution)/shard_map/cond
  702.6 42.7 %copy-start.47 = (s32[8192]{0:T(1024)S(1)}, s32[8192]{0:T(1024)}, u32[]{:S(2)}) copy-start(s32[8192]{0:T(1024)} %get-tuple-element.335) | copy-start | bytes 98308 | tf_op jit(solution)/shard_map/cond
  702.6 49.6 %copy-start.1 = (f32[768,768]{1,0:T(8,128)S(1)}, f32[768,768]{1,0:T(8,128)}, u32[]{:S(2)}) copy-start(f32[768,768]{1,0:T(8,128)} %copy-done) | copy-start | bytes 7077892 | tf_op jit(solution)/shard_map/cond
  741.5 164.0 %all-to-all-start.3 = ((f32[8,320,768]{2,1,0:T(8,128)}), f32[8,320,768]{2,1,0:T(8,128)}, u32[]{:S(2)}, u32[]{:S(2)}) async-start(f32[8,320,768]{2,1,0:T(8,128)} %bitcast.164), calls=%async_computation.3 | async-start | bytes 15728640 | tf_op jit(solution)/shard_map/cond/branch_1_fun/all_to_all | solution.py:64
  905.4 177.1 %all-to-all-start.4 = ((f32[8,640,768]{2,1,0:T(8,128)}), f32[8,640,768]{2,1,0:T(8,128)}, u32[]{:S(2)}, u32[]{:S(2)}) async-start(f32[8,640,768]{2,1,0:T(8,128)} %bitcast.160), calls=%async_computation.4 | async-start | bytes 31457280 | tf_op jit(solution)/shard_map/cond/branch_1_fun/all_to_all | solution.py:64
  1082.5 270.7 %all-to-all-start.5 = ((f32[8,640,768]{2,1,0:T(8,128)}), f32[8,640,768]{2,1,0:T(8,128)}, u32[]{:S(2)}, u32[]{:S(2)}) async-start(f32[8,640,768]{2,1,0:T(8,128)} %bitcast.159), calls=%async_computation.5 | async-start | bytes 31457280 | tf_op jit(solution)/shard_map/cond/branch_1_fun/all_to_all | solution.py:64
  1087.1 212.9 %all-reduce.9.cloned.1.call-start = ((), (), s32[]{:S(2)}) async-start(), calls=%async_computation.14 | async-start | bytes 9437184 | tf_op jit(solution)/shard_map/cond/branch_1_fun/psum | solution.py:142
  (10 other events, 88.3 us)
Sparse Core Ops, SparseCore 0:
  135.7 76.5 all-reduce.10
  1092.4 207.4 all-reduce.8

commit v2 on v0

v2 whole, which is shorter than its diff:
```python
import functools

import jax
import jax.numpy as jnp
from jax import lax
from jax.experimental import pallas as pl
from jax.experimental.pallas import tpu as pltpu
from jax.sharding import PartitionSpec as P

LEARN_RATE = 1.0
NEG_WEIGHT = 5.0
AXIS_NAME = 'vp'
HOT_ROWS = 768
LANES = 128
SUBLANES = 8
NO_ID = 2**30
VMEM_BYTES = 60 * 2**20
ANY = pl.BlockSpec(memory_space=pl.ANY)


def unique_capacity(num_ids, shards):
    common_slots = 3 * num_ids // shards
    return common_slots // 4 + (num_ids - common_slots + shards - 1) // shards


def tight_capacity(num_ids, shards):
    return (num_ids - 3 * num_ids // shards + shards - 1) // shards


def tile_view(rows):
    n, d = rows.shape
    return rows.reshape(n // SUBLANES, SUBLANES, d // LANES, LANES).transpose(0, 2, 1, 3).reshape(n * d // LANES, LANES)


def row_view(lines, d):
    n = lines.shape[0] * LANES // d
    return lines.reshape(n // SUBLANES, d // LANES, SUBLANES, LANES).transpose(0, 2, 1, 3).reshape(n, d)


def first_line(row, d):
    return (row // SUBLANES) * (SUBLANES * (d // LANES)) + row % SUBLANES


def gather_rows(table, rows, groups):
    n, d = rows.shape[0], table.shape[1]
    chunks, cap = d // LANES, n // groups
    view = tile_view(table)

    def body(line, t_ref, o_ref):
        group = pl.program_id(0)

        def step(t, carry):
            start = group * cap + t * SUBLANES
            got = [t_ref[pl.ds(line[start + j], chunks, stride=SUBLANES), :] for j in range(SUBLANES)]
            for j in range(SUBLANES):
                o_ref[pl.ds(t * SUBLANES * chunks + j, chunks, stride=SUBLANES), :] = got[j]
            return carry

        lax.fori_loop(0, cap // SUBLANES, step, 0, unroll=4)

    out = pl.pallas_call(
        body,
        grid_spec=pltpu.PrefetchScalarGridSpec(
            num_scalar_prefetch=1, grid=(groups,),
            in_specs=[pl.BlockSpec(view.shape, lambda s, i: (0, 0), pipeline_mode=pl.Buffered(1))],
            out_specs=pl.BlockSpec((cap * chunks, LANES), lambda s, i: (s, 0))),
        out_shape=jax.ShapeDtypeStruct((n * chunks, LANES), table.dtype),
        cost_estimate=pl.CostEstimate(flops=0, bytes_accessed=4 * d * (table.shape[0] + 3 * n), transcendentals=0),
        compiler_params=pltpu.CompilerParams(vmem_limit_bytes=VMEM_BYTES),
        name='gather_rows',
    )(first_line(rows, d), view)
    return row_view(out, d)


def pair_sums(x_hot, x_got, y_hot, y_got, x_row, y_row):
    d = x_hot.shape[1]
    chunks, pairs = d // LANES, x_row.shape[0]
    views = [tile_view(a) for a in (x_hot, x_got, y_hot, y_got)]
    xh_lines, xg_lines, yh_lines, yg_lines = [v.shape[0] for v in views]
    x_lines, y_lines = xh_lines + xg_lines, yh_lines + yg_lines

    def body(x_line, y_line, xh, xg, yh, yg, oh, og, x_all, y_all, total, sem):
        copies = [
            pltpu.make_async_copy(xh, x_all.at[pl.ds(0, xh_lines)], sem.at[0]),
            pltpu.make_async_copy(xg, x_all.at[pl.ds(xh_lines, xg_lines)], sem.at[1]),
            pltpu.make_async_copy(yh, y_all.at[pl.ds(0, yh_lines)], sem.at[2]),
            pltpu.make_async_copy(yg, y_all.at[pl.ds(yh_lines, yg_lines)], sem.at[3]),
        ]
        for copy in copies:
            copy.start()

        def zero(t, carry):
            total[pl.ds(pl.multiple_of(t * 64, 64), 64), :] = jnp.zeros((64, LANES), jnp.float32)
            return carry

        lax.fori_loop(0, y_lines // 64, zero, 0)
        for copy in copies:
            copy.wait()

        def step(t, carry):
            run, last = carry
            kept, parts, lines = [], [], []
            for j in range(SUBLANES):
                line = y_line[t * SUBLANES + j]
                x = x_all[pl.ds(x_line[t * SUBLANES + j], chunks, stride=SUBLANES), :]
                y = y_all[pl.ds(line, chunks, stride=SUBLANES), :]
                kept.append(x)
                lines.append(line)
                parts.append(jnp.sum(x * y, axis=0, keepdims=True))
            score = jnp.sum(jnp.concatenate(parts, axis=0), axis=1, keepdims=True)
            grad = jax.nn.sigmoid(score) - 1.0
            for j in range(SUBLANES):
                same = (lines[j] == last).astype(jnp.float32)
                run = run * same + grad[j:j + 1, :] * kept[j]
                total[pl.ds(lines[j], chunks, stride=SUBLANES), :] = run
                last = lines[j]
            return run, last

        lax.fori_loop(0, pairs // SUBLANES, step, (jnp.zeros((chunks, LANES), jnp.float32), jnp.int32(-1)), unroll=2)
        out_hot = pltpu.make_async_copy(total.at[pl.ds(0, yh_lines)], oh, sem.at[0])
        out_got = pltpu.make_async_copy(total.at[pl.ds(yh_lines, yg_lines)], og, sem.at[1])
        out_hot.start()
        out_got.start()
        out_hot.wait()
        out_got.wait()

    oh, og = pl.pallas_call(
        body,
        grid_spec=pltpu.PrefetchScalarGridSpec(
            num_scalar_prefetch=2, grid=(1,), in_specs=[ANY] * 4, out_specs=[ANY] * 2,
            scratch_shapes=[pltpu.VMEM((x_lines, LANES), jnp.float32), pltpu.VMEM((y_lines, LANES), jnp.float32),
                            pltpu.VMEM((y_lines, LANES), jnp.float32), pltpu.SemaphoreType.DMA((4,))]),
        out_shape=[jax.ShapeDtypeStruct((yh_lines, LANES), jnp.float32), jax.ShapeDtypeStruct((yg_lines, LANES), jnp.float32)],
        cost_estimate=pl.CostEstimate(flops=0, bytes_accessed=8 * 4 * d * pairs, transcendentals=0),
        compiler_params=pltpu.CompilerParams(vmem_limit_bytes=VMEM_BYTES),
        name='pair_sums',
    )(first_line(x_row, d), first_line(y_row, d), *views)
    return row_view(oh, d), row_view(og, d)


def subtract_rows(table, hot, parts):
    d = table.shape[1]
    chunks, batch = d // LANES, 16
    groups = parts[0][0].shape[0]
    caps = [rows.shape[1] for rows, _ in parts]
    view, hot_view = tile_view(table), tile_view(hot)
    lines = view.shape[0]
    count = len(parts)

    def body(*refs):
        line = refs[:count]
        t_hbm, h_ref = refs[count:count + 2]
        values = refs[count + 2:2 * count + 2]
        o_hbm, held, sem = refs[2 * count + 2:]
        group = pl.program_id(0)

        @pl.when(group == 0)
        def _():
            copy = pltpu.make_async_copy(t_hbm, held.at[pl.ds(0, lines)], sem)
            copy.start()
            copy.wait()

            def hot_step(t, carry):
                window = pl.ds(pl.multiple_of(t * 64, 64), 64)
                held[window, :] = held[window, :] - LEARN_RATE * h_ref[window, :]
                return carry

            lax.fori_loop(0, h_ref.shape[0] // 64, hot_step, 0)

        for p in range(count):
            def step(t, carry, p=p):
                at = [line[p][group * caps[p] + t * batch + j] for j in range(batch)]
                new = []
                for j in range(batch):
                    source = (t * (batch // SUBLANES) + j // SUBLANES) * SUBLANES * chunks + j % SUBLANES
                    value = values[p][pl.ds(source, chunks, stride=SUBLANES), :]
                    new.append(held[pl.ds(at[j], chunks, stride=SUBLANES), :] - LEARN_RATE * value)
                for j in range(batch):
                    held[pl.ds(at[j], chunks, stride=SUBLANES), :] = new[j]
                return carry

            lax.fori_loop(0, caps[p] // batch, step, 0)

        @pl.when(group == groups - 1)
        def _():
            copy = pltpu.make_async_copy(held.at[pl.ds(0, lines)], o_hbm, sem)
            copy.start()
            copy.wait()

    out = pl.pallas_call(
        body,
        grid_spec=pltpu.PrefetchScalarGridSpec(
            num_scalar_prefetch=count, grid=(groups,),
            in_specs=[ANY, pl.BlockSpec(hot_view.shape, lambda s, *i: (0, 0))] + [pl.BlockSpec((c * chunks, LANES), lambda s, *i: (s, 0)) for c in caps],
            out_specs=ANY,
            scratch_shapes=[pltpu.VMEM((lines + SUBLANES * chunks, LANES), jnp.float32), pltpu.SemaphoreType.DMA]),
        out_shape=jax.ShapeDtypeStruct((lines, LANES), jnp.float32),
        cost_estimate=pl.CostEstimate(flops=0, bytes_accessed=4 * d * (2 * table.shape[0] + 3 * groups * sum(caps)), transcendentals=0),
        compiler_params=pltpu.CompilerParams(vmem_limit_bytes=VMEM_BYTES),
        name='subtract_rows',
    )(*[first_line(rows.reshape(-1), d) for rows, _ in parts], view, hot_view, *[tile_view(values) for _, values in parts])
    return row_view(out, d)


def split_rows(sources, times, block=256):
    d = sources[0].shape[1]
    blocks = [a.shape[0] // block for a in sources]
    starts = [sum(blocks[:k]) for k in range(len(blocks))]
    total = sum(blocks) * block

    def body(*refs):
        ins, t_ref, (r_ref, h_ref, l_ref) = refs[:len(sources)], refs[len(sources)], refs[len(sources) + 1:]
        step = pl.program_id(0)
        for k, ref in enumerate(ins):
            @pl.when((step >= starts[k]) & (step < starts[k] + blocks[k]))
            def _(ref=ref):
                rounded = ref[...].astype(jnp.bfloat16)
                scaled = rounded.astype(jnp.float32) * t_ref[...]
                high = scaled.astype(jnp.bfloat16)
                r_ref[...] = rounded
                h_ref[...] = high
                l_ref[...] = (scaled - high.astype(jnp.float32)).astype(jnp.bfloat16)

    def pick(k):
        return lambda i: (jnp.clip(i - starts[k], 0, blocks[k] - 1), 0)

    spec = pl.BlockSpec((block, d), lambda i: (i, 0))
    return pl.pallas_call(
        body, grid=(sum(blocks),),
        in_specs=[pl.BlockSpec((block, d), pick(k)) for k in range(len(sources))] + [pl.BlockSpec((block, 1), lambda i: (i, 0))],
        out_specs=[spec] * 3, out_shape=[jax.ShapeDtypeStruct((total, d), jnp.bfloat16)] * 3,
        cost_estimate=pl.CostEstimate(flops=0, bytes_accessed=10 * d * total, transcendentals=0),
        name='split_rows',
    )(*sources, times.astype(jnp.float32)[:, None])


def running_count(flags):
    rows = flags.shape[0] // LANES
    grid = flags.reshape(rows, LANES).astype(jnp.bfloat16)
    upper = (jnp.arange(LANES)[:, None] <= jnp.arange(LANES)[None, :]).astype(jnp.bfloat16)
    inner = jnp.dot(grid, upper, preferred_element_type=jnp.float32)
    lower = (jnp.arange(rows)[:, None] > jnp.arange(rows)[None, :]).astype(jnp.bfloat16)
    outer = jnp.dot(lower, inner[:, -1:].astype(jnp.bfloat16), preferred_element_type=jnp.float32)
    return (inner + outer).astype(jnp.int32).reshape(-1)


def mark_unique(sorted_ids, shard_rows, shards, hot):
    previous = jnp.concatenate([jnp.full((1,), -1, jnp.int32), sorted_ids[:-1]])
    first = (sorted_ids != previous) & (sorted_ids >= hot)
    owner = sorted_ids // shard_rows
    rank = running_count(first) - 1
    owners = jnp.arange(shards, dtype=jnp.int32)
    counts = jnp.sum((first[None, :] & (owner[None, :] == owners[:, None])).astype(jnp.int32), axis=1)
    starts = jnp.sum(jnp.where(owners[None, :] < owners[:, None], counts[None, :], 0), axis=1)
    start_of = jnp.sum(jnp.where(owner[None, :] == owners[:, None], starts[:, None], 0), axis=0)
    return first, owner, rank - start_of, counts, starts


def cut_lists(packed, starts, capacity):
    padded = jnp.concatenate([packed, jnp.full((capacity,), packed.shape[0], jnp.int32)])
    return jnp.stack([lax.dynamic_slice(padded, (starts[s],), (capacity,)) for s in range(starts.shape[0])])


def ask_lists(sorted_ids, first, counts, starts, shard_rows, shards, capacity):
    num_ids = sorted_ids.shape[0]
    place = jnp.where(first, jnp.arange(num_ids, dtype=jnp.int32), num_ids)
    packed, places = lax.sort((jnp.where(first, sorted_ids, NO_ID), place), num_keys=1)
    valid = jnp.arange(capacity, dtype=jnp.int32)[None, :] < counts[:, None]
    past = (jnp.arange(shards, dtype=jnp.int32)[:, None] + 1) * shard_rows
    asked = jnp.where(valid, cut_lists(packed, starts, capacity), past)
    after = jnp.concatenate([places[1:], jnp.full((1,), num_ids, jnp.int32)])
    times = jnp.where(valid, cut_lists(after - places, starts, capacity), 0)
    return asked, times.reshape(-1)


def hot_times(ids, hot):
    return jnp.sum((ids[None, :] == jnp.arange(hot, dtype=jnp.int32)[:, None]).astype(jnp.int32), axis=1)


def cell_of(sorted_ids, owner, rank, shards, hot, capacity):
    return jnp.where(sorted_ids < hot, sorted_ids, jnp.minimum(hot + owner * capacity + rank, hot + shards * capacity - 1))


def exchange(rows, shards):
    return lax.all_to_all(rows.reshape(shards, -1, rows.shape[-1]), AXIS_NAME, 0, 0).reshape(rows.shape)


def exchange_ids(ids):
    return lax.all_to_all(ids, AXIS_NAME, 0, 0)


def dot(a, b, dims):
    return lax.dot_general(a, b, (dims, ((), ())), preferred_element_type=jnp.float32)


def after(value, earlier):
    return lax.optimization_barrier((value, earlier))


def when(predicate, update, value):
    return lax.while_loop(lambda state: state[0], lambda state: (jnp.zeros((), jnp.bool_), update(state[1])), (predicate, value))[1]


def plan_unique(sorted_ids, shard_rows, shards, capacity):
    num_ids = sorted_ids.shape[0]
    previous = jnp.concatenate([jnp.full((1,), -1, jnp.int32), sorted_ids[:-1]])
    first = (sorted_ids != previous)
    owner = sorted_ids // shard_rows
    rank = running_count(first) - 1
    owners = jnp.arange(shards, dtype=jnp.int32)
    counts = jnp.sum((first[None, :] & (owner[None, :] == owners[:, None])).astype(jnp.int32), axis=1)
    starts = jnp.sum(jnp.where(owners[None, :] < owners[:, None], counts[None, :], 0), axis=1)
    start_of = jnp.sum(jnp.where(owner[:, None] == owners[None, :], starts[None, :], 0), axis=1)
    packed = lax.sort(jnp.where(first, sorted_ids, jnp.int32(NO_ID)))
    packed = jnp.concatenate([packed, jnp.full((capacity,), NO_ID, jnp.int32)])
    asked = jnp.stack([lax.dynamic_slice(packed, (starts[s],), (capacity,)) for s in range(shards)])
    return owner, rank - start_of, asked


def full_step(shards, in_shard, out_shard, center_ids, context_ids, negative_ids):
    shard_rows = in_shard.shape[0]
    num_pairs, num_negs = center_ids.shape[0], negative_ids.shape[0]
    cap_pairs, cap_negs = unique_capacity(num_pairs, shards), unique_capacity(num_negs, shards)
    me = lax.axis_index(AXIS_NAME)
    take = functools.partial(jnp.take, axis=0, mode='clip')
    neg_sorted = lax.sort(negative_ids)
    cen_sorted, con_moved = lax.sort((center_ids, context_ids), num_keys=1)
    con_sorted, con_pos = lax.sort((con_moved, jnp.arange(num_pairs, dtype=jnp.int32)), num_keys=1)

    def fetch(table, sorted_ids, capacity):
        owner, rank, asked = plan_unique(sorted_ids, shard_rows, shards, capacity)
        local = jnp.clip(exchange_ids(asked) - me * shard_rows, 0, shard_rows - 1).reshape(-1)
        return owner * capacity + rank, local, exchange(take(table, local), shards)

    neg_cell, neg_local, neg_got = fetch(out_shard, neg_sorted, cap_negs)
    cen_cell, cen_local, cen_got = fetch(in_shard, cen_sorted, cap_pairs)
    con_cell, con_local, con_got = fetch(out_shard, con_sorted, cap_pairs)
    con_cell = lax.sort((con_pos, con_cell), num_keys=1)[1]
    negative_half = split_rows([take(neg_got, neg_cell)], jnp.ones((num_negs,), jnp.float32))[0]
    center_vec = take(cen_got, cen_cell)
    center_half = split_rows([center_vec], jnp.ones((num_pairs,), jnp.float32))[0]
    neg_grad = (NEG_WEIGHT / num_negs * jax.nn.sigmoid(dot(center_half, negative_half, ((1,), (1,))))).astype(jnp.bfloat16)
    context_vec = take(con_got, con_cell)
    pos_grad = (jax.nn.sigmoid(jnp.sum(center_vec * context_vec, axis=1)) - 1.0)[:, None]
    d_center = dot(neg_grad, negative_half, ((1,), (0,))) + pos_grad * context_vec
    d_negative = dot(neg_grad, center_half, ((0,), (0,)))

    def give(table, grads, cell, local, capacity):
        sums = jax.ops.segment_sum(grads, cell, num_segments=shards * capacity)
        return table.at[local].add(-LEARN_RATE * exchange(sums, shards))

    new_out = give(out_shard, d_negative, neg_cell, neg_local, cap_negs)
    new_out = give(new_out, pos_grad * center_vec, con_cell, con_local, cap_pairs)
    return give(in_shard, d_center, cen_cell, cen_local, cap_pairs), new_out


def tight_step(shards, in_shard, out_shard, center_ids, context_ids, negative_ids):
    shard_rows = in_shard.shape[0]
    num_pairs, num_negs = center_ids.shape[0], negative_ids.shape[0]
    hot = HOT_ROWS
    cap_pairs, cap_negs = tight_capacity(num_pairs, shards), tight_capacity(num_negs, shards)
    me = lax.axis_index(AXIS_NAME)

    hot_both = jnp.concatenate([in_shard[:hot], out_shard[:hot]])
    hot_both = lax.psum(jnp.where(me == 0, hot_both, 0.0), AXIS_NAME)
    hot_in, hot_out = hot_both[:hot], hot_both[hot:]

    neg_sorted = lax.sort(negative_ids)
    neg_first, _, _, neg_counts, neg_starts = mark_unique(neg_sorted, shard_rows, shards, hot)
    neg_asked, neg_times = ask_lists(neg_sorted, neg_first, neg_counts, neg_starts, shard_rows, shards, cap_negs)
    neg_local = exchange_ids(neg_asked) - me * shard_rows
    neg_send = gather_rows(out_shard, jnp.minimum(neg_local, shard_rows - 1).reshape(-1), shards)
    neg_got = exchange(neg_send, shards)

    cen_sorted, con_moved = lax.sort((center_ids, context_ids), num_keys=1)
    cen_first, cen_owner, cen_rank, cen_counts, cen_starts = mark_unique(cen_sorted, shard_rows, shards, hot)
    cen_asked, cen_times = ask_lists(cen_sorted, cen_first, cen_counts, cen_starts, shard_rows, shards, cap_pairs)
    cen_cell = cell_of(cen_sorted, cen_owner, cen_rank, shards, hot, cap_pairs)
    con_sorted, cen_by_con = lax.sort((con_moved, cen_cell), num_keys=1)
    con_first, con_owner, con_rank, con_counts, con_starts = mark_unique(con_sorted, shard_rows, shards, hot)
    con_asked, _ = ask_lists(con_sorted, con_first, con_counts, con_starts, shard_rows, shards, cap_pairs)
    con_cell = cell_of(con_sorted, con_owner, con_rank, shards, hot, cap_pairs)
    fits = (jnp.max(neg_counts) <= cap_negs) & (jnp.max(cen_counts) <= cap_pairs) & (jnp.max(con_counts) <= cap_pairs)
    spill = jnp.broadcast_to(1 - fits.astype(jnp.int32), (shards, 1))
    asked = exchange_ids(jnp.concatenate([cen_asked, con_asked, spill], axis=1))
    all_fit = jnp.sum(asked[:, -1]) == 0
    cen_local = asked[:, :cap_pairs] - me * shard_rows
    con_local = asked[:, cap_pairs:2 * cap_pairs] - me * shard_rows
    cen_order, con_by_cen = lax.sort((cen_by_con, con_cell), num_keys=1)

    cen_send = gather_rows(in_shard, jnp.minimum(cen_local, shard_rows - 1).reshape(-1), shards)
    cen_send, neg_got = after(cen_send, neg_got)
    cen_got = exchange(cen_send, shards)
    con_send = gather_rows(out_shard, jnp.minimum(con_local, shard_rows - 1).reshape(-1), shards)
    con_send, cen_got = after(con_send, cen_got)
    con_got = exchange(con_send, shards)

    neg_times = jnp.concatenate([hot_times(negative_ids, hot), neg_times])
    hot_cen_times = hot_times(center_ids, hot)
    w_half, w_high, w_low = split_rows([hot_out, neg_got], neg_times)
    uh_half, uh_high, uh_low = split_rows([hot_in], hot_cen_times)
    uc_half, uc_high, uc_low = split_rows([cen_got], cen_times)

    def neg_grads(u_half):
        return (NEG_WEIGHT / num_negs * jax.nn.sigmoid(dot(u_half, w_half, ((1,), (1,))))).astype(jnp.bfloat16)

    grad_h, grad_c = neg_grads(uh_half), neg_grads(uc_half)
    rows_in, cols_in = ((0,), (0,)), ((1,), (0,))

    def rest(times, half, high, low):
        return (times.astype(jnp.float32)[:, None] * half.astype(jnp.float32) - high.astype(jnp.float32) - low.astype(jnp.float32)).astype(jnp.bfloat16)

    d_neg = dot(grad_h, uh_high, rows_in) + dot(grad_h, uh_low, rows_in) + dot(grad_c, uc_high, rows_in)
    more = (jnp.max(cen_times) > 2) | (jnp.max(hot_cen_times) > 256)
    d_neg = when(more, lambda d: d + dot(grad_c, uc_low, rows_in) + dot(grad_h, rest(hot_cen_times, uh_half, uh_high, uh_low), rows_in) + dot(grad_c, rest(cen_times, uc_half, uc_high, uc_low), rows_in), d_neg)
    d_neg = jnp.where(neg_times[:, None] > 0, neg_times.astype(jnp.float32)[:, None] * d_neg, 0.0)
    neg_part, neg_hot = d_neg[hot:], d_neg[:hot]

    con_hot, con_part = pair_sums(hot_in, cen_got, hot_out, con_got, cen_by_con, con_cell)
    cen_hot, cen_part = pair_sums(hot_out, con_got, hot_in, cen_got, con_by_cen, cen_order)

    def center_grads(grad, times, pair_part):
        d = dot(grad, w_high, cols_in) + dot(grad[:, :hot], w_low[:hot], cols_in)
        more = (jnp.max(neg_times[hot:]) > 2) | (jnp.max(neg_times) > 256)
        d = when(more, lambda d: d + dot(grad[:, hot:], w_low[hot:], cols_in) + dot(grad, rest(neg_times, w_half, w_high, w_low), cols_in), d)
        return jnp.where(times[:, None] > 0, times.astype(jnp.float32)[:, None] * d + pair_part, 0.0)

    cen_hot = center_grads(grad_h, hot_cen_times, cen_hot)
    cen_part = center_grads(grad_c, cen_times, cen_part)

    neg_part, con_got = after(neg_part, con_got)
    neg_back = exchange(neg_part, shards)
    con_part, neg_back = after(con_part, neg_back)
    con_back = exchange(con_part, shards)
    cen_part, con_back = after(cen_part, con_back)
    cen_back = exchange(cen_part, shards)
    out_hot = jnp.where(me == 0, lax.psum(con_hot + neg_hot, AXIS_NAME), 0.0)
    in_hot = jnp.where(me == 0, lax.psum(cen_hot, AXIS_NAME), 0.0)
    new_out = subtract_rows(out_shard, out_hot, [(neg_local, neg_back), (con_local, con_back)])
    new_in = subtract_rows(in_shard, in_hot, [(cen_local, cen_back)])
    return new_in, new_out, all_fit


def solution(mesh):
    shards = mesh.shape[AXIS_NAME]

    def device_step(*args):
        new_in, new_out, all_fit = tight_step(shards, *args)
        return when(~all_fit, lambda _: full_step(shards, *args), (new_in, new_out))

    return jax.shard_map(device_step, mesh=mesh, in_specs=(P(AXIS_NAME, None), P(AXIS_NAME, None), P(AXIS_NAME), P(AXIS_NAME), P(AXIS_NAME)), out_specs=(P(AXIS_NAME, None), P(AXIS_NAME, None)), check_vma=False)
```

time: 6870 us -> 1400 us (0.20)
  waiting for transfers between devices: 3840 us -> 653 us
  local copies, waits for them, and re-layouts: 1650 us -> 26.5 us
  other arithmetic: 1090 us -> 108 us
  Pallas kernels: 0 us -> 345 us
    all_to_all x6 -> x8, waiting for transfers between devices: 3840 us -> 293 us  [the longest x6 289 us: exchange(): lax.all_to_all(rows.reshape(shards, -1, rows.shape[-1]), AXIS_NAME, 0, 0)]
    gather x12 -> x0, local copies, waits for them, and re-layouts: 1490 us -> none  [the longest x2 392 us: send_layout(): jnp.take(id_list, slot_of_cell, axis=0, mode='fill', fill_value=-1)]
    scatter-add x4 -> x0, other arithmetic: 634 us -> none  [the longest x2 492 us: send_grads(): jax.ops.segment_sum(arrived.reshape(shards * capacity, -1), local_rows, n...]
    psum x0 -> x2, waiting for transfers between devices: none -> 360 us  [the longest x1 202 us: tight_step(): in_hot = jnp.where(me == 0, lax.psum(cen_hot, AXIS_NAME), 0.0)]
    pallas_call x0 -> x10, Pallas kernels: none -> 345 us  [the longest x2 188 us: pair_sums(): pl.pallas_call(body, grid_spec=pltpu.PrefetchScalarGridSpec(num_scalar_pr...]
    select_n x17 -> x12, other arithmetic: 327 us -> 35.4 us  [the longest x2 20 us: center_grads(): jnp.where(times[:, None] > 0, times.astype(jnp.float32)[:, None] * d + pa...]
    scatter x4 -> x0, local copies, waits for them, and re-layouts: 153 us -> none  [the longest x2 76.6 us: send_layout(): cell_of_id = jnp.zeros_like(id_list).at[sort_order].set(cell_sorted)]
    dot_general x3 -> x13, matrix products: 205 us -> 154 us  [the longest x9 153 us: dot(): lax.dot_general(a, b, (dims, ((), ())), preferred_element_type=jnp.float32)]
  transfers between devices with their start and end apart: 6 -> 10, of which waited for: 4 -> 6; matrix products, arithmetic and copies ran while one was open for 25% -> 11% of each run, Pallas kernels for 0% -> 21%
where the time goes in v2:
time: 1400 us; the launch traced here: 1390 us
  waiting for transfers between devices  653 us (47%)
  Pallas kernels  345 us (25%)
  matrix products  154 us (11%)
  other arithmetic  108 us (8%)
  between operations  66.2 us (5%)
  starting transfers between devices  31.8 us (2%)
  local copies, waits for them, and re-layouts  26.5 us (2%)
    all_to_all x6, waiting for transfers between devices, exchange(): lax.all_to_all(rows.reshape(shards, -1, rows.shape[-1]), AXIS_NAME, 0, 0)  289 us
    psum x1, waiting for transfers between devices, tight_step(): in_hot = jnp.where(me == 0, lax.psum(cen_hot, AXIS_NAME), 0.0)  202 us
    pallas_call x2, Pallas kernels, pair_sums(): pl.pallas_call(body, grid_spec=pltpu.PrefetchScalarGridSpec(num_scalar_pr...  188 us
    psum x1, waiting for transfers between devices, tight_step(): hot_both = lax.psum(jnp.where(me == 0, hot_both, 0.0), AXIS_NAME)  158 us
    dot_general x9, matrix products, dot(): lax.dot_general(a, b, (dims, ((), ())), preferred_element_type=jnp.float32)  153 us
    pallas_call x2, Pallas kernels, subtract_rows(): pl.pallas_call(body, grid_spec=pltpu.PrefetchScalarGridSpec(num_scalar_pr...  65.9 us
    pallas_call x3, Pallas kernels, gather_rows(): pl.pallas_call(body, grid_spec=pltpu.PrefetchScalarGridSpec(num_scalar_pr...  49.9 us
    pallas_call x3, Pallas kernels, split_rows(): pl.pallas_call(body, grid=(sum(blocks),), in_specs=[pl.BlockSpec((block,...  41.6 us
  transfers between devices with their start and end apart: 10, of which 6 were waited for; matrix products, arithmetic and copies ran while one was open for 11% of the time, Pallas kernels for 21%

profile of v2, /device:TPU:0, one launch (start us, length us, event | category | flops | bytes accessed | tf_op | source)
XLA Modules:
  0.0 1387.1 jit_solution(6556429455789559769)
XLA Ops:
  7.2 6.5 sort.264
  24.7 7.7 sort.260
  33.5 6.9 sort.262
  69.1 5.9 sort.265
  80.3 6.8 sort.263
  92.2 6.9 sort.261
  114.2 13.8 gather_rows.4
  133.5 17.9 %gather_rows.3 = f32[30720,128]{1,0:T(8,128)} custom-call(s32[5120]{0:T(1024)} %fusion.100.line, f32[37728,128]{1,0:T(8,128)} %bitcast.301), custom_call_target="tpu_custom_call" | custom-call | bytes 66502656 | tf_op jit(solution)/shard_map/gather_rows/pallas_call | solution.py:61
  151.4 68.6 %all-to-all-done.11 = f32[8,320,768]{2,1,0:T(8,128)} async-done(((f32[8,320,768]{2,1,0:T(8,128)}), f32[8,320,768]{2,1,0:T(8,128)}, u32[]{:S(2)}, u32[]{:S(2)}) %all-to-all-start.11) | async-done | bytes 7864352 | tf_op jit(solution)/shard_map/all_to_all | solution.py:285
  249.3 6.9 sort.266
  260.5 18.3 %gather_rows.5 = f32[30720,128]{1,0:T(8,128)} custom-call(s32[5120]{0:T(1024)} %fusion.102.line, f32[37728,128]{1,0:T(8,128)} %bitcast.298), custom_call_target="tpu_custom_call" | custom-call | bytes 66502656 | tf_op jit(solution)/shard_map/gather_rows/pallas_call | solution.py:61
  278.8 158.4 %all-reduce.12.cloned.1.call-done = f32[1536,768]{1,0:T(8,128)} async-done(((f32[1536,768]{1,0:T(8,128)}), f32[1536,768]{1,0:T(8,128)}) %all-reduce.12.cloned.1.call-update) | async-done | bytes 4718608 | tf_op jit(solution)/shard_map/psum | solution.py:365
  437.2 4.9 fusion.157
  444.9 16.7 %split_rows.8 = (bf16[3328,768]{1,0:T(8,128)(2,1)}, bf16[3328,768]{1,0:T(8,128)(2,1)}, bf16[3328,768]{1,0:T(8,128)(2,1)}) custom-call(f32[768,768]{1,0:T(8,128)} %get-tuple-element.428.refs_0_, f32[2560,768]{1,0:T(8,128)} %bitcast.96.refs_1_, f32[3328,1]{1,0:T(8,128)} %copy.38.refs_2_), custom_call_target="tpu_custom_call" | custom-call | bytes 25559040 | tf_op jit(solution)/shard_map/split_rows/pallas_call | solution.py:228
  461.5 7.1 multiply_convert_fusion.2
  476.7 6.7 fusion.165
  483.4 6.8 fusion.166
  490.2 22.1 %split_rows.9 = (bf16[5120,768]{1,0:T(8,128)(2,1)}, bf16[5120,768]{1,0:T(8,128)(2,1)}, bf16[5120,768]{1,0:T(8,128)(2,1)}) custom-call(f32[5120,768]{1,0:T(8,128)} %bitcast.109.refs_0_, f32[5120,1]{1,0:T(8,128)} %bitcast.324), custom_call_target="tpu_custom_call" | custom-call | bytes 39321600 | tf_op jit(solution)/shard_map/split_rows/pallas_call | solution.py:228
  512.3 39.0 %multiply_convert_fusion.1 = bf16[5120,3328]{1,0:T(8,128)(2,1)} fusion(bf16[5120,768]{1,0:T(8,128)(2,1)} %get-tuple-element.576, bf16[3328,768]{1,0:T(8,128)(2,1)} %get-tuple-element.607), kind=kOutput, calls=%fused_computation.154 | convolution fusion | flops 26257653760 | bytes 47054848 | tf_op jit(solution)/shard_map/dot_general | solution.py:293
  551.3 39.6 %add_add_fusion = f32[3328,768]{1,0:T(8,128)} fusion(f32[3328,768]{1,0:T(8,128)} %fusion.165, f32[3328,768]{1,0:T(8,128)} %fusion.166, bf16[5120,3328]{1,0:T(8,128)(2,1)} %multiply_convert_fusion.1, bf16[5120,768]{1,0:T(8,128)(2,1)} %get-tuple-element.577), kind=kOutput, calls=%fused_computation.161 | convolution fusion | flops 26177568768 | bytes 72613888 | tf_op jit(solution)/shard_map/dot_general | solution.py:293
  590.8 4.5 all-to-all-start.13
  596.1 5.5 multiply_select_fusion
  608.9 159.1 %all-to-all-done.13 = f32[8,640,768]{2,1,0:T(8,128)} async-done(((f32[8,640,768]{2,1,0:T(8,128)}), f32[8,640,768]{2,1,0:T(8,128)}, u32[]{:S(2)}, u32[]{:S(2)}) %all-to-all-start.13) | async-done | bytes 15728672 | tf_op jit(solution)/shard_map/all_to_all | solution.py:285
  771.8 12.3 fusion.51
  784.2 33.7 %convolution_add_fusion = f32[5120,768]{1,0:T(8,128)} fusion(f32[5120,768]{1,0:T(8,128)} %fusion.51, bf16[5120,3328]{1,0:T(8,128)(2,1)} %get-tuple-element.714, bf16[3328,768]{1,0:T(8,128)(2,1)S(1)} %bitcast.345), kind=kOutput, calls=%fused_computation.163 | convolution fusion | flops 26176389120 | bytes 70647808 | tf_op jit(solution)/shard_map/dot_general | solution.py:293
  817.9 93.6 %pair_sums.3 = (f32[4608,128]{1,0:T(8,128)}, f32[30720,128]{1,0:T(8,128)}) custom-call(s32[8192]{0:T(1024)} %fusion.68.x_line, s32[8192]{0:T(1024)} %get-tuple-element.359.y_line, f32[4608,128]{1,0:T(8,128)} %bitcast.316, f32[30720,128]{1,0:T(8,128)} %bitcast.119.yg.xg, f32[4608,128]{1,0:T(8,128)} %bitcast.318, f32[30720,128]{1,0:T(8,128)} %bitcast.113.xg.yg), custom_call_target="tpu_custom_call" | custom-call | bytes 201326592 | tf_op jit(solution)/shard_map/pair_sums/pallas_call | solution.py:127
  916.2 94.2 %pair_sums.2 = (f32[4608,128]{1,0:T(8,128)}, f32[30720,128]{1,0:T(8,128)}) custom-call(s32[8192]{0:T(1024)} %get-tuple-element.509.x_line, s32[8192]{0:T(1024)} %get-tuple-element.510.y_line, f32[4608,128]{1,0:T(8,128)} %bitcast.319, f32[30720,128]{1,0:T(8,128)} %bitcast.113.xg.yg, f32[4608,128]{1,0:T(8,128)} %bitcast.317, f32[30720,128]{1,0:T(8,128)} %bitcast.119.yg.xg), custom_call_target="tpu_custom_call" | custom-call | bytes 201326592 | tf_op jit(solution)/shard_map/pair_sums/pallas_call | solution.py:127
  1010.4 16.6 %add_select_fusion.3 = f32[5120,768]{1,0:T(8,128)} fusion(f32[5120,768]{1,0:T(8,128)} %bitcast.323, f32[5120,768]{1,0:T(8,128)} %get-tuple-element.262, f32[5120]{0:T(1024)S(1)} %copy-done.48, pred[5120]{0:T(1024)(128)(4,1)S(1)} %copy-done.54), kind=kLoop, calls=%fused_computation.157 | loop fusion | flops 11796480 | bytes 47211520 | tf_op jit(solution)/shard_map/jit(_where)/select_n | solution.py:426
  1027.0 61.7 %all-to-all-done.15 = f32[8,640,768]{2,1,0:T(8,128)} async-done(((f32[8,640,768]{2,1,0:T(8,128)}), f32[8,640,768]{2,1,0:T(8,128)}, u32[]{:S(2)}, u32[]{:S(2)}) %all-to-all-start.15) | async-done | bytes 15728672 | tf_op jit(solution)/shard_map/all_to_all | solution.py:285
  1104.2 201.8 %all-reduce.14.cloned.1.call-done = (f32[768,768]{1,0:T(8,128)}, f32[768,768]{1,0:T(8,128)}) async-done(((f32[768,768]{1,0:T(8,128)}, f32[768,768]{1,0:T(8,128)}), (f32[768,768]{1,0:T(8,128)}, f32[768,768]{1,0:T(8,128)})) %all-reduce.14.cloned.1.call-update) | async-done | bytes 4718608 | tf_op jit(solution)/shard_map/psum | solution.py:438
  1312.5 36.2 %subtract_rows.3 = f32[37728,128]{1,0:T(8,128)} custom-call(s32[2560]{0:T(1024)} %get-tuple-element.479.refs_0_, s32[5120]{0:T(1024)} %fusion.104.refs_1_, f32[37728,128]{1,0:T(8,128)} %bitcast.299, f32[4608,128]{1,0:T(8,128)} %bitcast.330, f32[15360,128]{1,0:T(8,128)} %bitcast.159.refs_4_, f32[30720,128]{1,0:T(8,128)} %bitcast.162.refs_5_), custom_call_target="tpu_custom_call" | custom-call | bytes 109412352 | tf_op jit(solution)/shard_map/subtract_rows/pallas_call | solution.py:190
  1348.7 29.8 %subtract_rows.2 = f32[37728,128]{1,0:T(8,128)} custom-call(s32[5120]{0:T(1024)} %fusion.98.refs_0_, f32[37728,128]{1,0:T(8,128)} %bitcast.302, f32[4608,128]{1,0:T(8,128)} %bitcast.329, f32[30720,128]{1,0:T(8,128)} %bitcast.147.refs_3_), custom_call_target="tpu_custom_call" | custom-call | bytes 85819392 | tf_op jit(solution)/shard_map/subtract_rows/pallas_call | solution.py:190
  (218 shorter events, 104.7 us)
Async XLA Ops:
  102.5 8.8 all-to-all-start.10
  111.5 16.5 %all-to-all-start.9 = ((s32[8,1,1281]{2,1,0:T(1,128)}), s32[8,1,1281]{2,1,0:T(1,128)S(1)}, u32[]{:S(2)}, u32[]{:S(2)}) async-start(s32[8,1,1281]{2,1,0:T(1,128)} %all_to_all.66), calls=%async_computation.9 | async-start | bytes 90112 | tf_op jit(solution)/shard_map/all_to_all | solution.py:289
  127.9 92.0 %all-to-all-start.11 = ((f32[8,320,768]{2,1,0:T(8,128)}), f32[8,320,768]{2,1,0:T(8,128)}, u32[]{:S(2)}, u32[]{:S(2)}) async-start(f32[8,320,768]{2,1,0:T(8,128)} %bitcast.320), calls=%async_computation.11 | async-start | bytes 15728640 | tf_op jit(solution)/shard_map/all_to_all | solution.py:285
  219.9 270.2 %all-to-all-start.12 = ((f32[8,640,768]{2,1,0:T(8,128)}), f32[8,640,768]{2,1,0:T(8,128)}, u32[]{:S(2)}, u32[]{:S(2)}) async-start(f32[8,640,768]{2,1,0:T(8,128)} %bitcast.313), calls=%async_computation.12 | async-start | bytes 31457280 | tf_op jit(solution)/shard_map/all_to_all | solution.py:285
  224.3 212.9 %all-reduce.12.cloned.1.call-start = ((), (), s32[]{:S(2)}) async-start(), calls=%async_computation.17 | async-start | bytes 9437184 | tf_op jit(solution)/shard_map/psum | solution.py:365
  228.2 13.1 copy-start.28
  230.7 48.1 %copy-start.26 = (s32[5120]{0:T(1024)}, s32[5120]{0:T(1024)S(1)}, u32[]{:S(2)}) copy-start(s32[5120]{0:T(1024)S(1)} %select_n.520) | copy-start | bytes 61444
  244.5 34.3 %copy-start.45 = (s32[768]{0:T(1024)}, s32[768]{0:T(1024)S(1)}, u32[]{:S(2)}) copy-start(s32[768]{0:T(1024)S(1)} %convert_reduce_fusion.3) | copy-start | bytes 9220
  245.1 33.7 %copy-start.52 = (f32[768]{0:T(1024)}, f32[768]{0:T(1024)S(1)}, u32[]{:S(2)}) copy-start(f32[768]{0:T(1024)S(1)} %get-tuple-element.482) | copy-start | bytes 9220
  444.8 23.8 %copy-start.59 = (bf16[768,768]{1,0:T(8,128)(2,1)}, bf16[768,768]{1,0:T(8,128)(2,1)S(1)}, u32[]{:S(2)}) copy-start(bf16[768,768]{1,0:T(8,128)(2,1)S(1)} %get-tuple-element.571) | copy-start | bytes 3538948
  444.8 31.8 %copy-start.61 = (bf16[768,768]{1,0:T(8,128)(2,1)}, bf16[768,768]{1,0:T(8,128)(2,1)S(1)}, u32[]{:S(2)}) copy-start(bf16[768,768]{1,0:T(8,128)(2,1)S(1)} %get-tuple-element.572) | copy-start | bytes 3538948
  444.9 38.5 %copy-start.63 = (bf16[768,768]{1,0:T(8,128)(2,1)}, bf16[768,768]{1,0:T(8,128)(2,1)S(1)}, u32[]{:S(2)}) copy-start(bf16[768,768]{1,0:T(8,128)(2,1)S(1)} %get-tuple-element.573) | copy-start | bytes 3538948
  461.5 7.2 copy-start.58
  468.7 14.7 %copy-start.43 = (bf16[768,3328]{1,0:T(8,128)(2,1)}, bf16[768,3328]{1,0:T(8,128)(2,1)S(1)}, u32[]{:S(2)}) copy-start(bf16[768,3328]{1,0:T(8,128)(2,1)S(1)} %multiply_convert_fusion.2) | copy-start | bytes 15335428
  590.8 4.5 copy-start.27
  590.8 4.5 copy-start.46
  590.8 4.5 copy-start.60
  590.8 4.5 copy-start.62
  590.8 177.2 %all-to-all-start.13 = ((f32[8,640,768]{2,1,0:T(8,128)}), f32[8,640,768]{2,1,0:T(8,128)}, u32[]{:S(2)}, u32[]{:S(2)}) async-start(f32[8,640,768]{2,1,0:T(8,128)} %bitcast.314), calls=%async_computation.13 | async-start | bytes 31457280 | tf_op jit(solution)/shard_map/all_to_all | solution.py:285
  768.0 16.1 %slice-start = ((s8[5111808]{0:T(1024)(128)(4,1)}), s8[917504]{0:T(1024)(128)(4,1)S(1)}, s32[]{:S(2)}) async-start(s8[5111808]{0:T(1024)(128)(4,1)} %bitcast.344), calls=%async_computation.19 | async-start | bytes 1835008
  768.0 143.5 %all-to-all-start.14 = ((f32[8,320,768]{2,1,0:T(8,128)}), f32[8,320,768]{2,1,0:T(8,128)}, u32[]{:S(2)}, u32[]{:S(2)}) async-start(f32[8,320,768]{2,1,0:T(8,128)} %bitcast.321), calls=%async_computation.14 | async-start | bytes 15728640 | tf_op jit(solution)/shard_map/all_to_all | solution.py:285
  771.8 12.4 slice-start.1
  911.5 177.1 %all-to-all-start.15 = ((f32[8,640,768]{2,1,0:T(8,128)}), f32[8,640,768]{2,1,0:T(8,128)}, u32[]{:S(2)}, u32[]{:S(2)}) async-start(f32[8,640,768]{2,1,0:T(8,128)} %bitcast.322), calls=%async_computation.15 | async-start | bytes 31457280 | tf_op jit(solution)/shard_map/all_to_all | solution.py:285
  916.2 94.2 %copy-start.48 = (f32[5120]{0:T(1024)S(1)}, f32[5120]{0:T(1024)}, u32[]{:S(2)}) copy-start(f32[5120]{0:T(1024)} %convert_element_type.205) | copy-start | bytes 61444
  916.2 94.2 %copy-start.54 = (pred[5120]{0:T(1024)(128)(4,1)S(1)}, pred[5120]{0:T(1024)(128)(4,1)}, u32[]{:S(2)}) copy-start(pred[5120]{0:T(1024)(128)(4,1)} %broadcast_compare_fusion) | copy-start | bytes 15364
  1088.6 4.6 copy-start.5
  1088.6 260.1 %all-to-all-start.16 = ((f32[8,640,768]{2,1,0:T(8,128)}), f32[8,640,768]{2,1,0:T(8,128)}, u32[]{:S(2)}, u32[]{:S(2)}) async-start(f32[8,640,768]{2,1,0:T(8,128)} %bitcast.315), calls=%async_computation.16 | async-start | bytes 31457280 | tf_op jit(solution)/shard_map/all_to_all | solution.py:285
  1093.1 212.9 %all-reduce.14.cloned.1.call-start = ((), (), s32[]{:S(2)}) async-start(), calls=%async_computation.18 | async-start | bytes 9437184 | tf_op jit(solution)/shard_map/psum | solution.py:438
  1093.5 7.5 copy-start.50
  1093.5 7.5 copy-start.49
  1348.7 29.8 %copy-start.29 = (s32[8192]{0:T(1024)S(1)}, s32[8192]{0:T(1024)}, u32[]{:S(2)}) copy-start(s32[8192]{0:T(1024)} %param.15) | copy-start | bytes 98308
  1348.7 29.8 %copy-start.31 = (s32[8192]{0:T(1024)S(1)}, s32[8192]{0:T(1024)}, u32[]{:S(2)}) copy-start(s32[8192]{0:T(1024)} %param.16) | copy-start | bytes 98308
  (7 other events, 18.9 us)
Sparse Core Ops, SparseCore 0:
  230.8 206.3 all-reduce.11
  1101.1 204.8 all-reduce.13

commit v3 on v2

--- a/solution.py
+++ b/solution.py
@@ -7,12 +7,14 @@
 from jax.experimental.pallas import tpu as pltpu
 from jax.sharding import PartitionSpec as P
 
+
 LEARN_RATE = 1.0
 NEG_WEIGHT = 5.0
 AXIS_NAME = 'vp'
 HOT_ROWS = 768
 LANES = 128
 SUBLANES = 8
+PAIR_TILES = 4
 NO_ID = 2**30
 VMEM_BYTES = 60 * 2**20
 ANY = pl.BlockSpec(memory_space=pl.ANY)
@@ -79,7 +81,7 @@
     xh_lines, xg_lines, yh_lines, yg_lines = [v.shape[0] for v in views]
     x_lines, y_lines = xh_lines + xg_lines, yh_lines + yg_lines
 
-    def body(x_line, y_line, xh, xg, yh, yg, oh, og, x_all, y_all, total, sem):
+    def body(x_line, y_line, xh, xg, yh, yg, oh, og, x_all, y_all, total, prod, sem):
         copies = [
             pltpu.make_async_copy(xh, x_all.at[pl.ds(0, xh_lines)], sem.at[0]),
             pltpu.make_async_copy(xg, x_all.at[pl.ds(xh_lines, xg_lines)], sem.at[1]),
@@ -99,24 +101,30 @@
 
         def step(t, carry):
             run, last = carry
-            kept, parts, lines = [], [], []
-            for j in range(SUBLANES):
-                line = y_line[t * SUBLANES + j]
-                x = x_all[pl.ds(x_line[t * SUBLANES + j], chunks, stride=SUBLANES), :]
+            kept, lines, grads = [], [], []
+            for i in range(PAIR_TILES * SUBLANES):
+                tile, j = i // SUBLANES, i % SUBLANES
+                line = y_line[t * PAIR_TILES * SUBLANES + i]
+                x = x_all[pl.ds(x_line[t * PAIR_TILES * SUBLANES + i], chunks, stride=SUBLANES), :]
                 y = y_all[pl.ds(line, chunks, stride=SUBLANES), :]
+                prod[pl.ds(tile * SUBLANES * chunks + j, chunks, stride=SUBLANES), :] = x * y
                 kept.append(x)
                 lines.append(line)
-                parts.append(jnp.sum(x * y, axis=0, keepdims=True))
-            score = jnp.sum(jnp.concatenate(parts, axis=0), axis=1, keepdims=True)
-            grad = jax.nn.sigmoid(score) - 1.0
-            for j in range(SUBLANES):
-                same = (lines[j] == last).astype(jnp.float32)
-                run = run * same + grad[j:j + 1, :] * kept[j]
-                total[pl.ds(lines[j], chunks, stride=SUBLANES), :] = run
-                last = lines[j]
+            for tile in range(PAIR_TILES):
+                part = prod[pl.ds(tile * SUBLANES * chunks, SUBLANES), :]
+                for k in range(1, chunks):
+                    part = part + prod[pl.ds((tile * chunks + k) * SUBLANES, SUBLANES), :]
+                score = jnp.broadcast_to(jnp.sum(part, axis=1, keepdims=True), (SUBLANES, LANES))
+                grads.append(jax.nn.sigmoid(score) - 1.0)
+            for i in range(PAIR_TILES * SUBLANES):
+                tile, j = i // SUBLANES, i % SUBLANES
+                same = (lines[i] == last).astype(jnp.float32)
+                run = run * same + jnp.broadcast_to(grads[tile][j:j + 1, :], (chunks, LANES)) * kept[i]
+                total[pl.ds(lines[i], chunks, stride=SUBLANES), :] = run
+                last = lines[i]
             return run, last
 
-        lax.fori_loop(0, pairs // SUBLANES, step, (jnp.zeros((chunks, LANES), jnp.float32), jnp.int32(-1)), unroll=2)
+        lax.fori_loop(0, pairs // (PAIR_TILES * SUBLANES), step, (jnp.zeros((chunks, LANES), jnp.float32), jnp.int32(-1)))
         out_hot = pltpu.make_async_copy(total.at[pl.ds(0, yh_lines)], oh, sem.at[0])
         out_got = pltpu.make_async_copy(total.at[pl.ds(yh_lines, yg_lines)], og, sem.at[1])
         out_hot.start()
@@ -129,7 +137,8 @@
         grid_spec=pltpu.PrefetchScalarGridSpec(
             num_scalar_prefetch=2, grid=(1,), in_specs=[ANY] * 4, out_specs=[ANY] * 2,
             scratch_shapes=[pltpu.VMEM((x_lines, LANES), jnp.float32), pltpu.VMEM((y_lines, LANES), jnp.float32),
-                            pltpu.VMEM((y_lines, LANES), jnp.float32), pltpu.SemaphoreType.DMA((4,))]),
+                            pltpu.VMEM((y_lines, LANES), jnp.float32), pltpu.VMEM((PAIR_TILES * SUBLANES * chunks, LANES), jnp.float32),
+                            pltpu.SemaphoreType.DMA((4,))]),
         out_shape=[jax.ShapeDtypeStruct((yh_lines, LANES), jnp.float32), jax.ShapeDtypeStruct((yg_lines, LANES), jnp.float32)],
         cost_estimate=pl.CostEstimate(flops=0, bytes_accessed=8 * 4 * d * pairs, transcendentals=0),
         compiler_params=pltpu.CompilerParams(vmem_limit_bytes=VMEM_BYTES),
@@ -253,24 +262,29 @@
     counts = jnp.sum((first[None, :] & (owner[None, :] == owners[:, None])).astype(jnp.int32), axis=1)
     starts = jnp.sum(jnp.where(owners[None, :] < owners[:, None], counts[None, :], 0), axis=1)
     start_of = jnp.sum(jnp.where(owner[None, :] == owners[:, None], starts[:, None], 0), axis=0)
-    return first, owner, rank - start_of, counts, starts
-
-
-def cut_lists(packed, starts, capacity):
-    padded = jnp.concatenate([packed, jnp.full((capacity,), packed.shape[0], jnp.int32)])
-    return jnp.stack([lax.dynamic_slice(padded, (starts[s],), (capacity,)) for s in range(starts.shape[0])])
-
-
-def ask_lists(sorted_ids, first, counts, starts, shard_rows, shards, capacity):
+    return first, owner, rank - start_of, counts
+
+
+def ask_lists(sorted_ids, first, owner, rank, counts, shard_rows, shards, capacity):
     num_ids = sorted_ids.shape[0]
-    place = jnp.where(first, jnp.arange(num_ids, dtype=jnp.int32), num_ids)
-    packed, places = lax.sort((jnp.where(first, sorted_ids, NO_ID), place), num_keys=1)
-    valid = jnp.arange(capacity, dtype=jnp.int32)[None, :] < counts[:, None]
-    past = (jnp.arange(shards, dtype=jnp.int32)[:, None] + 1) * shard_rows
-    asked = jnp.where(valid, cut_lists(packed, starts, capacity), past)
-    after = jnp.concatenate([places[1:], jnp.full((1,), num_ids, jnp.int32)])
-    times = jnp.where(valid, cut_lists(after - places, starts, capacity), 0)
-    return asked, times.reshape(-1)
+    cells = shards * capacity
+    key = jnp.where(first & (rank < capacity), owner * capacity + rank, NO_ID)
+    owners = jnp.arange(shards, dtype=jnp.int32)[:, None]
+    slot = jnp.arange(capacity, dtype=jnp.int32)[None, :]
+    past = (owners + 1) * shard_rows
+    ends = jnp.sum((sorted_ids[None, :] < past).astype(jnp.int32), axis=1, keepdims=True)
+    fill_key = jnp.where(slot >= counts[:, None], owners * capacity + slot, NO_ID)
+
+    def flat(values):
+        return jnp.broadcast_to(values, (shards, capacity)).reshape(-1)
+
+    _, asked, places = lax.sort((
+        jnp.concatenate([key, fill_key.reshape(-1)]),
+        jnp.concatenate([sorted_ids, flat(past)]),
+        jnp.concatenate([jnp.arange(num_ids, dtype=jnp.int32), flat(ends)])), num_keys=1)
+    places = places[:cells]
+    times = jnp.concatenate([places[1:], jnp.full((1,), num_ids, jnp.int32)]) - places
+    return asked[:cells].reshape(shards, capacity), times
 
 
 def hot_times(ids, hot):
@@ -302,7 +316,6 @@
 
 
 def plan_unique(sorted_ids, shard_rows, shards, capacity):
-    num_ids = sorted_ids.shape[0]
     previous = jnp.concatenate([jnp.full((1,), -1, jnp.int32), sorted_ids[:-1]])
     first = (sorted_ids != previous)
     owner = sorted_ids // shard_rows
@@ -366,30 +379,30 @@
     hot_in, hot_out = hot_both[:hot], hot_both[hot:]
 
     neg_sorted = lax.sort(negative_ids)
-    neg_first, _, _, neg_counts, neg_starts = mark_unique(neg_sorted, shard_rows, shards, hot)
-    neg_asked, neg_times = ask_lists(neg_sorted, neg_first, neg_counts, neg_starts, shard_rows, shards, cap_negs)
-    neg_local = exchange_ids(neg_asked) - me * shard_rows
-    neg_send = gather_rows(out_shard, jnp.minimum(neg_local, shard_rows - 1).reshape(-1), shards)
-    neg_got = exchange(neg_send, shards)
+    neg_first, neg_owner, neg_rank, neg_counts = mark_unique(neg_sorted, shard_rows, shards, hot)
+    neg_asked, neg_times = ask_lists(neg_sorted, neg_first, neg_owner, neg_rank, neg_counts, shard_rows, shards, cap_negs)
 
     cen_sorted, con_moved = lax.sort((center_ids, context_ids), num_keys=1)
-    cen_first, cen_owner, cen_rank, cen_counts, cen_starts = mark_unique(cen_sorted, shard_rows, shards, hot)
-    cen_asked, cen_times = ask_lists(cen_sorted, cen_first, cen_counts, cen_starts, shard_rows, shards, cap_pairs)
+    cen_first, cen_owner, cen_rank, cen_counts = mark_unique(cen_sorted, shard_rows, shards, hot)
+    cen_asked, cen_times = ask_lists(cen_sorted, cen_first, cen_owner, cen_rank, cen_counts, shard_rows, shards, cap_pairs)
     cen_cell = cell_of(cen_sorted, cen_owner, cen_rank, shards, hot, cap_pairs)
     con_sorted, cen_by_con = lax.sort((con_moved, cen_cell), num_keys=1)
-    con_first, con_owner, con_rank, con_counts, con_starts = mark_unique(con_sorted, shard_rows, shards, hot)
-    con_asked, _ = ask_lists(con_sorted, con_first, con_counts, con_starts, shard_rows, shards, cap_pairs)
+    con_first, con_owner, con_rank, con_counts = mark_unique(con_sorted, shard_rows, shards, hot)
+    con_asked, _ = ask_lists(con_sorted, con_first, con_owner, con_rank, con_counts, shard_rows, shards, cap_pairs)
     con_cell = cell_of(con_sorted, con_owner, con_rank, shards, hot, cap_pairs)
     fits = (jnp.max(neg_counts) <= cap_negs) & (jnp.max(cen_counts) <= cap_pairs) & (jnp.max(con_counts) <= cap_pairs)
     spill = jnp.broadcast_to(1 - fits.astype(jnp.int32), (shards, 1))
-    asked = exchange_ids(jnp.concatenate([cen_asked, con_asked, spill], axis=1))
+    asked = exchange_ids(jnp.concatenate([cen_asked, con_asked, neg_asked, spill], axis=1))
     all_fit = jnp.sum(asked[:, -1]) == 0
     cen_local = asked[:, :cap_pairs] - me * shard_rows
     con_local = asked[:, cap_pairs:2 * cap_pairs] - me * shard_rows
+    neg_local = asked[:, 2 * cap_pairs:-1] - me * shard_rows
+    neg_send = gather_rows(out_shard, jnp.minimum(neg_local, shard_rows - 1).reshape(-1), shards)
+    neg_got = exchange(neg_send, shards)
     cen_order, con_by_cen = lax.sort((cen_by_con, con_cell), num_keys=1)
 
     cen_send = gather_rows(in_shard, jnp.minimum(cen_local, shard_rows - 1).reshape(-1), shards)
-    cen_send, neg_got = after(cen_send, neg_got)
+    cen_send, neg_got, hot_in, hot_out = lax.optimization_barrier((cen_send, neg_got, hot_in, hot_out))
     cen_got = exchange(cen_send, shards)
     con_send = gather_rows(out_shard, jnp.minimum(con_local, shard_rows - 1).reshape(-1), shards)
     con_send, cen_got = after(con_send, cen_got)
@@ -432,9 +445,10 @@
     neg_back = exchange(neg_part, shards)
     con_part, neg_back = after(con_part, neg_back)
     con_back = exchange(con_part, shards)
-    cen_part, con_back = after(cen_part, con_back)
+    out_hot = lax.psum(con_hot + neg_hot, AXIS_NAME)
+    cen_part, con_back, out_hot = lax.optimization_barrier((cen_part, con_back, out_hot))
     cen_back = exchange(cen_part, shards)
-    out_hot = jnp.where(me == 0, lax.psum(con_hot + neg_hot, AXIS_NAME), 0.0)
+    out_hot = jnp.where(me == 0, out_hot, 0.0)
     in_hot = jnp.where(me == 0, lax.psum(cen_hot, AXIS_NAME), 0.0)
     new_out = subtract_rows(out_shard, out_hot, [(neg_local, neg_back), (con_local, con_back)])
     new_in = subtract_rows(in_shard, in_hot, [(cen_local, cen_back)])

time: 1400 us -> 1380 us (0.986)
  between operations: 66.2 us -> 21 us
  Pallas kernels: 345 us -> 300 us
  waiting for transfers between devices: 653 us -> 697 us
    all_to_all x6, waiting for transfers between devices: 289 us -> 426 us  [exchange(): lax.all_to_all(rows.reshape(shards, -1, rows.shape[-1]), AXIS_NAME, 0, 0)]
    psum x1, waiting for transfers between devices: 158 us -> 71.4 us  [tight_step(): hot_both = lax.psum(jnp.where(me == 0, hot_both, 0.0), AXIS_NAME)]
    pallas_call x2, Pallas kernels: 188 us -> 143 us  [pair_sums(): pl.pallas_call(body, grid_spec=pltpu.PrefetchScalarGridSpec(num_scalar_pr...]
  transfers between devices with their start and end apart: 10 -> 9, of which waited for: 6 -> 7; matrix products, arithmetic and copies ran while one was open for 11% -> 11% of each run, Pallas kernels for 21% -> 10%
where the time goes in v3:
time: 1380 us; the launch traced here: 1370 us
  waiting for transfers between devices  697 us (51%)
  Pallas kernels  300 us (22%)
  matrix products  164 us (12%)
  other arithmetic  114 us (8%)
  local copies, waits for them, and re-layouts  35.5 us (3%)
  starting transfers between devices  29.7 us (2%)
  between operations  21 us (2%)
    all_to_all x6, waiting for transfers between devices, exchange(): lax.all_to_all(rows.reshape(shards, -1, rows.shape[-1]), AXIS_NAME, 0, 0)  426 us
    psum x1, waiting for transfers between devices, tight_step(): in_hot = jnp.where(me == 0, lax.psum(cen_hot, AXIS_NAME), 0.0)  194 us
    dot_general x9, matrix products, dot(): lax.dot_general(a, b, (dims, ((), ())), preferred_element_type=jnp.float32)  163 us
    pallas_call x2, Pallas kernels, pair_sums(): pl.pallas_call(body, grid_spec=pltpu.PrefetchScalarGridSpec(num_scalar_pr...  143 us
    psum x1, waiting for transfers between devices, tight_step(): hot_both = lax.psum(jnp.where(me == 0, hot_both, 0.0), AXIS_NAME)  71.4 us
    pallas_call x2, Pallas kernels, subtract_rows(): pl.pallas_call(body, grid_spec=pltpu.PrefetchScalarGridSpec(num_scalar_pr...  65.9 us
    pallas_call x3, Pallas kernels, gather_rows(): pl.pallas_call(body, grid_spec=pltpu.PrefetchScalarGridSpec(num_scalar_pr...  49.7 us
    pallas_call x3, Pallas kernels, split_rows(): pl.pallas_call(body, grid=(sum(blocks),), in_specs=[pl.BlockSpec((block,...  42.1 us
  transfers between devices with their start and end apart: 9, of which 7 were waited for; matrix products, arithmetic and copies ran while one was open for 11% of the time, Pallas kernels for 10%

profile of v3, /device:TPU:0, one launch (start us, length us, event | category | flops | bytes accessed | tf_op | source)
XLA Modules:
  0.0 1368.9 jit_solution(2619335853330925656)
XLA Ops:
  7.2 7.7 sort.285
  16.0 6.9 sort.287
  24.8 6.5 sort.289
  34.3 8.3 sort.288
  42.7 8.5 sort.286
  53.8 11.2 broadcast_in_dim.228
  65.3 7.6 sort.290
  84.3 14.0 %gather_rows.4 = f32[15360,128]{1,0:T(8,128)} custom-call(s32[2560]{0:T(1024)} %fusion.126.line, f32[37728,128]{1,0:T(8,128)} %bitcast.276), custom_call_target="tpu_custom_call" | custom-call | bytes 42909696 | tf_op jit(solution)/shard_map/gather_rows/pallas_call | solution.py:63
  127.0 6.9 sort.291
  138.3 17.9 %gather_rows.5 = f32[30720,128]{1,0:T(8,128)} custom-call(s32[5120]{0:T(1024)} %fusion.99.line, f32[37728,128]{1,0:T(8,128)} %bitcast.277), custom_call_target="tpu_custom_call" | custom-call | bytes 66502656 | tf_op jit(solution)/shard_map/gather_rows/pallas_call | solution.py:63
  156.8 17.9 %gather_rows.3 = f32[30720,128]{1,0:T(8,128)} custom-call(s32[5120]{0:T(1024)} %fusion.97.line, f32[37728,128]{1,0:T(8,128)} %bitcast.280), custom_call_target="tpu_custom_call" | custom-call | bytes 66502656 | tf_op jit(solution)/shard_map/gather_rows/pallas_call | solution.py:63
  174.7 71.4 %all-reduce.7.cloned.1.call-done = f32[1536,768]{1,0:T(8,128)} async-done(((f32[1536,768]{1,0:T(8,128)}), f32[1536,768]{1,0:T(8,128)}) %all-reduce.7.cloned.1.call-update) | async-done | bytes 4718608 | tf_op jit(solution)/shard_map/psum | solution.py:378
  254.6 16.2 %split_rows.8 = (bf16[3328,768]{1,0:T(8,128)(2,1)}, bf16[3328,768]{1,0:T(8,128)(2,1)}, bf16[3328,768]{1,0:T(8,128)(2,1)}) custom-call(f32[768,768]{1,0:T(8,128)} %get-tuple-element.255.refs_0_, f32[2560,768]{1,0:T(8,128)} %bitcast.78.refs_1_, f32[3328,1]{1,0:T(8,128)} %copy.38.refs_2_), custom_call_target="tpu_custom_call" | custom-call | bytes 25559040 | tf_op jit(solution)/shard_map/split_rows/pallas_call | solution.py:237
  275.4 8.4 multiply_convert_fusion.2
  283.9 7.6 fusion.155
  294.3 9.3 fusion.157
  303.5 9.1 fusion.156
  318.4 129.7 %all-to-all-done.11 = f32[8,640,768]{2,1,0:T(8,128)} async-done(((f32[8,640,768]{2,1,0:T(8,128)}), f32[8,640,768]{2,1,0:T(8,128)}, u32[]{:S(2)}, u32[]{:S(2)}) %all-to-all-start.11) | async-done | bytes 15728672 | tf_op jit(solution)/shard_map/all_to_all | solution.py:299
  448.1 22.1 %split_rows.9 = (bf16[5120,768]{1,0:T(8,128)(2,1)}, bf16[5120,768]{1,0:T(8,128)(2,1)}, bf16[5120,768]{1,0:T(8,128)(2,1)}) custom-call(f32[5120,768]{1,0:T(8,128)} %bitcast.88.refs_0_, f32[5120,1]{1,0:T(8,128)} %copy.39.refs_1_), custom_call_target="tpu_custom_call" | custom-call | bytes 39321600 | tf_op jit(solution)/shard_map/split_rows/pallas_call | solution.py:237
  470.2 38.8 %multiply_convert_fusion.1 = bf16[5120,3328]{1,0:T(8,128)(2,1)} fusion(bf16[5120,768]{1,0:T(8,128)(2,1)} %get-tuple-element.519, bf16[3328,768]{1,0:T(8,128)(2,1)} %get-tuple-element.550), kind=kOutput, calls=%fused_computation.154 | convolution fusion | flops 26257653760 | bytes 47054848 | tf_op jit(solution)/shard_map/dot_general | solution.py:307
  509.0 39.6 %add_add_fusion = f32[3328,768]{1,0:T(8,128)} fusion(f32[3328,768]{1,0:T(8,128)} %fusion.156, f32[3328,768]{1,0:T(8,128)} %fusion.157, bf16[5120,3328]{1,0:T(8,128)(2,1)} %multiply_convert_fusion.1, bf16[5120,768]{1,0:T(8,128)(2,1)} %get-tuple-element.520), kind=kOutput, calls=%fused_computation.161 | convolution fusion | flops 26177568768 | bytes 72613888 | tf_op jit(solution)/shard_map/dot_general | solution.py:307
  566.8 159.1 %all-to-all-done.12 = f32[8,640,768]{2,1,0:T(8,128)} async-done(((f32[8,640,768]{2,1,0:T(8,128)}), f32[8,640,768]{2,1,0:T(8,128)}, u32[]{:S(2)}, u32[]{:S(2)}) %all-to-all-start.12) | async-done | bytes 15728672 | tf_op jit(solution)/shard_map/all_to_all | solution.py:299
  729.6 12.2 fusion.51
  741.7 35.3 %convolution_add_fusion = f32[5120,768]{1,0:T(8,128)} fusion(f32[5120,768]{1,0:T(8,128)} %fusion.51, bf16[5120,3328]{1,0:T(8,128)(2,1)} %get-tuple-element.652, bf16[3328,768]{1,0:T(8,128)(2,1)} %get-tuple-element.551), kind=kOutput, calls=%fused_computation.163 | convolution fusion | flops 26176389120 | bytes 70647808 | tf_op jit(solution)/shard_map/dot_general | solution.py:307
  777.1 71.2 %pair_sums.3 = (f32[4608,128]{1,0:T(8,128)}, f32[30720,128]{1,0:T(8,128)}) custom-call(s32[8192]{0:T(1024)} %fusion.69.x_line, s32[8192]{0:T(1024)} %get-tuple-element.368.y_line, f32[4608,128]{1,0:T(8,128)} %bitcast.295, f32[30720,128]{1,0:T(8,128)} %bitcast.98.yg.xg, f32[4608,128]{1,0:T(8,128)} %bitcast.297, f32[30720,128]{1,0:T(8,128)} %bitcast.92.xg.yg), custom_call_target="tpu_custom_call" | custom-call | bytes 201326592 | tf_op jit(solution)/shard_map/pair_sums/pallas_call | solution.py:135
  852.4 71.3 %pair_sums.2 = (f32[4608,128]{1,0:T(8,128)}, f32[30720,128]{1,0:T(8,128)}) custom-call(s32[8192]{0:T(1024)} %get-tuple-element.452.x_line, s32[8192]{0:T(1024)} %get-tuple-element.453.y_line, f32[4608,128]{1,0:T(8,128)} %bitcast.298, f32[30720,128]{1,0:T(8,128)} %bitcast.92.xg.yg, f32[4608,128]{1,0:T(8,128)} %bitcast.296, f32[30720,128]{1,0:T(8,128)} %bitcast.98.yg.xg), custom_call_target="tpu_custom_call" | custom-call | bytes 201326592 | tf_op jit(solution)/shard_map/pair_sums/pallas_call | solution.py:135
  932.3 17.1 %add_select_fusion.3 = f32[5120,768]{1,0:T(8,128)} fusion(f32[5120,768]{1,0:T(8,128)} %bitcast.302, f32[5120,768]{1,0:T(8,128)} %get-tuple-element.270, f32[5120]{0:T(1024)S(1)} %copy-done.49, pred[5120]{0:T(1024)(128)(4,1)S(1)} %copy-done.56), kind=kLoop, calls=%fused_computation.157 | loop fusion | flops 11796480 | bytes 47211520 | tf_op jit(solution)/shard_map/jit(_where)/select_n | solution.py:439
  949.4 194.1 %all-reduce.9.cloned.1.call-done = (f32[768,768]{1,0:T(8,128)}, f32[768,768]{1,0:T(8,128)}) async-done(((f32[768,768]{1,0:T(8,128)}, f32[768,768]{1,0:T(8,128)}), (f32[768,768]{1,0:T(8,128)}, f32[768,768]{1,0:T(8,128)})) %all-reduce.9.cloned.1.call-update) | async-done | bytes 4718608 | tf_op jit(solution)/shard_map/psum | solution.py:452
  1143.5 9.9 all-to-all-done.14
  1166.8 36.2 %subtract_rows.3 = f32[37728,128]{1,0:T(8,128)} custom-call(s32[2560]{0:T(1024)} %fusion.128.refs_0_, s32[5120]{0:T(1024)} %fusion.101.refs_1_, f32[37728,128]{1,0:T(8,128)} %bitcast.278, f32[4608,128]{1,0:T(8,128)} %bitcast.308, f32[15360,128]{1,0:T(8,128)} %bitcast.139.refs_4_, f32[30720,128]{1,0:T(8,128)} %bitcast.142.refs_5_), custom_call_target="tpu_custom_call" | custom-call | bytes 109412352 | tf_op jit(solution)/shard_map/subtract_rows/pallas_call | solution.py:199
  1202.9 127.7 %all-to-all-done.15 = f32[8,640,768]{2,1,0:T(8,128)} async-done(((f32[8,640,768]{2,1,0:T(8,128)}), f32[8,640,768]{2,1,0:T(8,128)}, u32[]{:S(2)}, u32[]{:S(2)}) %all-to-all-start.15) | async-done | bytes 15728672 | tf_op jit(solution)/shard_map/all_to_all | solution.py:299
  1330.6 29.7 %subtract_rows.2 = f32[37728,128]{1,0:T(8,128)} custom-call(s32[5120]{0:T(1024)} %fusion.95.refs_0_, f32[37728,128]{1,0:T(8,128)} %bitcast.281, f32[4608,128]{1,0:T(8,128)} %bitcast.307, f32[30720,128]{1,0:T(8,128)} %bitcast.130.refs_3_), custom_call_target="tpu_custom_call" | custom-call | bytes 85819392 | tf_op jit(solution)/shard_map/subtract_rows/pallas_call | solution.py:199
  (197 shorter events, 118.7 us)
Async XLA Ops:
  73.7 9.2 all-to-all-start.9
  83.0 54.1 %copy-start.45 = (s32[8,1,1601]{2,0,1:T(8,128)}, s32[8,1,1601]{2,0,1:T(8,128)S(1)}, u32[]{:S(2)}) copy-start(s32[8,1,1601]{2,0,1:T(8,128)S(1)} %copy.46) | copy-start | bytes 153700
  98.2 7.0 slice-start
  98.2 152.6 %all-to-all-start.10 = ((f32[8,320,768]{2,1,0:T(8,128)}), f32[8,320,768]{2,1,0:T(8,128)}, u32[]{:S(2)}, u32[]{:S(2)}) async-start(f32[8,320,768]{2,1,0:T(8,128)} %bitcast.299), calls=%async_computation.10 | async-start | bytes 15728640 | tf_op jit(solution)/shard_map/all_to_all | solution.py:299
  102.0 144.0 %all-reduce.7.cloned.1.call-start = ((), (), s32[]{:S(2)}) async-start(), calls=%async_computation.16 | async-start | bytes 9437184 | tf_op jit(solution)/shard_map/psum | solution.py:378
  105.3 15.7 %copy-start.29 = (s32[8192]{0:T(1024)S(1)}, s32[8192]{0:T(1024)}, u32[]{:S(2)}) copy-start(s32[8192]{0:T(1024)} %param.15) | copy-start | bytes 98308
  118.6 37.5 %copy-start.48 = (f32[5120]{0:T(1024)}, f32[5120]{0:T(1024)S(1)}, u32[]{:S(2)}) copy-start(f32[5120]{0:T(1024)S(1)} %get-tuple-element.439) | copy-start | bytes 61444
  124.1 32.1 %copy-start.46 = (s32[768]{0:T(1024)}, s32[768]{0:T(1024)S(1)}, u32[]{:S(2)}) copy-start(s32[768]{0:T(1024)S(1)} %convert_reduce_fusion.3) | copy-start | bytes 9220
  254.6 20.8 %copy-start.59 = (bf16[768,768]{1,0:T(8,128)(2,1)}, bf16[768,768]{1,0:T(8,128)(2,1)S(1)}, u32[]{:S(2)}) copy-start(bf16[768,768]{1,0:T(8,128)(2,1)S(1)} %get-tuple-element.514) | copy-start | bytes 3538948
  254.6 48.9 %copy-start.61 = (bf16[768,768]{1,0:T(8,128)(2,1)}, bf16[768,768]{1,0:T(8,128)(2,1)S(1)}, u32[]{:S(2)}) copy-start(bf16[768,768]{1,0:T(8,128)(2,1)S(1)} %get-tuple-element.515) | copy-start | bytes 3538948
  270.9 177.3 %all-to-all-start.11 = ((f32[8,640,768]{2,1,0:T(8,128)}), f32[8,640,768]{2,1,0:T(8,128)}, u32[]{:S(2)}, u32[]{:S(2)}) async-start(f32[8,640,768]{2,1,0:T(8,128)} %bitcast.293), calls=%async_computation.11 | async-start | bytes 31457280 | tf_op jit(solution)/shard_map/all_to_all | solution.py:299
  283.9 10.4 copy-start.63
  318.4 190.6 %copy-start.5 = (f32[768,768]{1,0:T(8,128)}, f32[768,768]{1,0:T(8,128)S(1)}, u32[]{:S(2)}) copy-start(f32[768,768]{1,0:T(8,128)S(1)} %get-tuple-element.260) | copy-start | bytes 7077892
  318.4 190.6 %copy-start.23 = (s32[3328]{0:T(1024)}, s32[3328]{0:T(1024)S(1)}, u32[]{:S(2)}) copy-start(s32[3328]{0:T(1024)S(1)} %get-tuple-element.631) | copy-start | bytes 39940
  548.6 4.5 copy-start.41
  548.6 4.5 copy-start.47
  548.6 4.6 copy-start.60
  548.6 4.6 copy-start.62
  548.6 177.2 %all-to-all-start.12 = ((f32[8,640,768]{2,1,0:T(8,128)}), f32[8,640,768]{2,1,0:T(8,128)}, u32[]{:S(2)}, u32[]{:S(2)}) async-start(f32[8,640,768]{2,1,0:T(8,128)} %bitcast.292), calls=%async_computation.12 | async-start | bytes 31457280 | tf_op jit(solution)/shard_map/all_to_all | solution.py:299
  725.8 122.4 %all-to-all-start.13 = ((f32[8,320,768]{2,1,0:T(8,128)}), f32[8,320,768]{2,1,0:T(8,128)}, u32[]{:S(2)}, u32[]{:S(2)}) async-start(f32[8,320,768]{2,1,0:T(8,128)} %bitcast.300), calls=%async_computation.13 | async-start | bytes 15728640 | tf_op jit(solution)/shard_map/all_to_all | solution.py:299
  729.5 414.0 %all-reduce.9.cloned.1.call-start = ((), (), s32[]{:S(2)}) async-start(), calls=%async_computation.17 | async-start | bytes 9437184 | tf_op jit(solution)/shard_map/psum | solution.py:452
  852.4 71.3 %copy-start.6 = (f32[768,768]{1,0:T(8,128)S(1)}, f32[768,768]{1,0:T(8,128)}, u32[]{:S(2)}) copy-start(f32[768,768]{1,0:T(8,128)} %copy-done.5) | copy-start | bytes 7077892
  852.4 71.3 %copy-start.55 = (f32[768]{0:T(1024)S(1)}, f32[768]{0:T(1024)}, u32[]{:S(2)}) copy-start(f32[768]{0:T(1024)} %copy-done.54) | copy-start | bytes 9220
  852.4 71.4 %copy-start.58 = (pred[768]{0:T(1024)(128)(4,1)S(1)}, pred[768]{0:T(1024)(128)(4,1)}, u32[]{:S(2)}) copy-start(pred[768]{0:T(1024)(128)(4,1)} %broadcast_compare_fusion.2) | copy-start | bytes 2308
  927.2 226.2 %all-to-all-start.14 = ((f32[8,640,768]{2,1,0:T(8,128)}), f32[8,640,768]{2,1,0:T(8,128)}, u32[]{:S(2)}, u32[]{:S(2)}) async-start(f32[8,640,768]{2,1,0:T(8,128)} %bitcast.301), calls=%async_computation.14 | async-start | bytes 31457280 | tf_op jit(solution)/shard_map/all_to_all | solution.py:299
  1153.4 4.5 copy-start.51
  1153.4 4.6 copy-start.53
  1153.4 4.6 copy-start.50
  1153.4 11.8 copy-start.22
  1153.4 177.2 %all-to-all-start.15 = ((f32[8,640,768]{2,1,0:T(8,128)}), f32[8,640,768]{2,1,0:T(8,128)}, u32[]{:S(2)}, u32[]{:S(2)}) async-start(f32[8,640,768]{2,1,0:T(8,128)} %bitcast.294), calls=%async_computation.15 | async-start | bytes 31457280 | tf_op jit(solution)/shard_map/all_to_all | solution.py:299
  1330.6 29.8 %copy-start.30 = (s32[8192]{0:T(1024)S(1)}, s32[8192]{0:T(1024)}, u32[]{:S(2)}) copy-start(s32[8192]{0:T(1024)} %param.15) | copy-start | bytes 98308
  1330.6 29.8 %copy-start.32 = (s32[8192]{0:T(1024)S(1)}, s32[8192]{0:T(1024)}, u32[]{:S(2)}) copy-start(s32[8192]{0:T(1024)} %param.16) | copy-start | bytes 98308
  (8 other events, 13.9 us)
Sparse Core Ops, SparseCore 0:
  109.5 136.4 all-reduce.6
  927.3 216.1 all-reduce.8

commit v4 on v3

--- a/solution.py
+++ b/solution.py
@@ -25,6 +25,11 @@
     return common_slots // 4 + (num_ids - common_slots + shards - 1) // shards
 
 
+def context_capacity(num_ids, shards):
+    share = tight_capacity(num_ids, shards) * 5 // 8
+    return share + 64, tight_capacity(num_ids, shards) - share + 64
+
+
 def tight_capacity(num_ids, shards):
     return (num_ids - 3 * num_ids // shards + shards - 1) // shards
 
@@ -58,7 +63,7 @@
                 o_ref[pl.ds(t * SUBLANES * chunks + j, chunks, stride=SUBLANES), :] = got[j]
             return carry
 
-        lax.fori_loop(0, cap // SUBLANES, step, 0, unroll=4)
+        lax.fori_loop(0, cap // SUBLANES, step, 0, unroll=2)
 
     out = pl.pallas_call(
         body,
@@ -74,20 +79,28 @@
     return row_view(out, d)
 
 
-def pair_sums(x_hot, x_got, y_hot, y_got, x_row, y_row):
-    d = x_hot.shape[1]
-    chunks, pairs = d // LANES, x_row.shape[0]
-    views = [tile_view(a) for a in (x_hot, x_got, y_hot, y_got)]
-    xh_lines, xg_lines, yh_lines, yg_lines = [v.shape[0] for v in views]
-    x_lines, y_lines = xh_lines + xg_lines, yh_lines + yg_lines
-
-    def body(x_line, y_line, xh, xg, yh, yg, oh, og, x_all, y_all, total, prod, sem):
-        copies = [
-            pltpu.make_async_copy(xh, x_all.at[pl.ds(0, xh_lines)], sem.at[0]),
-            pltpu.make_async_copy(xg, x_all.at[pl.ds(xh_lines, xg_lines)], sem.at[1]),
-            pltpu.make_async_copy(yh, y_all.at[pl.ds(0, yh_lines)], sem.at[2]),
-            pltpu.make_async_copy(yg, y_all.at[pl.ds(yh_lines, yg_lines)], sem.at[3]),
-        ]
+def pair_sums(x_parts, y_parts, x_row, y_row, count, from_y=False):
+    d = x_parts[0].shape[1]
+    chunks, per_step = d // LANES, PAIR_TILES * SUBLANES
+    views = [tile_view(a) for a in x_parts + y_parts]
+    num_x, num_y = len(x_parts), len(y_parts)
+    sizes = [v.shape[0] for v in views]
+    x_lines, y_lines = sum(sizes[:num_x]), sum(sizes[num_x:])
+    y_size = y_lines + SUBLANES * chunks
+    y_starts = [sum(sizes[num_x:num_x + k]) for k in range(num_y)]
+
+    def body(*refs):
+        number, x_line, y_line = refs[:3]
+        ins = refs[3:3 + num_x + num_y]
+        outs = refs[3 + num_x + num_y:3 + num_x + 2 * num_y]
+        x_all, y_all, total, prod, sem = refs[3 + num_x + 2 * num_y:]
+        copies = []
+        for k, ref in enumerate(ins):
+            start = sum(sizes[:k]) if k < num_x else y_starts[k - num_x]
+            held = x_all if k < num_x else y_all
+            copies.append(pltpu.make_async_copy(ref, held.at[pl.ds(start, sizes[k])], sem.at[k]))
+            if from_y and k >= num_x:
+                copies.append(pltpu.make_async_copy(ref, total.at[pl.ds(start, sizes[k])], sem.at[k + num_y]))
         for copy in copies:
             copy.start()
 
@@ -95,17 +108,18 @@
             total[pl.ds(pl.multiple_of(t * 64, 64), 64), :] = jnp.zeros((64, LANES), jnp.float32)
             return carry
 
-        lax.fori_loop(0, y_lines // 64, zero, 0)
+        if not from_y:
+            lax.fori_loop(0, y_lines // 64, zero, 0)
         for copy in copies:
             copy.wait()
 
         def step(t, carry):
             run, last = carry
             kept, lines, grads = [], [], []
-            for i in range(PAIR_TILES * SUBLANES):
+            for i in range(per_step):
                 tile, j = i // SUBLANES, i % SUBLANES
-                line = y_line[t * PAIR_TILES * SUBLANES + i]
-                x = x_all[pl.ds(x_line[t * PAIR_TILES * SUBLANES + i], chunks, stride=SUBLANES), :]
+                line = y_line[t * per_step + i]
+                x = x_all[pl.ds(x_line[t * per_step + i], chunks, stride=SUBLANES), :]
                 y = y_all[pl.ds(line, chunks, stride=SUBLANES), :]
                 prod[pl.ds(tile * SUBLANES * chunks + j, chunks, stride=SUBLANES), :] = x * y
                 kept.append(x)
@@ -116,35 +130,35 @@
                     part = part + prod[pl.ds((tile * chunks + k) * SUBLANES, SUBLANES), :]
                 score = jnp.broadcast_to(jnp.sum(part, axis=1, keepdims=True), (SUBLANES, LANES))
                 grads.append(jax.nn.sigmoid(score) - 1.0)
-            for i in range(PAIR_TILES * SUBLANES):
+            for i in range(per_step):
                 tile, j = i // SUBLANES, i % SUBLANES
                 same = (lines[i] == last).astype(jnp.float32)
                 run = run * same + jnp.broadcast_to(grads[tile][j:j + 1, :], (chunks, LANES)) * kept[i]
-                total[pl.ds(lines[i], chunks, stride=SUBLANES), :] = run
+                at = pl.ds(lines[i], chunks, stride=SUBLANES)
+                total[at, :] = y_all[at, :] - LEARN_RATE * run if from_y else run
                 last = lines[i]
             return run, last
 
-        lax.fori_loop(0, pairs // (PAIR_TILES * SUBLANES), step, (jnp.zeros((chunks, LANES), jnp.float32), jnp.int32(-1)))
-        out_hot = pltpu.make_async_copy(total.at[pl.ds(0, yh_lines)], oh, sem.at[0])
-        out_got = pltpu.make_async_copy(total.at[pl.ds(yh_lines, yg_lines)], og, sem.at[1])
-        out_hot.start()
-        out_got.start()
-        out_hot.wait()
-        out_got.wait()
-
-    oh, og = pl.pallas_call(
+        lax.fori_loop(0, pl.cdiv(number[0], per_step), step, (jnp.zeros((chunks, LANES), jnp.float32), jnp.int32(-1)))
+        copies = [pltpu.make_async_copy(total.at[pl.ds(y_starts[k], sizes[num_x + k])], outs[k], sem.at[k]) for k in range(num_y)]
+        for copy in copies:
+            copy.start()
+        for copy in copies:
+            copy.wait()
+
+    results = pl.pallas_call(
         body,
         grid_spec=pltpu.PrefetchScalarGridSpec(
-            num_scalar_prefetch=2, grid=(1,), in_specs=[ANY] * 4, out_specs=[ANY] * 2,
-            scratch_shapes=[pltpu.VMEM((x_lines, LANES), jnp.float32), pltpu.VMEM((y_lines, LANES), jnp.float32),
-                            pltpu.VMEM((y_lines, LANES), jnp.float32), pltpu.VMEM((PAIR_TILES * SUBLANES * chunks, LANES), jnp.float32),
-                            pltpu.SemaphoreType.DMA((4,))]),
-        out_shape=[jax.ShapeDtypeStruct((yh_lines, LANES), jnp.float32), jax.ShapeDtypeStruct((yg_lines, LANES), jnp.float32)],
-        cost_estimate=pl.CostEstimate(flops=0, bytes_accessed=8 * 4 * d * pairs, transcendentals=0),
+            num_scalar_prefetch=3, grid=(1,), in_specs=[ANY] * (num_x + num_y), out_specs=[ANY] * num_y,
+            scratch_shapes=[pltpu.VMEM((x_lines, LANES), jnp.float32), pltpu.VMEM((y_size, LANES), jnp.float32),
+                            pltpu.VMEM((y_size, LANES), jnp.float32), pltpu.VMEM((per_step * chunks, LANES), jnp.float32),
+                            pltpu.SemaphoreType.DMA((num_x + 2 * num_y,))]),
+        out_shape=[jax.ShapeDtypeStruct((n, LANES), jnp.float32) for n in sizes[num_x:]],
+        cost_estimate=pl.CostEstimate(flops=0, bytes_accessed=8 * 4 * d * x_row.shape[0], transcendentals=0),
         compiler_params=pltpu.CompilerParams(vmem_limit_bytes=VMEM_BYTES),
         name='pair_sums',
-    )(first_line(x_row, d), first_line(y_row, d), *views)
-    return row_view(oh, d), row_view(og, d)
+    )(count.astype(jnp.int32).reshape(1), first_line(x_row, d), first_line(y_row, d), *views)
+    return [row_view(r, d) for r in results]
 
 
 def subtract_rows(table, hot, parts):
@@ -253,9 +267,9 @@
     return (inner + outer).astype(jnp.int32).reshape(-1)
 
 
-def mark_unique(sorted_ids, shard_rows, shards, hot):
+def mark_unique(sorted_ids, shard_rows, shards, hot, limit=NO_ID):
     previous = jnp.concatenate([jnp.full((1,), -1, jnp.int32), sorted_ids[:-1]])
-    first = (sorted_ids != previous) & (sorted_ids >= hot)
+    first = (sorted_ids != previous) & (sorted_ids >= hot) & (sorted_ids < limit)
     owner = sorted_ids // shard_rows
     rank = running_count(first) - 1
     owners = jnp.arange(shards, dtype=jnp.int32)
@@ -265,26 +279,29 @@
     return first, owner, rank - start_of, counts
 
 
+def fill_cells(counts, capacity, shards):
+    owners = jnp.arange(shards, dtype=jnp.int32)[:, None]
+    slot = jnp.arange(capacity, dtype=jnp.int32)[None, :]
+    return jnp.where(slot >= counts[:, None], owners * capacity + slot, NO_ID).reshape(-1)
+
+
+def spread(values, capacity):
+    return jnp.broadcast_to(values[:, None], (values.shape[0], capacity)).reshape(-1)
+
+
 def ask_lists(sorted_ids, first, owner, rank, counts, shard_rows, shards, capacity):
     num_ids = sorted_ids.shape[0]
     cells = shards * capacity
+    pack = 2 * num_ids
     key = jnp.where(first & (rank < capacity), owner * capacity + rank, NO_ID)
-    owners = jnp.arange(shards, dtype=jnp.int32)[:, None]
-    slot = jnp.arange(capacity, dtype=jnp.int32)[None, :]
-    past = (owners + 1) * shard_rows
-    ends = jnp.sum((sorted_ids[None, :] < past).astype(jnp.int32), axis=1, keepdims=True)
-    fill_key = jnp.where(slot >= counts[:, None], owners * capacity + slot, NO_ID)
-
-    def flat(values):
-        return jnp.broadcast_to(values, (shards, capacity)).reshape(-1)
-
-    _, asked, places = lax.sort((
-        jnp.concatenate([key, fill_key.reshape(-1)]),
-        jnp.concatenate([sorted_ids, flat(past)]),
-        jnp.concatenate([jnp.arange(num_ids, dtype=jnp.int32), flat(ends)])), num_keys=1)
-    places = places[:cells]
+    past = (jnp.arange(shards, dtype=jnp.int32) + 1) * shard_rows
+    ends = jnp.sum((sorted_ids[None, :] < past[:, None]).astype(jnp.int32), axis=1)
+    packed = lax.sort((
+        jnp.concatenate([key, fill_cells(counts, capacity, shards)]),
+        jnp.concatenate([sorted_ids * pack + jnp.arange(num_ids, dtype=jnp.int32), spread(past * pack + ends, capacity)])), num_keys=1)[1][:cells]
+    places = packed % pack
     times = jnp.concatenate([places[1:], jnp.full((1,), num_ids, jnp.int32)]) - places
-    return asked[:cells].reshape(shards, capacity), times
+    return (packed // pack).reshape(shards, capacity), times
 
 
 def hot_times(ids, hot):
@@ -386,20 +403,45 @@
     cen_first, cen_owner, cen_rank, cen_counts = mark_unique(cen_sorted, shard_rows, shards, hot)
     cen_asked, cen_times = ask_lists(cen_sorted, cen_first, cen_owner, cen_rank, cen_counts, shard_rows, shards, cap_pairs)
     cen_cell = cell_of(cen_sorted, cen_owner, cen_rank, shards, hot, cap_pairs)
-    con_sorted, cen_by_con = lax.sort((con_moved, cen_cell), num_keys=1)
-    con_first, con_owner, con_rank, con_counts = mark_unique(con_sorted, shard_rows, shards, hot)
-    con_asked, _ = ask_lists(con_sorted, con_first, con_owner, con_rank, con_counts, shard_rows, shards, cap_pairs)
-    con_cell = cell_of(con_sorted, con_owner, con_rank, shards, hot, cap_pairs)
-    fits = (jnp.max(neg_counts) <= cap_negs) & (jnp.max(cen_counts) <= cap_pairs) & (jnp.max(con_counts) <= cap_pairs)
+    cap_con, cap_ship = context_capacity(num_pairs, shards)
+    past_all = shards * shard_rows
+    sent = (cen_sorted < hot) & (con_moved >= hot)
+    con_keys, cen_by_con = lax.sort((con_moved + jnp.where(sent, past_all, 0), cen_cell), num_keys=1)
+    stays = con_keys < past_all
+    num_stay = jnp.sum(stays.astype(jnp.int32))
+    con_first, con_owner, con_rank, con_counts = mark_unique(con_keys, shard_rows, shards, hot, past_all)
+    con_cell = jnp.where(stays, cell_of(con_keys, con_owner, con_rank, shards, hot, cap_con), hot + shards * cap_con)
+    sent_center = cen_by_con
+    cen_key = jnp.where(stays, cen_by_con, hot + shards * cap_pairs)
+    cen_by_con = jnp.where(stays, cen_by_con, 0)
+    owners = jnp.arange(shards, dtype=jnp.int32)
+    past = (owners + 1) * shard_rows
+    ship_owner = con_owner - shards
+    ship_upto = jnp.sum((con_keys[None, :] < (past + past_all)[:, None]).astype(jnp.int32), axis=1)
+    ship_from = jnp.concatenate([num_stay[None], ship_upto[:-1]])
+    ship_counts = ship_upto - ship_from
+    from_of = jnp.sum(jnp.where(ship_owner[None, :] == owners[:, None], ship_from[:, None], 0), axis=0)
+    ship_rank = jnp.arange(num_pairs, dtype=jnp.int32) - from_of
+    con_cells = shards * cap_con
+    key = jnp.where(con_first & (con_rank < cap_con), con_owner * cap_con + con_rank, NO_ID)
+    key = jnp.where(stays | (ship_rank >= cap_ship), key, con_cells + ship_owner * cap_ship + ship_rank)
+    ship_fill = fill_cells(ship_counts, cap_ship, shards)
+    pack = 2 * hot
+    both = lax.sort((
+        jnp.concatenate([key, fill_cells(con_counts, cap_con, shards), jnp.where(ship_fill < NO_ID, con_cells + ship_fill, NO_ID)]),
+        jnp.concatenate([jnp.where(stays, con_keys, (con_keys - past_all) * pack + sent_center), spread(past, cap_con), spread(past * pack + hot, cap_ship)])), num_keys=1)[1]
+    con_asked = both[:con_cells].reshape(shards, cap_con)
+    shipped = both[con_cells:con_cells + shards * cap_ship].reshape(shards, cap_ship)
+    fits = (jnp.max(neg_counts) <= cap_negs) & (jnp.max(cen_counts) <= cap_pairs) & (jnp.max(con_counts) <= cap_con) & (jnp.max(ship_counts) <= cap_ship)
     spill = jnp.broadcast_to(1 - fits.astype(jnp.int32), (shards, 1))
-    asked = exchange_ids(jnp.concatenate([cen_asked, con_asked, neg_asked, spill], axis=1))
+    asked = exchange_ids(jnp.concatenate([cen_asked, con_asked, neg_asked, shipped, spill], axis=1))
     all_fit = jnp.sum(asked[:, -1]) == 0
-    cen_local = asked[:, :cap_pairs] - me * shard_rows
-    con_local = asked[:, cap_pairs:2 * cap_pairs] - me * shard_rows
-    neg_local = asked[:, 2 * cap_pairs:-1] - me * shard_rows
+    cuts = [0, cap_pairs, cap_pairs + cap_con, cap_pairs + cap_con + cap_negs, asked.shape[1] - 1]
+    cen_local, con_local, neg_local = [asked[:, cuts[k]:cuts[k + 1]] - me * shard_rows for k in range(3)]
+    taken = asked[:, cuts[3]:cuts[4]].reshape(-1)
     neg_send = gather_rows(out_shard, jnp.minimum(neg_local, shard_rows - 1).reshape(-1), shards)
     neg_got = exchange(neg_send, shards)
-    cen_order, con_by_cen = lax.sort((cen_by_con, con_cell), num_keys=1)
+    cen_order, con_by_cen = lax.sort((cen_key, jnp.where(stays, con_cell, 0)), num_keys=1)
 
     cen_send = gather_rows(in_shard, jnp.minimum(cen_local, shard_rows - 1).reshape(-1), shards)
     cen_send, neg_got, hot_in, hot_out = lax.optimization_barrier((cen_send, neg_got, hot_in, hot_out))
@@ -408,6 +450,12 @@
     con_send, cen_got = after(con_send, cen_got)
     con_got = exchange(con_send, shards)
 
+    taken_by_con = lax.sort(taken - me * shard_rows * pack)
+    taken_by_cen = lax.sort((taken % pack) * (2 * shard_rows) + taken // pack - me * shard_rows)
+    num_taken = jnp.sum((taken % pack < hot).astype(jnp.int32))
+    base_out, = pair_sums([hot_in], [out_shard], jnp.minimum(taken_by_con % pack, hot - 1), taken_by_con // pack, num_taken, True)
+    ship_hot, = pair_sums([out_shard], [hot_in], jnp.minimum(taken_by_cen % (2 * shard_rows), shard_rows - 1), taken_by_cen // (2 * shard_rows), num_taken)
+
     neg_times = jnp.concatenate([hot_times(negative_ids, hot), neg_times])
     hot_cen_times = hot_times(center_ids, hot)
     w_half, w_high, w_low = split_rows([hot_out, neg_got], neg_times)
@@ -429,8 +477,8 @@
     d_neg = jnp.where(neg_times[:, None] > 0, neg_times.astype(jnp.float32)[:, None] * d_neg, 0.0)
     neg_part, neg_hot = d_neg[hot:], d_neg[:hot]
 
-    con_hot, con_part = pair_sums(hot_in, cen_got, hot_out, con_got, cen_by_con, con_cell)
-    cen_hot, cen_part = pair_sums(hot_out, con_got, hot_in, cen_got, con_by_cen, cen_order)
+    con_hot, con_part = pair_sums([hot_in, cen_got], [hot_out, con_got], cen_by_con, con_cell, num_stay)
+    cen_hot, cen_part = pair_sums([hot_out, con_got], [hot_in, cen_got], con_by_cen, cen_order, num_stay)
 
     def center_grads(grad, times, pair_part):
         d = dot(grad, w_high, cols_in) + dot(grad[:, :hot], w_low[:hot], cols_in)
@@ -438,7 +486,7 @@
         d = when(more, lambda d: d + dot(grad[:, hot:], w_low[hot:], cols_in) + dot(grad, rest(neg_times, w_half, w_high, w_low), cols_in), d)
         return jnp.where(times[:, None] > 0, times.astype(jnp.float32)[:, None] * d + pair_part, 0.0)
 
-    cen_hot = center_grads(grad_h, hot_cen_times, cen_hot)
+    cen_hot = center_grads(grad_h, hot_cen_times, cen_hot) + ship_hot
     cen_part = center_grads(grad_c, cen_times, cen_part)
 
     neg_part, con_got = after(neg_part, con_got)
@@ -446,11 +494,12 @@
     con_part, neg_back = after(con_part, neg_back)
     con_back = exchange(con_part, shards)
     out_hot = lax.psum(con_hot + neg_hot, AXIS_NAME)
-    cen_part, con_back, out_hot = lax.optimization_barrier((cen_part, con_back, out_hot))
+    cen_part, con_back, out_hot, cen_hot = lax.optimization_barrier((cen_part, con_back, out_hot, cen_hot))
     cen_back = exchange(cen_part, shards)
     out_hot = jnp.where(me == 0, out_hot, 0.0)
-    in_hot = jnp.where(me == 0, lax.psum(cen_hot, AXIS_NAME), 0.0)
-    new_out = subtract_rows(out_shard, out_hot, [(neg_local, neg_back), (con_local, con_back)])
+    in_hot = lax.psum(cen_hot, AXIS_NAME)
+    in_hot = jnp.where(me == 0, in_hot, 0.0)
+    new_out = subtract_rows(base_out, out_hot, [(neg_local, neg_back), (con_local, con_back)])
     new_in = subtract_rows(in_shard, in_hot, [(cen_local, cen_back)])
     return new_in, new_out, all_fit
 

time: 1380 us -> 1200 us (0.87)
  waiting for transfers between devices: 697 us -> 481 us
  other arithmetic: 114 us -> 140 us
  Pallas kernels: 300 us -> 325 us
    all_to_all x6, waiting for transfers between devices: 426 us -> 256 us  [exchange(): lax.all_to_all(rows.reshape(shards, -1, rows.shape[-1]), AXIS_NAME, 0, 0)]
    psum x1 -> x2, waiting for transfers between devices: 194 us -> 154 us  [the longest x1 96.3 us: tight_step(): in_hot = lax.psum(cen_hot, AXIS_NAME)]
    pallas_call x2 -> x4, Pallas kernels: 143 us -> 172 us  [pair_sums(): pl.pallas_call(body, grid_spec=pltpu.PrefetchScalarGridSpec(num_scalar_pr...]
    sort x5 -> x7, other arithmetic: 38.2 us -> 59.1 us  [the longest x2 25.6 us: ask_lists(): lax.sort((jnp.concatenate([key, fill_cells(counts, capacity, shards)]), j...]
  transfers between devices with their start and end apart: 9 -> 10, of which waited for: 7 -> 8; matrix products, arithmetic and copies ran while one was open for 11% -> 15% of each run, Pallas kernels for 10% -> 20%
where the time goes in v4:
time: 1200 us; the launch traced here: 1190 us
  waiting for transfers between devices  481 us (40%)
  Pallas kernels  325 us (27%)
  matrix products  164 us (14%)
  other arithmetic  140 us (12%)
  starting transfers between devices  29 us (2%)
  local copies, waits for them, and re-layouts  25.8 us (2%)
  between operations  21.5 us (2%)
    all_to_all x6, waiting for transfers between devices, exchange(): lax.all_to_all(rows.reshape(shards, -1, rows.shape[-1]), AXIS_NAME, 0, 0)  256 us
    pallas_call x4, Pallas kernels, pair_sums(): pl.pallas_call(body, grid_spec=pltpu.PrefetchScalarGridSpec(num_scalar_pr...  172 us
    dot_general x9, matrix products, dot(): lax.dot_general(a, b, (dims, ((), ())), preferred_element_type=jnp.float32)  163 us
    psum x1, waiting for transfers between devices, tight_step(): in_hot = lax.psum(cen_hot, AXIS_NAME)  96.3 us
    psum x1, waiting for transfers between devices, tight_step(): hot_both = lax.psum(jnp.where(me == 0, hot_both, 0.0), AXIS_NAME)  66.1 us
    pallas_call x2, Pallas kernels, subtract_rows(): pl.pallas_call(body, grid_spec=pltpu.PrefetchScalarGridSpec(num_scalar_pr...  62.2 us
    psum x1, waiting for transfers between devices, tight_step(): out_hot = lax.psum(con_hot + neg_hot, AXIS_NAME)  57.2 us
    pallas_call x3, Pallas kernels, gather_rows(): pl.pallas_call(body, grid_spec=pltpu.PrefetchScalarGridSpec(num_scalar_pr...  48.8 us
  transfers between devices with their start and end apart: 10, of which 8 were waited for; matrix products, arithmetic and copies ran while one was open for 15% of the time, Pallas kernels for 20%

profile of v4, /device:TPU:0, one launch (start us, length us, event | category | flops | bytes accessed | tf_op | source)
XLA Modules:
  0.0 1187.5 jit_solution(5666558524423641169)
XLA Ops:
  7.2 7.7 sort.297
  24.3 6.9 sort.299
  37.6 8.3 sort.300
  49.5 8.0 sort.302
  58.7 17.6 %sort.298 = (s32[13312]{0:T(1024)}, s32[13312]{0:T(1024)S(1)}, s32[13312]{0:T(1024)}) sort(s32[13312]{0:T(1024)S(1)} %get-tuple-element.466, s32[13312]{0:T(1024)S(1)} %get-tuple-element.467, s32[13312]{0:T(1024)S(1)} %iota.214), dimensions={0}, to_apply=%region_5.6 | sort | flops 186368 | bytes 319488 | tf_op jit(solution)/shard_map/sort | solution.py:299
  88.6 14.2 %gather_rows.5 = f32[15360,128]{1,0:T(8,128)} custom-call(s32[2560]{0:T(1024)} %fusion.133.line, f32[37728,128]{1,0:T(8,128)} %bitcast.284), custom_call_target="tpu_custom_call" | custom-call | bytes 42909696 | tf_op jit(solution)/shard_map/gather_rows/pallas_call | solution.py:68
  141.1 16.4 %gather_rows.3 = f32[22272,128]{1,0:T(8,128)} custom-call(s32[3712]{0:T(1024)} %fusion.113.line, f32[37728,128]{1,0:T(8,128)} %bitcast.285), custom_call_target="tpu_custom_call" | custom-call | bytes 53526528 | tf_op jit(solution)/shard_map/gather_rows/pallas_call | solution.py:68
  159.8 18.3 %gather_rows.4 = f32[30720,128]{1,0:T(8,128)} custom-call(s32[5120]{0:T(1024)} %fusion.102.line, f32[37728,128]{1,0:T(8,128)} %bitcast.289), custom_call_target="tpu_custom_call" | custom-call | bytes 66502656 | tf_op jit(solution)/shard_map/gather_rows/pallas_call | solution.py:68
  184.5 66.1 %all-reduce.7.cloned.1.call-done = f32[1536,768]{1,0:T(8,128)} async-done(((f32[1536,768]{1,0:T(8,128)}), f32[1536,768]{1,0:T(8,128)}) %all-reduce.7.cloned.1.call-update) | async-done | bytes 4718608 | tf_op jit(solution)/shard_map/psum | solution.py:395
  259.2 16.2 %split_rows.8 = (bf16[3328,768]{1,0:T(8,128)(2,1)}, bf16[3328,768]{1,0:T(8,128)(2,1)}, bf16[3328,768]{1,0:T(8,128)(2,1)}) custom-call(f32[768,768]{1,0:T(8,128)} %get-tuple-element.257.refs_0_, f32[2560,768]{1,0:T(8,128)} %bitcast.84.refs_1_, f32[3328,1]{1,0:T(8,128)} %copy.38.refs_2_), custom_call_target="tpu_custom_call" | custom-call | bytes 25559040 | tf_op jit(solution)/shard_map/split_rows/pallas_call | solution.py:251
  279.7 8.5 multiply_convert_fusion.2
  288.2 22.3 %pair_sums.6 = f32[4608,128]{1,0:T(8,128)} custom-call(s32[1]{0:T(128)} %bitcast.125.refs_0_, s32[2432]{0:T(1024)} %get-tuple-element.463.refs_1_, s32[2432]{0:T(1024)} %get-tuple-element.462.refs_2_, f32[37728,128]{1,0:T(8,128)} %bitcast.286, f32[4608,128]{1,0:T(8,128)} %bitcast.301), custom_call_target="tpu_custom_call" | custom-call | bytes 59768832 | tf_op jit(solution)/shard_map/pair_sums/pallas_call | solution.py:149
  310.5 7.6 fusion.201
  320.8 9.2 fusion.199
  330.1 9.2 fusion.200
  339.5 112.9 %all-to-all-done.11 = f32[8,640,768]{2,1,0:T(8,128)} async-done(((f32[8,640,768]{2,1,0:T(8,128)}), f32[8,640,768]{2,1,0:T(8,128)}, u32[]{:S(2)}, u32[]{:S(2)}) %all-to-all-start.11) | async-done | bytes 15728672 | tf_op jit(solution)/shard_map/all_to_all | solution.py:316
  452.4 22.1 %split_rows.7 = (bf16[5120,768]{1,0:T(8,128)(2,1)}, bf16[5120,768]{1,0:T(8,128)(2,1)}, bf16[5120,768]{1,0:T(8,128)(2,1)}) custom-call(f32[5120,768]{1,0:T(8,128)} %bitcast.86.refs_0_, f32[5120,1]{1,0:T(8,128)} %copy.37.refs_1_), custom_call_target="tpu_custom_call" | custom-call | bytes 39321600 | tf_op jit(solution)/shard_map/split_rows/pallas_call | solution.py:251
  474.5 38.8 %multiply_convert_fusion.1 = bf16[5120,3328]{1,0:T(8,128)(2,1)} fusion(bf16[5120,768]{1,0:T(8,128)(2,1)} %get-tuple-element.537, bf16[3328,768]{1,0:T(8,128)(2,1)} %get-tuple-element.568), kind=kOutput, calls=%fused_computation.154 | convolution fusion | flops 26257653760 | bytes 47054848 | tf_op jit(solution)/shard_map/dot_general | solution.py:324
  513.3 39.6 %add_add_fusion = f32[3328,768]{1,0:T(8,128)} fusion(f32[3328,768]{1,0:T(8,128)} %fusion.199, f32[3328,768]{1,0:T(8,128)} %fusion.200, bf16[5120,3328]{1,0:T(8,128)(2,1)} %multiply_convert_fusion.1, bf16[5120,768]{1,0:T(8,128)(2,1)} %get-tuple-element.538), kind=kOutput, calls=%fused_computation.161 | convolution fusion | flops 26177568768 | bytes 72613888 | tf_op jit(solution)/shard_map/dot_general | solution.py:324
  570.8 112.6 %all-to-all-done.12 = f32[8,464,768]{2,1,0:T(8,128)} async-done(((f32[8,464,768]{2,1,0:T(8,128)}), f32[8,464,768]{2,1,0:T(8,128)}, u32[]{:S(2)}, u32[]{:S(2)}) %all-to-all-start.12) | async-done | bytes 11403296 | tf_op jit(solution)/shard_map/all_to_all | solution.py:316
  687.0 12.2 %fusion.51 = f32[5120,768]{1,0:T(8,128)} fusion(bf16[5120,3328]{1,0:T(8,128)(2,1)} %get-tuple-element.668, bf16[3328,768]{1,0:T(8,128)(2,1)} %get-tuple-element.566), kind=kOutput, calls=%fused_computation.164 | convolution fusion | flops 6039797760 | bytes 24772608 | tf_op jit(solution)/shard_map/dot_general | solution.py:324
  699.2 35.2 %convolution_add_fusion = f32[5120,768]{1,0:T(8,128)} fusion(f32[5120,768]{1,0:T(8,128)} %fusion.51, bf16[5120,3328]{1,0:T(8,128)(2,1)} %get-tuple-element.668, bf16[3328,768]{1,0:T(8,128)(2,1)} %get-tuple-element.569), kind=kOutput, calls=%fused_computation.163 | convolution fusion | flops 26176389120 | bytes 70647808 | tf_op jit(solution)/shard_map/dot_general | solution.py:324
  734.4 56.8 %pair_sums.5 = (f32[4608,128]{1,0:T(8,128)}, f32[22272,128]{1,0:T(8,128)}) custom-call(s32[1]{0:T(128)} %bitcast.58.refs_0_, s32[8192]{0:T(1024)} %get-tuple-element.451.refs_1_, s32[8192]{0:T(1024)} %get-tuple-element.368.refs_2_, f32[4608,128]{1,0:T(8,128)} %bitcast.302, f32[30720,128]{1,0:T(8,128)} %bitcast.100.refs_6_.refs_4_, f32[4608,128]{1,0:T(8,128)} %bitcast.308, ...), custom_call_target="tpu_custom_call" | custom-call | bytes 201326592 | tf_op jit(solution)/shard_map/pair_sums/pallas_call | solution.py:149
  800.3 59.1 %pair_sums.4 = (f32[4608,128]{1,0:T(8,128)}, f32[30720,128]{1,0:T(8,128)}) custom-call(s32[1]{0:T(128)} %bitcast.58.refs_0_, s32[8192]{0:T(1024)} %fusion.65.refs_1_, s32[8192]{0:T(1024)} %fusion.67.refs_2_, f32[4608,128]{1,0:T(8,128)} %bitcast.309, f32[22272,128]{1,0:T(8,128)} %bitcast.94.refs_4_.refs_6_, f32[4608,128]{1,0:T(8,128)} %bitcast.303, ...), custom_call_target="tpu_custom_call" | custom-call | bytes 201326592 | tf_op jit(solution)/shard_map/pair_sums/pallas_call | solution.py:149
  859.5 17.2 %add_select_fusion.3 = f32[5120,768]{1,0:T(8,128)} fusion(f32[5120,768]{1,0:T(8,128)} %bitcast.312, f32[5120,768]{1,0:T(8,128)} %get-tuple-element.262, f32[5120]{0:T(1024)S(1)} %copy-done.52, pred[5120]{0:T(1024)(128)(4,1)S(1)} %copy-done.60), kind=kLoop, calls=%fused_computation.157 | loop fusion | flops 11796480 | bytes 47211520 | tf_op jit(solution)/shard_map/jit(_where)/select_n | solution.py:487
  878.6 57.2 %all-reduce.9.cloned.1.call-done = f32[768,768]{1,0:T(8,128)} async-done(((f32[768,768]{1,0:T(8,128)}), f32[768,768]{1,0:T(8,128)}) %all-reduce.9.cloned.1.call-update) | async-done | bytes 2359312 | tf_op jit(solution)/shard_map/psum | solution.py:496
  935.8 11.2 all-to-all-done.14
  962.4 34.0 %pair_sums.7.refs_2_ = f32[37728,128]{1,0:T(8,128)} custom-call(s32[1]{0:T(128)} %bitcast.125.refs_0_, s32[2432]{0:T(1024)} %get-tuple-element.461.refs_1_, s32[2432]{0:T(1024)} %get-tuple-element.460.refs_2_, f32[4608,128]{1,0:T(8,128)} %bitcast.304, f32[37728,128]{1,0:T(8,128)} %bitcast.287), custom_call_target="tpu_custom_call" | custom-call | bytes 59768832 | tf_op jit(solution)/shard_map/pair_sums/pallas_call | solution.py:149
  998.0 32.5 %subtract_rows.3 = f32[37728,128]{1,0:T(8,128)} custom-call(s32[2560]{0:T(1024)} %fusion.144.refs_0_, s32[3712]{0:T(1024)} %fusion.115.refs_1_, f32[37728,128]{1,0:T(8,128)} %pair_sums.7.refs_2_, f32[4608,128]{1,0:T(8,128)} %bitcast.319, f32[15360,128]{1,0:T(8,128)} %bitcast.144.refs_4_, f32[22272,128]{1,0:T(8,128)} %bitcast.147.refs_5_), custom_call_target="tpu_custom_call" | custom-call | bytes 96436224 | tf_op jit(solution)/shard_map/subtract_rows/pallas_call | solution.py:213
  1030.5 96.3 %all-reduce.11.cloned.1.call-done = f32[768,768]{1,0:T(8,128)} async-done(((f32[768,768]{1,0:T(8,128)}), f32[768,768]{1,0:T(8,128)}) %all-reduce.11.cloned.1.call-update) | async-done | bytes 2359312 | tf_op jit(solution)/shard_map/psum | solution.py:500
  1130.0 19.4 %all-to-all-done.15 = f32[8,640,768]{2,1,0:T(8,128)} async-done(((f32[8,640,768]{2,1,0:T(8,128)}), f32[8,640,768]{2,1,0:T(8,128)}, u32[]{:S(2)}, u32[]{:S(2)}) %all-to-all-start.15) | async-done | bytes 15728672 | tf_op jit(solution)/shard_map/all_to_all | solution.py:316
  1149.4 29.7 %subtract_rows.2 = f32[37728,128]{1,0:T(8,128)} custom-call(s32[5120]{0:T(1024)} %fusion.99.refs_0_, f32[37728,128]{1,0:T(8,128)} %bitcast.290, f32[4608,128]{1,0:T(8,128)} %bitcast.318, f32[30720,128]{1,0:T(8,128)} %bitcast.135.refs_3_), custom_call_target="tpu_custom_call" | custom-call | bytes 85819392 | tf_op jit(solution)/shard_map/subtract_rows/pallas_call | solution.py:213
  (239 shorter events, 142.9 us)
Async XLA Ops:
  77.2 59.6 %copy-start.32 = (s32[5120]{0:T(1024)}, s32[5120]{0:T(1024)S(1)}, u32[]{:S(2)}) copy-start(s32[5120]{0:T(1024)S(1)} %get-tuple-element.536) | copy-start | bytes 61444
  77.9 9.2 all-to-all-start.9
  87.2 71.8 %copy-start.48 = (s32[8,1,1729]{2,0,1:T(8,128)}, s32[8,1,1729]{2,0,1:T(8,128)S(1)}, u32[]{:S(2)}) copy-start(s32[8,1,1729]{2,0,1:T(8,128)S(1)} %copy.46) | copy-start | bytes 165988
  102.7 7.0 slice-start
  102.7 152.6 %all-to-all-start.10 = ((f32[8,320,768]{2,1,0:T(8,128)}), f32[8,320,768]{2,1,0:T(8,128)}, u32[]{:S(2)}, u32[]{:S(2)}) async-start(f32[8,320,768]{2,1,0:T(8,128)} %bitcast.310), calls=%async_computation.10 | async-start | bytes 15728640 | tf_op jit(solution)/shard_map/all_to_all | solution.py:316
  106.5 144.0 %all-reduce.7.cloned.1.call-start = ((), (), s32[]{:S(2)}) async-start(), calls=%async_computation.16 | async-start | bytes 9437184 | tf_op jit(solution)/shard_map/psum | solution.py:395
  109.8 10.5 copy-start.34
  123.4 34.1 %copy-start.49 = (s32[768]{0:T(1024)}, s32[768]{0:T(1024)S(1)}, u32[]{:S(2)}) copy-start(s32[768]{0:T(1024)S(1)} %convert_reduce_fusion.3) | copy-start | bytes 9220
  124.9 32.6 %copy-start.51 = (f32[5120]{0:T(1024)}, f32[5120]{0:T(1024)S(1)}, u32[]{:S(2)}) copy-start(f32[5120]{0:T(1024)S(1)} %convert_element_type.214) | copy-start | bytes 61444
  259.1 20.6 %copy-start.63 = (bf16[768,768]{1,0:T(8,128)(2,1)}, bf16[768,768]{1,0:T(8,128)(2,1)S(1)}, u32[]{:S(2)}) copy-start(bf16[768,768]{1,0:T(8,128)(2,1)S(1)} %get-tuple-element.532) | copy-start | bytes 3538948
  259.1 61.7 %copy-start.65 = (bf16[768,768]{1,0:T(8,128)(2,1)}, bf16[768,768]{1,0:T(8,128)(2,1)S(1)}, u32[]{:S(2)}) copy-start(bf16[768,768]{1,0:T(8,128)(2,1)S(1)} %get-tuple-element.533) | copy-start | bytes 3538948
  275.4 177.0 %all-to-all-start.11 = ((f32[8,640,768]{2,1,0:T(8,128)}), f32[8,640,768]{2,1,0:T(8,128)}, u32[]{:S(2)}, u32[]{:S(2)}) async-start(f32[8,640,768]{2,1,0:T(8,128)} %bitcast.305), calls=%async_computation.11 | async-start | bytes 31457280 | tf_op jit(solution)/shard_map/all_to_all | solution.py:316
  320.8 9.2 copy-start.67
  339.5 173.8 %copy-start.6 = (f32[768,768]{1,0:T(8,128)}, f32[768,768]{1,0:T(8,128)S(1)}, u32[]{:S(2)}) copy-start(f32[768,768]{1,0:T(8,128)S(1)} %get-tuple-element.277) | copy-start | bytes 7077892
  339.5 173.8 %copy-start.26 = (s32[3328]{0:T(1024)}, s32[3328]{0:T(1024)S(1)}, u32[]{:S(2)}) copy-start(s32[3328]{0:T(1024)S(1)} %get-tuple-element.647) | copy-start | bytes 39940
  552.9 130.5 %all-to-all-start.12 = ((f32[8,464,768]{2,1,0:T(8,128)}), f32[8,464,768]{2,1,0:T(8,128)}, u32[]{:S(2)}, u32[]{:S(2)}) async-start(f32[8,464,768]{2,1,0:T(8,128)} %bitcast.307), calls=%async_computation.12 | async-start | bytes 22806528 | tf_op jit(solution)/shard_map/all_to_all | solution.py:316
  683.4 107.8 %all-to-all-start.13 = ((f32[8,320,768]{2,1,0:T(8,128)}), f32[8,320,768]{2,1,0:T(8,128)}, u32[]{:S(2)}, u32[]{:S(2)}) async-start(f32[8,320,768]{2,1,0:T(8,128)} %bitcast.311), calls=%async_computation.13 | async-start | bytes 15728640 | tf_op jit(solution)/shard_map/all_to_all | solution.py:316
  791.2 155.7 %all-to-all-start.14 = ((f32[8,464,768]{2,1,0:T(8,128)}), f32[8,464,768]{2,1,0:T(8,128)}, u32[]{:S(2)}, u32[]{:S(2)}) async-start(f32[8,464,768]{2,1,0:T(8,128)} %bitcast.313), calls=%async_computation.14 | async-start | bytes 22806528 | tf_op jit(solution)/shard_map/all_to_all | solution.py:316
  795.2 140.6 %all-reduce.9.cloned.1.call-start = ((), (), s32[]{:S(2)}) async-start(), calls=%async_computation.17 | async-start | bytes 4718592 | tf_op jit(solution)/shard_map/psum | solution.py:496
  800.3 59.1 %copy-start.52 = (f32[5120]{0:T(1024)S(1)}, f32[5120]{0:T(1024)}, u32[]{:S(2)}) copy-start(f32[5120]{0:T(1024)} %copy-done.51) | copy-start | bytes 61444
  800.3 59.1 %copy-start.60 = (pred[5120]{0:T(1024)(128)(4,1)S(1)}, pred[5120]{0:T(1024)(128)(4,1)}, u32[]{:S(2)}) copy-start(pred[5120]{0:T(1024)(128)(4,1)} %broadcast_compare_fusion.1) | copy-start | bytes 15364
  859.4 17.2 %copy-start.5 = (f32[4608,128]{1,0:T(8,128)S(1)}, f32[4608,128]{1,0:T(8,128)}, u32[]{:S(2)}) copy-start(f32[4608,128]{1,0:T(8,128)} %pair_sums.6) | copy-start | bytes 7077892
  859.5 17.2 %copy-start.7 = (f32[768,768]{1,0:T(8,128)S(1)}, f32[768,768]{1,0:T(8,128)}, u32[]{:S(2)}) copy-start(f32[768,768]{1,0:T(8,128)} %copy-done.6) | copy-start | bytes 7077892
  859.5 17.2 %copy-start.25 = (f32[4608,128]{1,0:T(8,128)S(1)}, f32[4608,128]{1,0:T(8,128)}, u32[]{:S(2)}) copy-start(f32[4608,128]{1,0:T(8,128)} %get-tuple-element.278) | copy-start | bytes 7077892
  859.5 17.2 %copy-start.59 = (f32[768]{0:T(1024)S(1)}, f32[768]{0:T(1024)}, u32[]{:S(2)}) copy-start(f32[768]{0:T(1024)} %copy-done.58) | copy-start | bytes 9220
  859.5 17.2 %copy-start.62 = (pred[768]{0:T(1024)(128)(4,1)S(1)}, pred[768]{0:T(1024)(128)(4,1)}, u32[]{:S(2)}) copy-start(pred[768]{0:T(1024)(128)(4,1)} %broadcast_compare_fusion.3) | copy-start | bytes 2308
  947.0 5.1 copy-start.53
  947.0 202.5 %all-to-all-start.15 = ((f32[8,640,768]{2,1,0:T(8,128)}), f32[8,640,768]{2,1,0:T(8,128)}, u32[]{:S(2)}, u32[]{:S(2)}) async-start(f32[8,640,768]{2,1,0:T(8,128)} %bitcast.306), calls=%async_computation.15 | async-start | bytes 31457280 | tf_op jit(solution)/shard_map/all_to_all | solution.py:316
  951.5 175.3 %all-reduce.11.cloned.1.call-start = ((), (), s32[]{:S(2)}) async-start(), calls=%async_computation.18 | async-start | bytes 4718592 | tf_op jit(solution)/shard_map/psum | solution.py:500
  962.4 34.0 %copy-start.24 = (f32[768,768]{1,0:T(8,128)S(1)}, f32[768,768]{1,0:T(8,128)}, u32[]{:S(2)}) copy-start(f32[768,768]{1,0:T(8,128)} %all-reduce.9.cloned.1.call-done) | copy-start | bytes 7077892
  1149.4 29.8 %copy-start.35 = (s32[8192]{0:T(1024)S(1)}, s32[8192]{0:T(1024)}, u32[]{:S(2)}) copy-start(s32[8192]{0:T(1024)} %param.15) | copy-start | bytes 98308
  1149.4 29.8 %copy-start.37 = (s32[8192]{0:T(1024)S(1)}, s32[8192]{0:T(1024)}, u32[]{:S(2)}) copy-start(s32[8192]{0:T(1024)} %param.16) | copy-start | bytes 98308
  (13 other events, 47.0 us)
Sparse Core Ops, SparseCore 0:
  114.0 136.4 all-reduce.6
  800.4 135.3 all-reduce.8
  960.0 166.7 all-reduce.10

commit v5 on v4

--- a/solution.py
+++ b/solution.py
@@ -418,7 +418,7 @@
     past = (owners + 1) * shard_rows
     ship_owner = con_owner - shards
     ship_upto = jnp.sum((con_keys[None, :] < (past + past_all)[:, None]).astype(jnp.int32), axis=1)
-    ship_from = jnp.concatenate([num_stay[None], ship_upto[:-1]])
+    ship_from = jnp.sum((con_keys[None, :] < (past - shard_rows + past_all)[:, None]).astype(jnp.int32), axis=1)
     ship_counts = ship_upto - ship_from
     from_of = jnp.sum(jnp.where(ship_owner[None, :] == owners[:, None], ship_from[:, None], 0), axis=0)
     ship_rank = jnp.arange(num_pairs, dtype=jnp.int32) - from_of
@@ -432,11 +432,11 @@
         jnp.concatenate([jnp.where(stays, con_keys, (con_keys - past_all) * pack + sent_center), spread(past, cap_con), spread(past * pack + hot, cap_ship)])), num_keys=1)[1]
     con_asked = both[:con_cells].reshape(shards, cap_con)
     shipped = both[con_cells:con_cells + shards * cap_ship].reshape(shards, cap_ship)
-    fits = (jnp.max(neg_counts) <= cap_negs) & (jnp.max(cen_counts) <= cap_pairs) & (jnp.max(con_counts) <= cap_con) & (jnp.max(ship_counts) <= cap_ship)
-    spill = jnp.broadcast_to(1 - fits.astype(jnp.int32), (shards, 1))
+    over = (neg_counts > cap_negs) | (cen_counts > cap_pairs) | (con_counts > cap_con) | (ship_counts > cap_ship)
+    spill = jnp.broadcast_to(over.astype(jnp.int32)[None, :], (shards, shards))
     asked = exchange_ids(jnp.concatenate([cen_asked, con_asked, neg_asked, shipped, spill], axis=1))
-    all_fit = jnp.sum(asked[:, -1]) == 0
-    cuts = [0, cap_pairs, cap_pairs + cap_con, cap_pairs + cap_con + cap_negs, asked.shape[1] - 1]
+    all_fit = jnp.sum(asked[:, -shards:]) == 0
+    cuts = [0, cap_pairs, cap_pairs + cap_con, cap_pairs + cap_con + cap_negs, asked.shape[1] - shards]
     cen_local, con_local, neg_local = [asked[:, cuts[k]:cuts[k + 1]] - me * shard_rows for k in range(3)]
     taken = asked[:, cuts[3]:cuts[4]].reshape(-1)
     neg_send = gather_rows(out_shard, jnp.minimum(neg_local, shard_rows - 1).reshape(-1), shards)

time: 1200 us -> 1190 us (level)
  no operation moved by 1% of the time
where the time goes in v5:
time: 1190 us; the launch traced here: 1180 us
  waiting for transfers between devices  480 us (40%)
  Pallas kernels  325 us (27%)
  matrix products  164 us (14%)
  other arithmetic  136 us (11%)
  starting transfers between devices  29 us (2%)
  local copies, waits for them, and re-layouts  25.8 us (2%)
  between operations  19 us (2%)
    all_to_all x6, waiting for transfers between devices, exchange(): lax.all_to_all(rows.reshape(shards, -1, rows.shape[-1]), AXIS_NAME, 0, 0)  256 us
    pallas_call x4, Pallas kernels, pair_sums(): pl.pallas_call(body, grid_spec=pltpu.PrefetchScalarGridSpec(num_scalar_pr...  172 us
    dot_general x9, matrix products, dot(): lax.dot_general(a, b, (dims, ((), ())), preferred_element_type=jnp.float32)  163 us
    psum x1, waiting for transfers between devices, tight_step(): in_hot = lax.psum(cen_hot, AXIS_NAME)  96.3 us
    psum x1, waiting for transfers between devices, tight_step(): hot_both = lax.psum(jnp.where(me == 0, hot_both, 0.0), AXIS_NAME)  65.4 us
    pallas_call x2, Pallas kernels, subtract_rows(): pl.pallas_call(body, grid_spec=pltpu.PrefetchScalarGridSpec(num_scalar_pr...  62.2 us
    psum x1, waiting for transfers between devices, tight_step(): out_hot = lax.psum(con_hot + neg_hot, AXIS_NAME)  57.2 us
    pallas_call x3, Pallas kernels, gather_rows(): pl.pallas_call(body, grid_spec=pltpu.PrefetchScalarGridSpec(num_scalar_pr...  48.7 us
  transfers between devices with their start and end apart: 10, of which 8 were waited for; matrix products, arithmetic and copies ran while one was open for 15% of the time, Pallas kernels for 20%

profile of v5, /device:TPU:0, one launch (start us, length us, event | category | flops | bytes accessed | tf_op | source)
XLA Modules:
  0.0 1180.9 jit_solution(15321695288612861587)
XLA Ops:
  14.5 7.7 sort.297
  23.3 6.9 sort.299
  33.6 8.3 sort.300
  43.0 8.0 sort.302
  52.3 17.5 %sort.298 = (s32[13312]{0:T(1024)}, s32[13312]{0:T(1024)S(1)}, s32[13312]{0:T(1024)}) sort(s32[13312]{0:T(1024)S(1)} %get-tuple-element.469, s32[13312]{0:T(1024)S(1)} %get-tuple-element.470, s32[13312]{0:T(1024)S(1)} %iota.218), dimensions={0}, to_apply=%region_5.6 | sort | flops 186368 | bytes 319488 | tf_op jit(solution)/shard_map/sort | solution.py:299
  82.0 14.2 %gather_rows.5 = f32[15360,128]{1,0:T(8,128)} custom-call(s32[2560]{0:T(1024)} %fusion.133.line, f32[37728,128]{1,0:T(8,128)} %bitcast.283), custom_call_target="tpu_custom_call" | custom-call | bytes 42909696 | tf_op jit(solution)/shard_map/gather_rows/pallas_call | solution.py:68
  135.2 16.3 %gather_rows.3 = f32[22272,128]{1,0:T(8,128)} custom-call(s32[3712]{0:T(1024)} %fusion.113.line, f32[37728,128]{1,0:T(8,128)} %bitcast.284), custom_call_target="tpu_custom_call" | custom-call | bytes 53526528 | tf_op jit(solution)/shard_map/gather_rows/pallas_call | solution.py:68
  153.8 18.3 %gather_rows.4 = f32[30720,128]{1,0:T(8,128)} custom-call(s32[5120]{0:T(1024)} %fusion.102.line, f32[37728,128]{1,0:T(8,128)} %bitcast.288), custom_call_target="tpu_custom_call" | custom-call | bytes 66502656 | tf_op jit(solution)/shard_map/gather_rows/pallas_call | solution.py:68
  178.5 65.4 %all-reduce.7.cloned.1.call-done = f32[1536,768]{1,0:T(8,128)} async-done(((f32[1536,768]{1,0:T(8,128)}), f32[1536,768]{1,0:T(8,128)}) %all-reduce.7.cloned.1.call-update) | async-done | bytes 4718608 | tf_op jit(solution)/shard_map/psum | solution.py:395
  252.5 16.2 %split_rows.8 = (bf16[3328,768]{1,0:T(8,128)(2,1)}, bf16[3328,768]{1,0:T(8,128)(2,1)}, bf16[3328,768]{1,0:T(8,128)(2,1)}) custom-call(f32[768,768]{1,0:T(8,128)} %get-tuple-element.257.refs_0_, f32[2560,768]{1,0:T(8,128)} %bitcast.83.refs_1_, f32[3328,1]{1,0:T(8,128)} %copy.38.refs_2_), custom_call_target="tpu_custom_call" | custom-call | bytes 25559040 | tf_op jit(solution)/shard_map/split_rows/pallas_call | solution.py:251
  273.1 8.5 multiply_convert_fusion.2
  281.6 22.3 %pair_sums.6 = f32[4608,128]{1,0:T(8,128)} custom-call(s32[1]{0:T(128)} %bitcast.125.refs_0_, s32[2432]{0:T(1024)} %get-tuple-element.464.refs_1_, s32[2432]{0:T(1024)} %get-tuple-element.463.refs_2_, f32[37728,128]{1,0:T(8,128)} %bitcast.285, f32[4608,128]{1,0:T(8,128)} %bitcast.300), custom_call_target="tpu_custom_call" | custom-call | bytes 59768832 | tf_op jit(solution)/shard_map/pair_sums/pallas_call | solution.py:149
  303.9 7.6 fusion.200
  314.2 9.2 fusion.198
  323.4 9.2 fusion.199
  332.9 112.9 %all-to-all-done.11 = f32[8,640,768]{2,1,0:T(8,128)} async-done(((f32[8,640,768]{2,1,0:T(8,128)}), f32[8,640,768]{2,1,0:T(8,128)}, u32[]{:S(2)}, u32[]{:S(2)}) %all-to-all-start.11) | async-done | bytes 15728672 | tf_op jit(solution)/shard_map/all_to_all | solution.py:316
  445.8 22.1 %split_rows.7 = (bf16[5120,768]{1,0:T(8,128)(2,1)}, bf16[5120,768]{1,0:T(8,128)(2,1)}, bf16[5120,768]{1,0:T(8,128)(2,1)}) custom-call(f32[5120,768]{1,0:T(8,128)} %bitcast.85.refs_0_, f32[5120,1]{1,0:T(8,128)} %copy.37.refs_1_), custom_call_target="tpu_custom_call" | custom-call | bytes 39321600 | tf_op jit(solution)/shard_map/split_rows/pallas_call | solution.py:251
  467.9 38.8 %multiply_convert_fusion.1 = bf16[5120,3328]{1,0:T(8,128)(2,1)} fusion(bf16[5120,768]{1,0:T(8,128)(2,1)} %get-tuple-element.540, bf16[3328,768]{1,0:T(8,128)(2,1)} %get-tuple-element.571), kind=kOutput, calls=%fused_computation.154 | convolution fusion | flops 26257653760 | bytes 47054848 | tf_op jit(solution)/shard_map/dot_general | solution.py:324
  506.7 39.6 %add_add_fusion = f32[3328,768]{1,0:T(8,128)} fusion(f32[3328,768]{1,0:T(8,128)} %fusion.198, f32[3328,768]{1,0:T(8,128)} %fusion.199, bf16[5120,3328]{1,0:T(8,128)(2,1)} %multiply_convert_fusion.1, bf16[5120,768]{1,0:T(8,128)(2,1)} %get-tuple-element.541), kind=kOutput, calls=%fused_computation.161 | convolution fusion | flops 26177568768 | bytes 72613888 | tf_op jit(solution)/shard_map/dot_general | solution.py:324
  564.2 112.6 %all-to-all-done.12 = f32[8,464,768]{2,1,0:T(8,128)} async-done(((f32[8,464,768]{2,1,0:T(8,128)}), f32[8,464,768]{2,1,0:T(8,128)}, u32[]{:S(2)}, u32[]{:S(2)}) %all-to-all-start.12) | async-done | bytes 11403296 | tf_op jit(solution)/shard_map/all_to_all | solution.py:316
  680.4 12.2 %fusion.51 = f32[5120,768]{1,0:T(8,128)} fusion(bf16[5120,3328]{1,0:T(8,128)(2,1)} %get-tuple-element.671, bf16[3328,768]{1,0:T(8,128)(2,1)} %get-tuple-element.569), kind=kOutput, calls=%fused_computation.164 | convolution fusion | flops 6039797760 | bytes 24772608 | tf_op jit(solution)/shard_map/dot_general | solution.py:324
  692.6 35.2 %convolution_add_fusion = f32[5120,768]{1,0:T(8,128)} fusion(f32[5120,768]{1,0:T(8,128)} %fusion.51, bf16[5120,3328]{1,0:T(8,128)(2,1)} %get-tuple-element.671, bf16[3328,768]{1,0:T(8,128)(2,1)} %get-tuple-element.572), kind=kOutput, calls=%fused_computation.163 | convolution fusion | flops 26176389120 | bytes 70647808 | tf_op jit(solution)/shard_map/dot_general | solution.py:324
  727.8 56.8 %pair_sums.5 = (f32[4608,128]{1,0:T(8,128)}, f32[22272,128]{1,0:T(8,128)}) custom-call(s32[1]{0:T(128)} %bitcast.87.refs_0_, s32[8192]{0:T(1024)} %get-tuple-element.452.refs_1_, s32[8192]{0:T(1024)} %get-tuple-element.370.refs_2_, f32[4608,128]{1,0:T(8,128)} %bitcast.301, f32[30720,128]{1,0:T(8,128)} %bitcast.100.refs_6_.refs_4_, f32[4608,128]{1,0:T(8,128)} %bitcast.307, ...), custom_call_target="tpu_custom_call" | custom-call | bytes 201326592 | tf_op jit(solution)/shard_map/pair_sums/pallas_call | solution.py:149
  793.7 59.1 %pair_sums.4 = (f32[4608,128]{1,0:T(8,128)}, f32[30720,128]{1,0:T(8,128)}) custom-call(s32[1]{0:T(128)} %bitcast.87.refs_0_, s32[8192]{0:T(1024)} %fusion.65.refs_1_, s32[8192]{0:T(1024)} %fusion.67.refs_2_, f32[4608,128]{1,0:T(8,128)} %bitcast.308, f32[22272,128]{1,0:T(8,128)} %bitcast.94.refs_4_.refs_6_, f32[4608,128]{1,0:T(8,128)} %bitcast.302, ...), custom_call_target="tpu_custom_call" | custom-call | bytes 201326592 | tf_op jit(solution)/shard_map/pair_sums/pallas_call | solution.py:149
  852.9 17.2 %add_select_fusion.3 = f32[5120,768]{1,0:T(8,128)} fusion(f32[5120,768]{1,0:T(8,128)} %bitcast.311, f32[5120,768]{1,0:T(8,128)} %get-tuple-element.262, f32[5120]{0:T(1024)S(1)} %copy-done.52, pred[5120]{0:T(1024)(128)(4,1)S(1)} %copy-done.60), kind=kLoop, calls=%fused_computation.157 | loop fusion | flops 11796480 | bytes 47211520 | tf_op jit(solution)/shard_map/jit(_where)/select_n | solution.py:487
  872.0 57.2 %all-reduce.9.cloned.1.call-done = f32[768,768]{1,0:T(8,128)} async-done(((f32[768,768]{1,0:T(8,128)}), f32[768,768]{1,0:T(8,128)}) %all-reduce.9.cloned.1.call-update) | async-done | bytes 2359312 | tf_op jit(solution)/shard_map/psum | solution.py:496
  929.2 11.2 all-to-all-done.14
  955.8 34.0 %pair_sums.7.refs_2_ = f32[37728,128]{1,0:T(8,128)} custom-call(s32[1]{0:T(128)} %bitcast.125.refs_0_, s32[2432]{0:T(1024)} %get-tuple-element.462.refs_1_, s32[2432]{0:T(1024)} %get-tuple-element.461.refs_2_, f32[4608,128]{1,0:T(8,128)} %bitcast.303, f32[37728,128]{1,0:T(8,128)} %bitcast.286), custom_call_target="tpu_custom_call" | custom-call | bytes 59768832 | tf_op jit(solution)/shard_map/pair_sums/pallas_call | solution.py:149
  991.4 32.5 %subtract_rows.3 = f32[37728,128]{1,0:T(8,128)} custom-call(s32[2560]{0:T(1024)} %fusion.144.refs_0_, s32[3712]{0:T(1024)} %fusion.115.refs_1_, f32[37728,128]{1,0:T(8,128)} %pair_sums.7.refs_2_, f32[4608,128]{1,0:T(8,128)} %bitcast.318, f32[15360,128]{1,0:T(8,128)} %bitcast.144.refs_4_, f32[22272,128]{1,0:T(8,128)} %bitcast.147.refs_5_), custom_call_target="tpu_custom_call" | custom-call | bytes 96436224 | tf_op jit(solution)/shard_map/subtract_rows/pallas_call | solution.py:213
  1023.9 96.3 %all-reduce.11.cloned.1.call-done = f32[768,768]{1,0:T(8,128)} async-done(((f32[768,768]{1,0:T(8,128)}), f32[768,768]{1,0:T(8,128)}) %all-reduce.11.cloned.1.call-update) | async-done | bytes 2359312 | tf_op jit(solution)/shard_map/psum | solution.py:500
  1123.4 19.4 %all-to-all-done.15 = f32[8,640,768]{2,1,0:T(8,128)} async-done(((f32[8,640,768]{2,1,0:T(8,128)}), f32[8,640,768]{2,1,0:T(8,128)}, u32[]{:S(2)}, u32[]{:S(2)}) %all-to-all-start.15) | async-done | bytes 15728672 | tf_op jit(solution)/shard_map/all_to_all | solution.py:316
  1142.9 29.7 %subtract_rows.2 = f32[37728,128]{1,0:T(8,128)} custom-call(s32[5120]{0:T(1024)} %fusion.99.refs_0_, f32[37728,128]{1,0:T(8,128)} %bitcast.289, f32[4608,128]{1,0:T(8,128)} %bitcast.317, f32[30720,128]{1,0:T(8,128)} %bitcast.135.refs_3_), custom_call_target="tpu_custom_call" | custom-call | bytes 85819392 | tf_op jit(solution)/shard_map/subtract_rows/pallas_call | solution.py:213
  (236 shorter events, 139.6 us)
Async XLA Ops:
  70.5 60.2 %copy-start.32 = (s32[5120]{0:T(1024)}, s32[5120]{0:T(1024)S(1)}, u32[]{:S(2)}) copy-start(s32[5120]{0:T(1024)S(1)} %get-tuple-element.539) | copy-start | bytes 61444
  71.3 9.2 all-to-all-start.9
  80.6 72.4 %copy-start.48 = (s32[8,1,1736]{2,0,1:T(8,128)}, s32[8,1,1736]{2,0,1:T(8,128)S(1)}, u32[]{:S(2)}) copy-start(s32[8,1,1736]{2,0,1:T(8,128)S(1)} %copy.46) | copy-start | bytes 166660
  96.1 7.0 slice-start
  96.1 152.6 %all-to-all-start.10 = ((f32[8,320,768]{2,1,0:T(8,128)}), f32[8,320,768]{2,1,0:T(8,128)}, u32[]{:S(2)}, u32[]{:S(2)}) async-start(f32[8,320,768]{2,1,0:T(8,128)} %bitcast.309), calls=%async_computation.10 | async-start | bytes 15728640 | tf_op jit(solution)/shard_map/all_to_all | solution.py:316
  99.9 144.0 %all-reduce.7.cloned.1.call-start = ((), (), s32[]{:S(2)}) async-start(), calls=%async_computation.16 | async-start | bytes 9437184 | tf_op jit(solution)/shard_map/psum | solution.py:395
  103.1 10.5 copy-start.34
  116.8 34.7 %copy-start.49 = (s32[768]{0:T(1024)}, s32[768]{0:T(1024)S(1)}, u32[]{:S(2)}) copy-start(s32[768]{0:T(1024)S(1)} %convert_reduce_fusion.3) | copy-start | bytes 9220
  117.4 5.3 copy-start.58
  118.4 33.1 %copy-start.51 = (f32[5120]{0:T(1024)}, f32[5120]{0:T(1024)S(1)}, u32[]{:S(2)}) copy-start(f32[5120]{0:T(1024)S(1)} %convert_element_type.221) | copy-start | bytes 61444
  252.5 20.6 %copy-start.63 = (bf16[768,768]{1,0:T(8,128)(2,1)}, bf16[768,768]{1,0:T(8,128)(2,1)S(1)}, u32[]{:S(2)}) copy-start(bf16[768,768]{1,0:T(8,128)(2,1)S(1)} %get-tuple-element.535) | copy-start | bytes 3538948
  252.5 61.7 %copy-start.65 = (bf16[768,768]{1,0:T(8,128)(2,1)}, bf16[768,768]{1,0:T(8,128)(2,1)S(1)}, u32[]{:S(2)}) copy-start(bf16[768,768]{1,0:T(8,128)(2,1)S(1)} %get-tuple-element.536) | copy-start | bytes 3538948
  268.8 177.0 %all-to-all-start.11 = ((f32[8,640,768]{2,1,0:T(8,128)}), f32[8,640,768]{2,1,0:T(8,128)}, u32[]{:S(2)}, u32[]{:S(2)}) async-start(f32[8,640,768]{2,1,0:T(8,128)} %bitcast.304), calls=%async_computation.11 | async-start | bytes 31457280 | tf_op jit(solution)/shard_map/all_to_all | solution.py:316
  314.2 9.2 copy-start.67
  332.9 173.8 %copy-start.6 = (f32[768,768]{1,0:T(8,128)}, f32[768,768]{1,0:T(8,128)S(1)}, u32[]{:S(2)}) copy-start(f32[768,768]{1,0:T(8,128)S(1)} %get-tuple-element.277) | copy-start | bytes 7077892
  332.9 173.8 %copy-start.26 = (s32[3328]{0:T(1024)}, s32[3328]{0:T(1024)S(1)}, u32[]{:S(2)}) copy-start(s32[3328]{0:T(1024)S(1)} %get-tuple-element.650) | copy-start | bytes 39940
  546.3 130.5 %all-to-all-start.12 = ((f32[8,464,768]{2,1,0:T(8,128)}), f32[8,464,768]{2,1,0:T(8,128)}, u32[]{:S(2)}, u32[]{:S(2)}) async-start(f32[8,464,768]{2,1,0:T(8,128)} %bitcast.306), calls=%async_computation.12 | async-start | bytes 22806528 | tf_op jit(solution)/shard_map/all_to_all | solution.py:316
  676.8 107.8 %all-to-all-start.13 = ((f32[8,320,768]{2,1,0:T(8,128)}), f32[8,320,768]{2,1,0:T(8,128)}, u32[]{:S(2)}, u32[]{:S(2)}) async-start(f32[8,320,768]{2,1,0:T(8,128)} %bitcast.310), calls=%async_computation.13 | async-start | bytes 15728640 | tf_op jit(solution)/shard_map/all_to_all | solution.py:316
  784.6 155.7 %all-to-all-start.14 = ((f32[8,464,768]{2,1,0:T(8,128)}), f32[8,464,768]{2,1,0:T(8,128)}, u32[]{:S(2)}, u32[]{:S(2)}) async-start(f32[8,464,768]{2,1,0:T(8,128)} %bitcast.312), calls=%async_computation.14 | async-start | bytes 22806528 | tf_op jit(solution)/shard_map/all_to_all | solution.py:316
  788.6 140.6 %all-reduce.9.cloned.1.call-start = ((), (), s32[]{:S(2)}) async-start(), calls=%async_computation.17 | async-start | bytes 4718592 | tf_op jit(solution)/shard_map/psum | solution.py:496
  793.7 59.1 %copy-start.52 = (f32[5120]{0:T(1024)S(1)}, f32[5120]{0:T(1024)}, u32[]{:S(2)}) copy-start(f32[5120]{0:T(1024)} %copy-done.51) | copy-start | bytes 61444
  793.7 59.1 %copy-start.60 = (pred[5120]{0:T(1024)(128)(4,1)S(1)}, pred[5120]{0:T(1024)(128)(4,1)}, u32[]{:S(2)}) copy-start(pred[5120]{0:T(1024)(128)(4,1)} %broadcast_compare_fusion.1) | copy-start | bytes 15364
  852.9 17.2 %copy-start.5 = (f32[4608,128]{1,0:T(8,128)S(1)}, f32[4608,128]{1,0:T(8,128)}, u32[]{:S(2)}) copy-start(f32[4608,128]{1,0:T(8,128)} %pair_sums.6) | copy-start | bytes 7077892
  852.9 17.2 %copy-start.7 = (f32[768,768]{1,0:T(8,128)S(1)}, f32[768,768]{1,0:T(8,128)}, u32[]{:S(2)}) copy-start(f32[768,768]{1,0:T(8,128)} %copy-done.6) | copy-start | bytes 7077892
  852.9 17.2 %copy-start.25 = (f32[4608,128]{1,0:T(8,128)S(1)}, f32[4608,128]{1,0:T(8,128)}, u32[]{:S(2)}) copy-start(f32[4608,128]{1,0:T(8,128)} %get-tuple-element.278) | copy-start | bytes 7077892
  852.9 17.2 %copy-start.59 = (f32[768]{0:T(1024)S(1)}, f32[768]{0:T(1024)}, u32[]{:S(2)}) copy-start(f32[768]{0:T(1024)} %copy-done.58) | copy-start | bytes 9220
  852.9 17.2 %copy-start.62 = (pred[768]{0:T(1024)(128)(4,1)S(1)}, pred[768]{0:T(1024)(128)(4,1)}, u32[]{:S(2)}) copy-start(pred[768]{0:T(1024)(128)(4,1)} %broadcast_compare_fusion.3) | copy-start | bytes 2308
  940.4 202.5 %all-to-all-start.15 = ((f32[8,640,768]{2,1,0:T(8,128)}), f32[8,640,768]{2,1,0:T(8,128)}, u32[]{:S(2)}, u32[]{:S(2)}) async-start(f32[8,640,768]{2,1,0:T(8,128)} %bitcast.305), calls=%async_computation.15 | async-start | bytes 31457280 | tf_op jit(solution)/shard_map/all_to_all | solution.py:316
  944.9 175.3 %all-reduce.11.cloned.1.call-start = ((), (), s32[]{:S(2)}) async-start(), calls=%async_computation.18 | async-start | bytes 4718592 | tf_op jit(solution)/shard_map/psum | solution.py:500
  955.8 34.0 %copy-start.24 = (f32[768,768]{1,0:T(8,128)S(1)}, f32[768,768]{1,0:T(8,128)}, u32[]{:S(2)}) copy-start(f32[768,768]{1,0:T(8,128)} %all-reduce.9.cloned.1.call-done) | copy-start | bytes 7077892
  1142.8 29.8 %copy-start.35 = (s32[8192]{0:T(1024)S(1)}, s32[8192]{0:T(1024)}, u32[]{:S(2)}) copy-start(s32[8192]{0:T(1024)} %param.15) | copy-start | bytes 98308
  1142.8 29.8 %copy-start.37 = (s32[8192]{0:T(1024)S(1)}, s32[8192]{0:T(1024)}, u32[]{:S(2)}) copy-start(s32[8192]{0:T(1024)} %param.16) | copy-start | bytes 98308
  (13 other events, 47.5 us)
Sparse Core Ops, SparseCore 0:
  107.4 136.4 all-reduce.6
  793.8 135.3 all-reduce.8
  953.4 166.7 all-reduce.10

commit v6 on v5

--- a/solution.py
+++ b/solution.py
@@ -27,7 +27,7 @@
 
 def context_capacity(num_ids, shards):
     share = tight_capacity(num_ids, shards) * 5 // 8
-    return share + 64, tight_capacity(num_ids, shards) - share + 64
+    return share + 56, tight_capacity(num_ids, shards) - share + 64
 
 
 def tight_capacity(num_ids, shards):
@@ -63,7 +63,7 @@
                 o_ref[pl.ds(t * SUBLANES * chunks + j, chunks, stride=SUBLANES), :] = got[j]
             return carry
 
-        lax.fori_loop(0, cap // SUBLANES, step, 0, unroll=2)
+        lax.fori_loop(0, cap // SUBLANES, step, 0, unroll=2 if cap % (2 * SUBLANES) == 0 else 1)
 
     out = pl.pallas_call(
         body,
@@ -163,7 +163,7 @@
 
 def subtract_rows(table, hot, parts):
     d = table.shape[1]
-    chunks, batch = d // LANES, 16
+    chunks = d // LANES
     groups = parts[0][0].shape[0]
     caps = [rows.shape[1] for rows, _ in parts]
     view, hot_view = tile_view(table), tile_view(hot)
@@ -191,7 +191,9 @@
             lax.fori_loop(0, h_ref.shape[0] // 64, hot_step, 0)
 
         for p in range(count):
-            def step(t, carry, p=p):
+            batch = 16 if caps[p] % 16 == 0 else SUBLANES
+
+            def step(t, carry, p=p, batch=batch):
                 at = [line[p][group * caps[p] + t * batch + j] for j in range(batch)]
                 new = []
                 for j in range(batch):

time: 1190 us -> 1190 us (level)
  no operation moved by 1% of the time
where the time goes in v6:
time: 1190 us; the launch traced here: 1180 us
  waiting for transfers between devices  474 us (40%)
  Pallas kernels  326 us (27%)
  matrix products  164 us (14%)
  other arithmetic  136 us (11%)
  starting transfers between devices  28.9 us (2%)
  local copies, waits for them, and re-layouts  26 us (2%)
  between operations  19.1 us (2%)
    all_to_all x6, waiting for transfers between devices, exchange(): lax.all_to_all(rows.reshape(shards, -1, rows.shape[-1]), AXIS_NAME, 0, 0)  254 us
    pallas_call x4, Pallas kernels, pair_sums(): pl.pallas_call(body, grid_spec=pltpu.PrefetchScalarGridSpec(num_scalar_pr...  172 us
    dot_general x9, matrix products, dot(): lax.dot_general(a, b, (dims, ((), ())), preferred_element_type=jnp.float32)  163 us
    psum x1, waiting for transfers between devices, tight_step(): in_hot = lax.psum(cen_hot, AXIS_NAME)  95.8 us
    psum x1, waiting for transfers between devices, tight_step(): hot_both = lax.psum(jnp.where(me == 0, hot_both, 0.0), AXIS_NAME)  64.4 us
    pallas_call x2, Pallas kernels, subtract_rows(): pl.pallas_call(body, grid_spec=pltpu.PrefetchScalarGridSpec(num_scalar_pr...  62.7 us
    psum x1, waiting for transfers between devices, tight_step(): out_hot = lax.psum(con_hot + neg_hot, AXIS_NAME)  55.6 us
    pallas_call x3, Pallas kernels, gather_rows(): pl.pallas_call(body, grid_spec=pltpu.PrefetchScalarGridSpec(num_scalar_pr...  49.7 us
  transfers between devices with their start and end apart: 10, of which 8 were waited for; matrix products, arithmetic and copies ran while one was open for 15% of the time, Pallas kernels for 20%

profile of v6, /device:TPU:0, one launch (start us, length us, event | category | flops | bytes accessed | tf_op | source)
XLA Modules:
  0.0 1176.9 jit_solution(8796919498307064218)
XLA Ops:
  14.5 7.7 sort.297
  23.3 6.9 sort.299
  33.8 8.3 sort.300
  43.3 8.0 sort.302
  52.6 17.5 %sort.298 = (s32[13312]{0:T(1024)}, s32[13312]{0:T(1024)S(1)}, s32[13312]{0:T(1024)}) sort(s32[13312]{0:T(1024)S(1)} %get-tuple-element.469, s32[13312]{0:T(1024)S(1)} %get-tuple-element.470, s32[13312]{0:T(1024)S(1)} %iota.218), dimensions={0}, to_apply=%region_5.6 | sort | flops 186368 | bytes 319488 | tf_op jit(solution)/shard_map/sort | solution.py:301
  82.3 14.2 %gather_rows.5 = f32[15360,128]{1,0:T(8,128)} custom-call(s32[2560]{0:T(1024)} %fusion.133.line, f32[37728,128]{1,0:T(8,128)} %bitcast.283), custom_call_target="tpu_custom_call" | custom-call | bytes 42909696 | tf_op jit(solution)/shard_map/gather_rows/pallas_call | solution.py:68
  135.6 17.2 %gather_rows.3 = f32[21888,128]{1,0:T(8,128)} custom-call(s32[3648]{0:T(1024)} %fusion.113.line, f32[37728,128]{1,0:T(8,128)} %bitcast.284), custom_call_target="tpu_custom_call" | custom-call | bytes 52936704 | tf_op jit(solution)/shard_map/gather_rows/pallas_call | solution.py:68
  155.2 18.3 %gather_rows.4 = f32[30720,128]{1,0:T(8,128)} custom-call(s32[5120]{0:T(1024)} %fusion.102.line, f32[37728,128]{1,0:T(8,128)} %bitcast.288), custom_call_target="tpu_custom_call" | custom-call | bytes 66502656 | tf_op jit(solution)/shard_map/gather_rows/pallas_call | solution.py:68
  179.8 64.4 %all-reduce.7.cloned.1.call-done = f32[1536,768]{1,0:T(8,128)} async-done(((f32[1536,768]{1,0:T(8,128)}), f32[1536,768]{1,0:T(8,128)}) %all-reduce.7.cloned.1.call-update) | async-done | bytes 4718608 | tf_op jit(solution)/shard_map/psum | solution.py:397
  252.9 16.2 %split_rows.8 = (bf16[3328,768]{1,0:T(8,128)(2,1)}, bf16[3328,768]{1,0:T(8,128)(2,1)}, bf16[3328,768]{1,0:T(8,128)(2,1)}) custom-call(f32[768,768]{1,0:T(8,128)} %get-tuple-element.257.refs_0_, f32[2560,768]{1,0:T(8,128)} %bitcast.83.refs_1_, f32[3328,1]{1,0:T(8,128)} %copy.38.refs_2_), custom_call_target="tpu_custom_call" | custom-call | bytes 25559040 | tf_op jit(solution)/shard_map/split_rows/pallas_call | solution.py:253
  273.5 8.5 multiply_convert_fusion.2
  282.0 22.2 %pair_sums.6 = f32[4608,128]{1,0:T(8,128)} custom-call(s32[1]{0:T(128)} %bitcast.125.refs_0_, s32[2432]{0:T(1024)} %get-tuple-element.464.refs_1_, s32[2432]{0:T(1024)} %get-tuple-element.463.refs_2_, f32[37728,128]{1,0:T(8,128)} %bitcast.285, f32[4608,128]{1,0:T(8,128)} %bitcast.300), custom_call_target="tpu_custom_call" | custom-call | bytes 59768832 | tf_op jit(solution)/shard_map/pair_sums/pallas_call | solution.py:149
  304.2 7.6 fusion.200
  314.5 9.2 fusion.198
  323.7 9.2 fusion.199
  333.2 113.0 %all-to-all-done.11 = f32[8,640,768]{2,1,0:T(8,128)} async-done(((f32[8,640,768]{2,1,0:T(8,128)}), f32[8,640,768]{2,1,0:T(8,128)}, u32[]{:S(2)}, u32[]{:S(2)}) %all-to-all-start.11) | async-done | bytes 15728672 | tf_op jit(solution)/shard_map/all_to_all | solution.py:318
  446.1 22.0 %split_rows.7 = (bf16[5120,768]{1,0:T(8,128)(2,1)}, bf16[5120,768]{1,0:T(8,128)(2,1)}, bf16[5120,768]{1,0:T(8,128)(2,1)}) custom-call(f32[5120,768]{1,0:T(8,128)} %bitcast.85.refs_0_, f32[5120,1]{1,0:T(8,128)} %copy.37.refs_1_), custom_call_target="tpu_custom_call" | custom-call | bytes 39321600 | tf_op jit(solution)/shard_map/split_rows/pallas_call | solution.py:253
  468.2 38.8 %multiply_convert_fusion.1 = bf16[5120,3328]{1,0:T(8,128)(2,1)} fusion(bf16[5120,768]{1,0:T(8,128)(2,1)} %get-tuple-element.540, bf16[3328,768]{1,0:T(8,128)(2,1)} %get-tuple-element.571), kind=kOutput, calls=%fused_computation.154 | convolution fusion | flops 26257653760 | bytes 47054848 | tf_op jit(solution)/shard_map/dot_general | solution.py:326
  507.0 39.6 %add_add_fusion = f32[3328,768]{1,0:T(8,128)} fusion(f32[3328,768]{1,0:T(8,128)} %fusion.198, f32[3328,768]{1,0:T(8,128)} %fusion.199, bf16[5120,3328]{1,0:T(8,128)(2,1)} %multiply_convert_fusion.1, bf16[5120,768]{1,0:T(8,128)(2,1)} %get-tuple-element.541), kind=kOutput, calls=%fused_computation.161 | convolution fusion | flops 26177568768 | bytes 72613888 | tf_op jit(solution)/shard_map/dot_general | solution.py:326
  564.6 110.5 %all-to-all-done.12 = f32[8,456,768]{2,1,0:T(8,128)} async-done(((f32[8,456,768]{2,1,0:T(8,128)}), f32[8,456,768]{2,1,0:T(8,128)}, u32[]{:S(2)}, u32[]{:S(2)}) %all-to-all-start.12) | async-done | bytes 11206688 | tf_op jit(solution)/shard_map/all_to_all | solution.py:318
  678.6 12.2 %fusion.51 = f32[5120,768]{1,0:T(8,128)} fusion(bf16[5120,3328]{1,0:T(8,128)(2,1)} %get-tuple-element.671, bf16[3328,768]{1,0:T(8,128)(2,1)} %get-tuple-element.569), kind=kOutput, calls=%fused_computation.164 | convolution fusion | flops 6039797760 | bytes 24772608 | tf_op jit(solution)/shard_map/dot_general | solution.py:326
  690.8 35.2 %convolution_add_fusion = f32[5120,768]{1,0:T(8,128)} fusion(f32[5120,768]{1,0:T(8,128)} %fusion.51, bf16[5120,3328]{1,0:T(8,128)(2,1)} %get-tuple-element.671, bf16[3328,768]{1,0:T(8,128)(2,1)} %get-tuple-element.572), kind=kOutput, calls=%fused_computation.163 | convolution fusion | flops 26176389120 | bytes 70647808 | tf_op jit(solution)/shard_map/dot_general | solution.py:326
  726.0 56.7 %pair_sums.5 = (f32[4608,128]{1,0:T(8,128)}, f32[21888,128]{1,0:T(8,128)}) custom-call(s32[1]{0:T(128)} %bitcast.87.refs_0_, s32[8192]{0:T(1024)} %get-tuple-element.452.refs_1_, s32[8192]{0:T(1024)} %get-tuple-element.370.refs_2_, f32[4608,128]{1,0:T(8,128)} %bitcast.301, f32[30720,128]{1,0:T(8,128)} %bitcast.100.refs_6_.refs_4_, f32[4608,128]{1,0:T(8,128)} %bitcast.307, ...), custom_call_target="tpu_custom_call" | custom-call | bytes 201326592 | tf_op jit(solution)/shard_map/pair_sums/pallas_call | solution.py:149
  791.8 59.0 %pair_sums.4 = (f32[4608,128]{1,0:T(8,128)}, f32[30720,128]{1,0:T(8,128)}) custom-call(s32[1]{0:T(128)} %bitcast.87.refs_0_, s32[8192]{0:T(1024)} %fusion.65.refs_1_, s32[8192]{0:T(1024)} %fusion.67.refs_2_, f32[4608,128]{1,0:T(8,128)} %bitcast.308, f32[21888,128]{1,0:T(8,128)} %bitcast.94.refs_4_.refs_6_, f32[4608,128]{1,0:T(8,128)} %bitcast.302, ...), custom_call_target="tpu_custom_call" | custom-call | bytes 201326592 | tf_op jit(solution)/shard_map/pair_sums/pallas_call | solution.py:149
  850.9 17.2 %add_select_fusion.3 = f32[5120,768]{1,0:T(8,128)} fusion(f32[5120,768]{1,0:T(8,128)} %bitcast.311, f32[5120,768]{1,0:T(8,128)} %get-tuple-element.262, f32[5120]{0:T(1024)S(1)} %copy-done.52, pred[5120]{0:T(1024)(128)(4,1)S(1)} %copy-done.60), kind=kLoop, calls=%fused_computation.157 | loop fusion | flops 11796480 | bytes 47211520 | tf_op jit(solution)/shard_map/jit(_where)/select_n | solution.py:489
  870.0 55.6 %all-reduce.9.cloned.1.call-done = f32[768,768]{1,0:T(8,128)} async-done(((f32[768,768]{1,0:T(8,128)}), f32[768,768]{1,0:T(8,128)}) %all-reduce.9.cloned.1.call-update) | async-done | bytes 2359312 | tf_op jit(solution)/shard_map/psum | solution.py:498
  925.7 10.6 all-to-all-done.14
  951.8 34.0 %pair_sums.7.refs_2_ = f32[37728,128]{1,0:T(8,128)} custom-call(s32[1]{0:T(128)} %bitcast.125.refs_0_, s32[2432]{0:T(1024)} %get-tuple-element.462.refs_1_, s32[2432]{0:T(1024)} %get-tuple-element.461.refs_2_, f32[4608,128]{1,0:T(8,128)} %bitcast.303, f32[37728,128]{1,0:T(8,128)} %bitcast.286), custom_call_target="tpu_custom_call" | custom-call | bytes 59768832 | tf_op jit(solution)/shard_map/pair_sums/pallas_call | solution.py:149
  987.3 33.0 %subtract_rows.3 = f32[37728,128]{1,0:T(8,128)} custom-call(s32[2560]{0:T(1024)} %fusion.144.refs_0_, s32[3648]{0:T(1024)} %fusion.115.refs_1_, f32[37728,128]{1,0:T(8,128)} %pair_sums.7.refs_2_, f32[4608,128]{1,0:T(8,128)} %bitcast.318, f32[15360,128]{1,0:T(8,128)} %bitcast.144.refs_4_, f32[21888,128]{1,0:T(8,128)} %bitcast.147.refs_5_), custom_call_target="tpu_custom_call" | custom-call | bytes 95846400 | tf_op jit(solution)/shard_map/subtract_rows/pallas_call | solution.py:215
  1020.3 95.8 %all-reduce.11.cloned.1.call-done = f32[768,768]{1,0:T(8,128)} async-done(((f32[768,768]{1,0:T(8,128)}), f32[768,768]{1,0:T(8,128)}) %all-reduce.11.cloned.1.call-update) | async-done | bytes 2359312 | tf_op jit(solution)/shard_map/psum | solution.py:502
  1119.4 19.4 %all-to-all-done.15 = f32[8,640,768]{2,1,0:T(8,128)} async-done(((f32[8,640,768]{2,1,0:T(8,128)}), f32[8,640,768]{2,1,0:T(8,128)}, u32[]{:S(2)}, u32[]{:S(2)}) %all-to-all-start.15) | async-done | bytes 15728672 | tf_op jit(solution)/shard_map/all_to_all | solution.py:318
  1138.8 29.7 %subtract_rows.2 = f32[37728,128]{1,0:T(8,128)} custom-call(s32[5120]{0:T(1024)} %fusion.99.refs_0_, f32[37728,128]{1,0:T(8,128)} %bitcast.289, f32[4608,128]{1,0:T(8,128)} %bitcast.317, f32[30720,128]{1,0:T(8,128)} %bitcast.135.refs_3_), custom_call_target="tpu_custom_call" | custom-call | bytes 85819392 | tf_op jit(solution)/shard_map/subtract_rows/pallas_call | solution.py:215
  (236 shorter events, 139.8 us)
Async XLA Ops:
  70.9 60.4 %copy-start.32 = (s32[5120]{0:T(1024)}, s32[5120]{0:T(1024)S(1)}, u32[]{:S(2)}) copy-start(s32[5120]{0:T(1024)S(1)} %get-tuple-element.539) | copy-start | bytes 61444
  71.7 9.2 all-to-all-start.9
  80.9 73.4 %copy-start.48 = (s32[8,1,1728]{2,0,1:T(8,128)}, s32[8,1,1728]{2,0,1:T(8,128)S(1)}, u32[]{:S(2)}) copy-start(s32[8,1,1728]{2,0,1:T(8,128)S(1)} %copy.46) | copy-start | bytes 165892
  96.4 7.0 slice-start
  96.4 152.6 %all-to-all-start.10 = ((f32[8,320,768]{2,1,0:T(8,128)}), f32[8,320,768]{2,1,0:T(8,128)}, u32[]{:S(2)}, u32[]{:S(2)}) async-start(f32[8,320,768]{2,1,0:T(8,128)} %bitcast.309), calls=%async_computation.10 | async-start | bytes 15728640 | tf_op jit(solution)/shard_map/all_to_all | solution.py:318
  100.2 144.0 %all-reduce.7.cloned.1.call-start = ((), (), s32[]{:S(2)}) async-start(), calls=%async_computation.16 | async-start | bytes 9437184 | tf_op jit(solution)/shard_map/psum | solution.py:397
  103.5 10.6 copy-start.34
  117.3 35.6 %copy-start.49 = (s32[768]{0:T(1024)}, s32[768]{0:T(1024)S(1)}, u32[]{:S(2)}) copy-start(s32[768]{0:T(1024)S(1)} %convert_reduce_fusion.3) | copy-start | bytes 9220
  117.9 5.3 copy-start.58
  118.8 34.1 %copy-start.51 = (f32[5120]{0:T(1024)}, f32[5120]{0:T(1024)S(1)}, u32[]{:S(2)}) copy-start(f32[5120]{0:T(1024)S(1)} %convert_element_type.221) | copy-start | bytes 61444
  252.8 20.6 %copy-start.63 = (bf16[768,768]{1,0:T(8,128)(2,1)}, bf16[768,768]{1,0:T(8,128)(2,1)S(1)}, u32[]{:S(2)}) copy-start(bf16[768,768]{1,0:T(8,128)(2,1)S(1)} %get-tuple-element.535) | copy-start | bytes 3538948
  252.9 61.7 %copy-start.65 = (bf16[768,768]{1,0:T(8,128)(2,1)}, bf16[768,768]{1,0:T(8,128)(2,1)S(1)}, u32[]{:S(2)}) copy-start(bf16[768,768]{1,0:T(8,128)(2,1)S(1)} %get-tuple-element.536) | copy-start | bytes 3538948
  269.1 177.0 %all-to-all-start.11 = ((f32[8,640,768]{2,1,0:T(8,128)}), f32[8,640,768]{2,1,0:T(8,128)}, u32[]{:S(2)}, u32[]{:S(2)}) async-start(f32[8,640,768]{2,1,0:T(8,128)} %bitcast.304), calls=%async_computation.11 | async-start | bytes 31457280 | tf_op jit(solution)/shard_map/all_to_all | solution.py:318
  314.5 9.2 copy-start.67
  333.1 173.9 %copy-start.6 = (f32[768,768]{1,0:T(8,128)}, f32[768,768]{1,0:T(8,128)S(1)}, u32[]{:S(2)}) copy-start(f32[768,768]{1,0:T(8,128)S(1)} %get-tuple-element.277) | copy-start | bytes 7077892
  333.1 173.9 %copy-start.26 = (s32[3328]{0:T(1024)}, s32[3328]{0:T(1024)S(1)}, u32[]{:S(2)}) copy-start(s32[3328]{0:T(1024)S(1)} %get-tuple-element.650) | copy-start | bytes 39940
  546.7 128.3 %all-to-all-start.12 = ((f32[8,456,768]{2,1,0:T(8,128)}), f32[8,456,768]{2,1,0:T(8,128)}, u32[]{:S(2)}, u32[]{:S(2)}) async-start(f32[8,456,768]{2,1,0:T(8,128)} %bitcast.306), calls=%async_computation.12 | async-start | bytes 22413312 | tf_op jit(solution)/shard_map/all_to_all | solution.py:318
  675.0 107.7 %all-to-all-start.13 = ((f32[8,320,768]{2,1,0:T(8,128)}), f32[8,320,768]{2,1,0:T(8,128)}, u32[]{:S(2)}, u32[]{:S(2)}) async-start(f32[8,320,768]{2,1,0:T(8,128)} %bitcast.310), calls=%async_computation.13 | async-start | bytes 15728640 | tf_op jit(solution)/shard_map/all_to_all | solution.py:318
  782.8 153.6 %all-to-all-start.14 = ((f32[8,456,768]{2,1,0:T(8,128)}), f32[8,456,768]{2,1,0:T(8,128)}, u32[]{:S(2)}, u32[]{:S(2)}) async-start(f32[8,456,768]{2,1,0:T(8,128)} %bitcast.312), calls=%async_computation.14 | async-start | bytes 22413312 | tf_op jit(solution)/shard_map/all_to_all | solution.py:318
  786.7 139.0 %all-reduce.9.cloned.1.call-start = ((), (), s32[]{:S(2)}) async-start(), calls=%async_computation.17 | async-start | bytes 4718592 | tf_op jit(solution)/shard_map/psum | solution.py:498
  791.8 59.1 %copy-start.52 = (f32[5120]{0:T(1024)S(1)}, f32[5120]{0:T(1024)}, u32[]{:S(2)}) copy-start(f32[5120]{0:T(1024)} %copy-done.51) | copy-start | bytes 61444
  791.8 59.1 %copy-start.60 = (pred[5120]{0:T(1024)(128)(4,1)S(1)}, pred[5120]{0:T(1024)(128)(4,1)}, u32[]{:S(2)}) copy-start(pred[5120]{0:T(1024)(128)(4,1)} %broadcast_compare_fusion.1) | copy-start | bytes 15364
  850.9 17.2 %copy-start.5 = (f32[4608,128]{1,0:T(8,128)S(1)}, f32[4608,128]{1,0:T(8,128)}, u32[]{:S(2)}) copy-start(f32[4608,128]{1,0:T(8,128)} %pair_sums.6) | copy-start | bytes 7077892
  850.9 17.2 %copy-start.7 = (f32[768,768]{1,0:T(8,128)S(1)}, f32[768,768]{1,0:T(8,128)}, u32[]{:S(2)}) copy-start(f32[768,768]{1,0:T(8,128)} %copy-done.6) | copy-start | bytes 7077892
  850.9 17.2 %copy-start.25 = (f32[4608,128]{1,0:T(8,128)S(1)}, f32[4608,128]{1,0:T(8,128)}, u32[]{:S(2)}) copy-start(f32[4608,128]{1,0:T(8,128)} %get-tuple-element.278) | copy-start | bytes 7077892
  850.9 17.2 %copy-start.59 = (f32[768]{0:T(1024)S(1)}, f32[768]{0:T(1024)}, u32[]{:S(2)}) copy-start(f32[768]{0:T(1024)} %copy-done.58) | copy-start | bytes 9220
  850.9 17.2 %copy-start.62 = (pred[768]{0:T(1024)(128)(4,1)S(1)}, pred[768]{0:T(1024)(128)(4,1)}, u32[]{:S(2)}) copy-start(pred[768]{0:T(1024)(128)(4,1)} %broadcast_compare_fusion.3) | copy-start | bytes 2308
  936.3 202.5 %all-to-all-start.15 = ((f32[8,640,768]{2,1,0:T(8,128)}), f32[8,640,768]{2,1,0:T(8,128)}, u32[]{:S(2)}, u32[]{:S(2)}) async-start(f32[8,640,768]{2,1,0:T(8,128)} %bitcast.305), calls=%async_computation.15 | async-start | bytes 31457280 | tf_op jit(solution)/shard_map/all_to_all | solution.py:318
  940.9 175.3 %all-reduce.11.cloned.1.call-start = ((), (), s32[]{:S(2)}) async-start(), calls=%async_computation.18 | async-start | bytes 4718592 | tf_op jit(solution)/shard_map/psum | solution.py:502
  951.8 34.0 %copy-start.24 = (f32[768,768]{1,0:T(8,128)S(1)}, f32[768,768]{1,0:T(8,128)}, u32[]{:S(2)}) copy-start(f32[768,768]{1,0:T(8,128)} %all-reduce.9.cloned.1.call-done) | copy-start | bytes 7077892
  1138.8 29.8 %copy-start.35 = (s32[8192]{0:T(1024)S(1)}, s32[8192]{0:T(1024)}, u32[]{:S(2)}) copy-start(s32[8192]{0:T(1024)} %param.15) | copy-start | bytes 98308
  1138.8 29.8 %copy-start.37 = (s32[8192]{0:T(1024)S(1)}, s32[8192]{0:T(1024)}, u32[]{:S(2)}) copy-start(s32[8192]{0:T(1024)} %param.16) | copy-start | bytes 98308
  (13 other events, 47.4 us)
Sparse Core Ops, SparseCore 0:
  107.7 136.4 all-reduce.6
  791.9 133.7 all-reduce.8
  949.4 166.7 all-reduce.10
